TPU v7x, 128 devices: a whole 4x4x4 slice. The times are simulated.
128 devices in a mesh: row: 8 (over z_hi, x), col: 16 (over z_lo, y, core).
Axes of the slice: x: 4, y: 4, z: 4 (z_hi: 2, z_lo: 2; z = z_hi * 2 + z_lo), core: 2. Of those that a mesh axis runs over, the one named last changes fastest.
Arguments:
- left_features: bfloat16 [768, 4096], P(('row', 'col')), may hold values from -6 to 6
- right_features: bfloat16 [768, 4096], P(('row', 'col')), may hold values from -6 to 6
- weight: bfloat16 [1024, 128], replicated, may hold values from -2 to 2
- bias: float32 [128], replicated, may hold values from -3 to 3
- upstream: bfloat16 [768, 768, 128], P('row', 'col'), may hold values from -0.59765625 to 0.59765625
Outputs:
- pair_out: bfloat16 [768, 768, 128], P('row', 'col')
- grad_left: bfloat16 [768, 4096], P(('row', 'col'))
- grad_right: bfloat16 [768, 4096], P(('row', 'col'))
- grad_weight: float32 [1024, 128], replicated
- grad_bias: float32 [128], replicated
All inputs are finite; a program needn't handle non-finite values.
Results may differ from a plain program's by a relative error of at most 0.0063.
Values may be sent and summed in bfloat16 or wider, within the bound.
No kernel may reach another device: no remote copies, remote signals or barrier semaphores. Data moves between devices by JAX's collectives and lax.ppermute only.
A program may use at most 128 MiB of HBM per device.

v0:
```python
import jax
import jax.numpy as jnp
from jax import lax
from jax.sharding import PartitionSpec as P

CH = 32
SEQS = 128


block_rows = 16


def side_by_side(arrays, axis, dim, along):
    widths = [a.shape[along] for a in arrays]
    both = jnp.concatenate(arrays, axis=along)
    whole = lax.all_gather(both, axis, axis=dim, tiled=True)
    return tuple(jnp.split(whole, [sum(widths[:k]) for k in range(1, len(widths))], axis=along))


def together(arrays, axis):
    ends = [0]
    for a in arrays:
        ends.append(ends[-1] + a.size)
    total = lax.psum(jnp.concatenate([a.ravel() for a in arrays]), axis)
    return tuple((total[b:e].reshape(a.shape) for a, b, e in zip(arrays, ends, ends[1:])))


def term_pass(row_feats, col_feats, weight, bias, grads, forms):
    count = row_feats.shape[0]
    across = col_feats.shape[0]
    width = row_feats.shape[1]
    pairs = weight.shape[1]
    scale = 1.0 / SEQS
    col3 = col_feats.reshape(across, SEQS, CH)
    weight_t = weight.T
    forward_form, row_form, col_form = forms

    def one_block(carry, index):
        d_cols, d_weight, d_bias = carry
        start = index * block_rows
        rows = lax.dynamic_slice_in_dim(row_feats, start, block_rows, 0).reshape(
            block_rows, SEQS, CH
        )
        outer = jnp.einsum(forward_form, rows, col3, preferred_element_type=jnp.float32) * scale
        outer = outer.reshape(block_rows * across, CH * CH).astype(jnp.bfloat16)
        pre = jnp.dot(outer, weight, preferred_element_type=jnp.float32) + bias
        active = jnp.maximum(pre, 0.0)
        squared = active * active
        grad_block = lax.dynamic_slice_in_dim(grads, start, block_rows, 0).reshape(
            block_rows * across, pairs
        )
        d_pre = (active * grad_block.astype(jnp.float32)).astype(jnp.bfloat16)
        d_outer = jnp.dot(d_pre, weight_t, preferred_element_type=jnp.float32).astype(jnp.bfloat16)
        d_outer = d_outer.reshape(block_rows, across, CH, CH)
        d_row = jnp.einsum(row_form, d_outer, col3, preferred_element_type=jnp.float32) * scale
        d_cols = (
            d_cols + jnp.einsum(col_form, d_outer, rows, preferred_element_type=jnp.float32) * scale
        )
        d_weight = d_weight + jnp.einsum(
            "pk,pe->ke", outer, d_pre, preferred_element_type=jnp.float32
        )
        d_bias = d_bias + jnp.sum(d_pre.astype(jnp.float32), axis=0)
        return (
            (d_cols, d_weight, d_bias),
            (squared.reshape(block_rows, across, pairs), d_row.reshape(block_rows, width)),
        )

    init = (
        jnp.zeros((across, SEQS, CH), jnp.float32),
        jnp.zeros((CH * CH, pairs), jnp.float32),
        jnp.zeros((pairs,), jnp.float32),
    )
    steps = count // block_rows
    (d_cols, d_weight, d_bias), (squared, d_rows) = lax.scan(
        one_block, init, jnp.arange(steps, dtype=jnp.int32)
    )
    return (
        squared.reshape(count, across, pairs),
        d_rows.reshape(count, width),
        d_cols.reshape(across, width),
        d_weight,
        d_bias,
    )


def local(left_features, right_features, weight, bias, upstream):
    ratio = lax.axis_size("col") // lax.axis_size("row")
    row_count = lax.axis_size("row")
    col_index = lax.axis_index("col")
    left_rows, right_rows = (
        lax.all_gather(left_features, "col", axis=0, tiled=True),
        lax.all_gather(right_features, "col", axis=0, tiled=True),
    )
    count = left_rows.shape[0]
    half = count // ratio
    part_rows = half // row_count
    portion = col_index % ratio
    owner = col_index // ratio
    left_piece = lax.dynamic_slice_in_dim(left_rows, portion * half, half, 0)
    right_piece = lax.dynamic_slice_in_dim(right_rows, portion * half, half, 0)
    left_recv, right_recv = (
        lax.all_to_all(left_piece, "row", split_axis=0, concat_axis=0, tiled=True),
        lax.all_to_all(right_piece, "row", split_axis=0, concat_axis=0, tiled=True),
    )
    left_part = lax.dynamic_slice_in_dim(left_recv, owner * part_rows, part_rows, 0)
    right_part = lax.dynamic_slice_in_dim(right_recv, owner * part_rows, part_rows, 0)
    left_cols, right_cols = side_by_side((left_part, right_part), "row", 0, 1)
    direct_forms = ("isc,jsd->ijcd", "ijcd,jsd->isc", "ijcd,isc->jsd")
    mirror_forms = ("isd,jsc->ijcd", "ijcd,jsc->isd", "ijcd,isd->jsc")
    sq_direct, d_left_rows, d_right_cols, weight_one, bias_one = term_pass(
        left_rows, right_cols, weight, bias, upstream, direct_forms
    )
    sq_mirror, d_right_rows, d_left_cols, weight_two, bias_two = term_pass(
        right_rows, left_cols, weight, bias, upstream, mirror_forms
    )
    pair_out = ((sq_direct + sq_mirror) * 0.5).astype(jnp.bfloat16)
    left_share, right_share = (
        lax.psum_scatter(d_left_cols, "row", scatter_dimension=0, tiled=True),
        lax.psum_scatter(d_right_cols, "row", scatter_dimension=0, tiled=True),
    )
    target = jnp.arange(half, dtype=jnp.int32) // part_rows == owner
    target = target[:, None]
    left_slots = jnp.where(target, jnp.tile(left_share, (row_count, 1)), 0.0)
    right_slots = jnp.where(target, jnp.tile(right_share, (row_count, 1)), 0.0)
    left_back, right_back = (
        lax.all_to_all(left_slots, "row", split_axis=0, concat_axis=0, tiled=True),
        lax.all_to_all(right_slots, "row", split_axis=0, concat_axis=0, tiled=True),
    )
    start = portion * half
    left_slot = lax.dynamic_slice_in_dim(d_left_rows, start, half, 0) + left_back
    right_slot = lax.dynamic_slice_in_dim(d_right_rows, start, half, 0) + right_back
    d_left_rows = lax.dynamic_update_slice_in_dim(d_left_rows, left_slot, start, 0)
    d_right_rows = lax.dynamic_update_slice_in_dim(d_right_rows, right_slot, start, 0)
    grad_left, grad_right = (
        lax.psum_scatter(d_left_rows, "col", scatter_dimension=0, tiled=True),
        lax.psum_scatter(d_right_rows, "col", scatter_dimension=0, tiled=True),
    )
    grad_weight, grad_bias = together(
        (weight_one + weight_two, bias_one + bias_two), ("row", "col")
    )
    return (
        pair_out,
        grad_left.astype(jnp.bfloat16),
        grad_right.astype(jnp.bfloat16),
        grad_weight,
        grad_bias,
    )


def solution(mesh):
    placed = (P(("row", "col"), None), P(("row", "col"), None), P(), P(), P("row", "col", None))
    return jax.shard_map(
        local,
        mesh=mesh,
        in_specs=placed,
        out_specs=(
            P("row", "col", None),
            P(("row", "col"), None),
            P(("row", "col"), None),
            P(),
            P(),
        ),
        check_vma=False,
    )
```

profile of v0, /device:TPU:33, one launch (start us, length us, event | category | flops | bytes accessed | tf_op | source)
XLA Modules:
  0.0 951.9 jit_solution(11840749675674277259)
XLA Ops:
  7.2 22.1 %all-gather.1 = bf16[16,6,4096]{2,1,0:T(8,128)(2,1)S(1)} all-gather(bf16[1,6,4096]{2,1,0:T(8,128)(2,1)} %bitcast.215), channel_id=1, replica_groups=mesh['row'=8,'col'=16] {'col'}, dimensions={0}, use_global_device_ids=true | all-gather | bytes 835584 | tf_op jit(solution)/shard_map/all_gather | solution.py:92
  30.7 6.8 all-to-all-start.1
  37.5 21.5 %all-gather = bf16[16,6,4096]{2,1,0:T(8,128)(2,1)S(1)} all-gather(bf16[1,6,4096]{2,1,0:T(8,128)(2,1)S(1)} %bitcast.216), channel_id=1, replica_groups=mesh['row'=8,'col'=16] {'col'}, dimensions={0}, use_global_device_ids=true | all-gather | bytes 835584 | tf_op jit(solution)/shard_map/all_gather | solution.py:91
  65.5 5.7 all-to-all-start
  71.4 11.6 %all-to-all-done = bf16[8,6,4096]{2,1,0:T(8,128)(2,1)S(1)} async-done(((bf16[8,6,4096]{2,1,0:T(8,128)(2,1)}), bf16[8,6,4096]{2,1,0:T(8,128)(2,1)S(1)}, u32[]{:S(2)}, u32[]{:S(2)}) %all-to-all-start) | async-done | bytes 393248 | tf_op jit(solution)/shard_map/all_to_all | solution.py:102
  83.2 30.8 %all-gather.2 = bf16[8,6,8192]{2,1,0:T(8,128)(2,1)S(1)} all-gather(bf16[1,6,8192]{2,1,0:T(8,128)(2,1)S(1)} %maximum_bitcast_fusion), channel_id=1, replica_groups=mesh['row'=8,'col'=16] {'row'}, dimensions={0}, use_global_device_ids=true | all-gather | bytes 884736 | tf_op jit(solution)/shard_map/all_gather | solution.py:16
  120.6 298.9 %while.39 = (s32[]{:T(128)}, f32[48,128,32]{1,0,2:T(8,128)}, f32[1024,128]{1,0:T(8,128)}, f32[128]{0:T(128)S(1)}, f32[6,16,48,128]{3,2,1,0:T(8,128)}, /*index=5*...) while((s32[]{:T(128)}, f32[48,128,32]{1,0,2:T(8,128)}, ...), condition=%wide.region_5.6_spmd.clone, body=%wide.region_3.5_spmd.clone.sunk | while | flops 1212022912 | bytes 43782124 | solution.py:74
  126.3 6.8 copy.98
  133.1 6.1 convert_element_type.112
  145.8 6.0 reshape.166
  162.0 5.2 fusion.136
  173.8 6.8 copy.98
  180.6 6.1 convert_element_type.112
  193.3 6.0 reshape.166
  209.7 5.2 fusion.136
  221.5 6.8 copy.98
  228.3 6.1 convert_element_type.112
  241.0 6.0 reshape.166
  257.4 5.2 fusion.136
  269.2 6.8 copy.98
  276.0 6.1 convert_element_type.112
  288.7 6.0 reshape.166
  305.1 5.2 fusion.136
  316.9 6.8 copy.98
  323.7 6.1 convert_element_type.112
  336.4 6.0 reshape.166
  352.8 5.2 fusion.136
  364.6 6.8 copy.98
  371.4 6.1 convert_element_type.112
  384.1 6.0 reshape.166
  400.5 5.2 fusion.136
  427.4 267.7 %while.38 = (s32[]{:T(128)}, f32[48,128,32]{1,0,2:T(8,128)}, f32[1024,128]{1,0:T(8,128)}, f32[128]{0:T(128)S(1)}, f32[6,16,48,128]{3,2,1,0:T(8,128)}, /*index=5*...) while((s32[]{:T(128)}, f32[48,128,32]{1,0,2:T(8,128)}, ...), condition=%wide.region_2.3_spmd.clone, body=%wide.region_0.2_spmd.clone.sunk | while | flops 1212022912 | bytes 47190044 | solution.py:74
  432.4 4.7 copy.94
  437.0 6.1 convert_element_type.108
  449.0 6.0 reshape.164
  462.8 7.1 fusion.120
  476.0 4.7 copy.94
  480.7 6.1 convert_element_type.108
  492.6 6.0 reshape.164
  507.6 7.1 fusion.120
  520.8 4.7 copy.94
  525.5 6.1 convert_element_type.108
  537.4 6.0 reshape.164
  552.4 7.1 fusion.120
  565.6 4.7 copy.94
  570.3 6.1 convert_element_type.108
  582.2 6.0 reshape.164
  597.2 7.1 fusion.120
  610.4 4.7 copy.94
  615.0 6.1 convert_element_type.108
  627.0 6.0 reshape.164
  642.0 7.1 fusion.120
  655.2 4.7 copy.94
  659.8 6.1 convert_element_type.108
  671.7 6.0 reshape.164
  686.7 7.1 fusion.120
  703.7 27.5 %fusion.55 = (f32[8,4096]{1,0:T(8,128)S(1)}, f32[8,4096]{1,0:T(8,128)S(1)}) fusion(f32[48,4096]{1,0:T(8,128)} %reshape.127, f32[48,4096]{1,0:T(8,128)} %reshape.129), kind=kCustom, calls=%all-reduce-scatter.5 | all-reduce-scatter fusion | flops 524289 | bytes 1835520
  734.8 5.9 collective-permute-start.1
  748.0 4.8 all-to-all-start.3
  756.7 8.1 all-to-all-done.3
  772.6 11.5 %all-to-all-done.2 = f32[8,6,4096]{2,1,0:T(8,128)} async-done(((f32[8,6,4096]{2,1,0:T(8,128)}), f32[8,6,4096]{2,1,0:T(8,128)}, u32[]{:S(2)}, u32[]{:S(2)}) %all-to-all-start.2) | async-done | bytes 786464 | tf_op jit(solution)/shard_map/all_to_all | solution.py:126
  787.7 51.9 %fusion.54 = (f32[8,4096]{1,0:T(8,128)S(1)}, f32[8,4096]{1,0:T(8,128)S(1)}) fusion(f32[96,4096]{1,0:T(8,128)S(1)} %add_dynamic-update-slice_fusion.1, f32[96,4096]{1,0:T(8,128)S(1)} %add_dynamic-update-slice_fusion), kind=kCustom, calls=%all-reduce-scatter.4 | all-reduce-scatter fusion | flops 1048577 | bytes 3408384
  843.5 4.6 collective-permute-start.9
  850.1 73.1 %all-reduce.12.cloned.1.call-done = f32[131200]{0:T(1024)} async-done(((f32[131200]{0:T(1024)}), f32[131200]{0:T(1024)}) %all-reduce.12.cloned.1.call-update) | async-done | bytes 524816 | tf_op jit(solution)/shard_map/psum | solution.py:24
  (532 shorter events, 339.1 us)
Async XLA Ops:
  29.3 8.2 copy-start.27
  29.6 30.6 %copy-start.22 = (bf16[96,4096]{1,0:T(8,128)(2,1)}, bf16[96,4096]{1,0:T(8,128)(2,1)S(1)}, u32[]{:S(2)}) copy-start(bf16[96,4096]{1,0:T(8,128)(2,1)S(1)} %reshape.136) | copy-start | bytes 2359300
  30.7 34.9 %all-to-all-start.1 = ((bf16[8,6,4096]{2,1,0:T(8,128)(2,1)}), bf16[8,6,4096]{2,1,0:T(8,128)(2,1)S(1)}, u32[]{:S(2)}, u32[]{:S(2)}) async-start(bf16[8,6,4096]{2,1,0:T(8,128)(2,1)} %all_to_all.31), calls=%async_computation.1 | async-start | bytes 1048576 | tf_op jit(solution)/shard_map/all_to_all | solution.py:103
  37.5 24.7 %copy-start.7 = (bf16[1024,128]{1,0:T(8,128)(2,1)S(1)}, bf16[1024,128]{1,0:T(8,128)(2,1)}, u32[]{:S(2)}) copy-start(bf16[1024,128]{1,0:T(8,128)(2,1)} %param.11) | copy-start | bytes 786436
  65.5 17.4 %all-to-all-start = ((bf16[8,6,4096]{2,1,0:T(8,128)(2,1)}), bf16[8,6,4096]{2,1,0:T(8,128)(2,1)S(1)}, u32[]{:S(2)}, u32[]{:S(2)}) async-start(bf16[8,6,4096]{2,1,0:T(8,128)(2,1)} %all_to_all.28), calls=%async_computation | async-start | bytes 1048576 | tf_op jit(solution)/shard_map/all_to_all | solution.py:102
  120.8 20.8 %copy-start.11 = (bf16[128,1024]{1,0:T(8,128)(2,1)}, bf16[128,1024]{1,0:T(8,128)(2,1)S(1)}, u32[]{:S(2)}) copy-start(bf16[128,1024]{1,0:T(8,128)(2,1)S(1)} %get-tuple-element.638) | copy-start | bytes 786436 | tf_op jit(solution)/shard_map/while
  168.3 20.8 %copy-start.11 = (bf16[128,1024]{1,0:T(8,128)(2,1)}, bf16[128,1024]{1,0:T(8,128)(2,1)S(1)}, u32[]{:S(2)}) copy-start(bf16[128,1024]{1,0:T(8,128)(2,1)S(1)} %get-tuple-element.638) | copy-start | bytes 786436 | tf_op jit(solution)/shard_map/while
  216.0 20.8 %copy-start.11 = (bf16[128,1024]{1,0:T(8,128)(2,1)}, bf16[128,1024]{1,0:T(8,128)(2,1)S(1)}, u32[]{:S(2)}) copy-start(bf16[128,1024]{1,0:T(8,128)(2,1)S(1)} %get-tuple-element.638) | copy-start | bytes 786436 | tf_op jit(solution)/shard_map/while
  263.6 20.8 %copy-start.11 = (bf16[128,1024]{1,0:T(8,128)(2,1)}, bf16[128,1024]{1,0:T(8,128)(2,1)S(1)}, u32[]{:S(2)}) copy-start(bf16[128,1024]{1,0:T(8,128)(2,1)S(1)} %get-tuple-element.638) | copy-start | bytes 786436 | tf_op jit(solution)/shard_map/while
  311.4 20.8 %copy-start.11 = (bf16[128,1024]{1,0:T(8,128)(2,1)}, bf16[128,1024]{1,0:T(8,128)(2,1)S(1)}, u32[]{:S(2)}) copy-start(bf16[128,1024]{1,0:T(8,128)(2,1)S(1)} %get-tuple-element.638) | copy-start | bytes 786436 | tf_op jit(solution)/shard_map/while
  359.1 20.8 %copy-start.11 = (bf16[128,1024]{1,0:T(8,128)(2,1)}, bf16[128,1024]{1,0:T(8,128)(2,1)S(1)}, u32[]{:S(2)}) copy-start(bf16[128,1024]{1,0:T(8,128)(2,1)S(1)} %get-tuple-element.638) | copy-start | bytes 786436 | tf_op jit(solution)/shard_map/while
  427.4 16.8 %copy-start.9 = (bf16[1024,128]{1,0:T(8,128)(2,1)}, bf16[1024,128]{1,0:T(8,128)(2,1)S(1)}, u32[]{:S(2)}) copy-start(bf16[1024,128]{1,0:T(8,128)(2,1)S(1)} %get-tuple-element.584) | copy-start | bytes 786436 | tf_op jit(solution)/shard_map/while
  427.4 18.1 %copy-start.13 = (bf16[128,1024]{1,0:T(8,128)(2,1)}, bf16[128,1024]{1,0:T(8,128)(2,1)S(1)}, u32[]{:S(2)}) copy-start(bf16[128,1024]{1,0:T(8,128)(2,1)S(1)} %get-tuple-element.587) | copy-start | bytes 786436 | tf_op jit(solution)/shard_map/while
  462.8 8.2 copy-start.10
  462.8 8.2 copy-start.14
  462.8 8.1 copy-start.18
  471.0 16.8 %copy-start.9 = (bf16[1024,128]{1,0:T(8,128)(2,1)}, bf16[1024,128]{1,0:T(8,128)(2,1)S(1)}, u32[]{:S(2)}) copy-start(bf16[1024,128]{1,0:T(8,128)(2,1)S(1)} %get-tuple-element.584) | copy-start | bytes 786436 | tf_op jit(solution)/shard_map/while
  471.0 18.2 %copy-start.13 = (bf16[128,1024]{1,0:T(8,128)(2,1)}, bf16[128,1024]{1,0:T(8,128)(2,1)S(1)}, u32[]{:S(2)}) copy-start(bf16[128,1024]{1,0:T(8,128)(2,1)S(1)} %get-tuple-element.587) | copy-start | bytes 786436 | tf_op jit(solution)/shard_map/while
  507.6 7.1 copy-start.6
  507.6 8.2 copy-start.10
  507.6 8.2 copy-start.14
  507.6 8.2 copy-start.18
  515.8 16.8 %copy-start.9 = (bf16[1024,128]{1,0:T(8,128)(2,1)}, bf16[1024,128]{1,0:T(8,128)(2,1)S(1)}, u32[]{:S(2)}) copy-start(bf16[1024,128]{1,0:T(8,128)(2,1)S(1)} %get-tuple-element.584) | copy-start | bytes 786436 | tf_op jit(solution)/shard_map/while
  515.8 18.2 %copy-start.13 = (bf16[128,1024]{1,0:T(8,128)(2,1)}, bf16[128,1024]{1,0:T(8,128)(2,1)S(1)}, u32[]{:S(2)}) copy-start(bf16[128,1024]{1,0:T(8,128)(2,1)S(1)} %get-tuple-element.587) | copy-start | bytes 786436 | tf_op jit(solution)/shard_map/while
  552.4 7.1 copy-start.6
  552.4 8.2 copy-start.10
  552.4 8.2 copy-start.14
  552.4 8.1 copy-start.18
  560.6 16.8 %copy-start.9 = (bf16[1024,128]{1,0:T(8,128)(2,1)}, bf16[1024,128]{1,0:T(8,128)(2,1)S(1)}, u32[]{:S(2)}) copy-start(bf16[1024,128]{1,0:T(8,128)(2,1)S(1)} %get-tuple-element.584) | copy-start | bytes 786436 | tf_op jit(solution)/shard_map/while
  560.6 18.2 %copy-start.13 = (bf16[128,1024]{1,0:T(8,128)(2,1)}, bf16[128,1024]{1,0:T(8,128)(2,1)S(1)}, u32[]{:S(2)}) copy-start(bf16[128,1024]{1,0:T(8,128)(2,1)S(1)} %get-tuple-element.587) | copy-start | bytes 786436 | tf_op jit(solution)/shard_map/while
  597.1 7.1 copy-start.6
  597.1 8.2 copy-start.10
  597.1 8.2 copy-start.14
  597.1 8.2 copy-start.18
  605.3 16.8 %copy-start.9 = (bf16[1024,128]{1,0:T(8,128)(2,1)}, bf16[1024,128]{1,0:T(8,128)(2,1)S(1)}, u32[]{:S(2)}) copy-start(bf16[1024,128]{1,0:T(8,128)(2,1)S(1)} %get-tuple-element.584) | copy-start | bytes 786436 | tf_op jit(solution)/shard_map/while
  605.3 18.2 %copy-start.13 = (bf16[128,1024]{1,0:T(8,128)(2,1)}, bf16[128,1024]{1,0:T(8,128)(2,1)S(1)}, u32[]{:S(2)}) copy-start(bf16[128,1024]{1,0:T(8,128)(2,1)S(1)} %get-tuple-element.587) | copy-start | bytes 786436 | tf_op jit(solution)/shard_map/while
  641.9 8.2 copy-start.10
  641.9 8.2 copy-start.14
  641.9 8.1 copy-start.18
  650.1 16.8 %copy-start.9 = (bf16[1024,128]{1,0:T(8,128)(2,1)}, bf16[1024,128]{1,0:T(8,128)(2,1)S(1)}, u32[]{:S(2)}) copy-start(bf16[1024,128]{1,0:T(8,128)(2,1)S(1)} %get-tuple-element.584) | copy-start | bytes 786436 | tf_op jit(solution)/shard_map/while
  650.1 18.2 %copy-start.13 = (bf16[128,1024]{1,0:T(8,128)(2,1)}, bf16[128,1024]{1,0:T(8,128)(2,1)S(1)}, u32[]{:S(2)}) copy-start(bf16[128,1024]{1,0:T(8,128)(2,1)S(1)} %get-tuple-element.587) | copy-start | bytes 786436 | tf_op jit(solution)/shard_map/while
  686.7 8.2 copy-start.10
  686.7 8.2 copy-start.14
  686.7 8.1 copy-start.18
  703.7 38.9 %copy-start.15 = (f32[1024,128]{1,0:T(8,128)S(1)}, f32[1024,128]{1,0:T(8,128)}, u32[]{:S(2)}) copy-start(f32[1024,128]{1,0:T(8,128)} %get-tuple-element.153) | copy-start | bytes 1572868
  703.7 38.9 %copy-start.16 = (f32[1024,128]{1,0:T(8,128)S(1)}, f32[1024,128]{1,0:T(8,128)}, u32[]{:S(2)}) copy-start(f32[1024,128]{1,0:T(8,128)} %get-tuple-element.646) | copy-start | bytes 1572868
  731.3 15.1 %copy-start.29 = (pred[8,6]{1,0:T(8,128)(4,1)S(1)}, pred[8,6]{1,0:T(8,128)(4,1)}, u32[]{:S(2)}) copy-start(pred[8,6]{1,0:T(8,128)(4,1)} %fusion.52) | copy-start | bytes 148
  731.3 11.4 %collective-permute-start = (f32[8,4096]{1,0:T(8,128)S(1)}, f32[8,4096]{1,0:T(8,128)S(1)}, u32[]{:S(2)}, u32[]{:S(2)}) collective-permute-start(f32[8,4096]{1,0:T(8,128)S(1)} %get-tuple-element.351), channel_id=1, source_target_pairs={{0,16},{16,32},{32,48},{48,64},{64,80},{80,96},{96,112},{1,17},{17... | collective-permute-start | bytes 393224
  732.8 13.1 %collective-permute-start.6 = (f32[8,4096]{1,0:T(8,128)S(1)}, f32[8,4096]{1,0:T(8,128)S(1)}, u32[]{:S(2)}, u32[]{:S(2)}) collective-permute-start(f32[8,4096]{1,0:T(8,128)S(1)} %get-tuple-element.352), channel_id=1, source_target_pairs={{0,16},{16,32},{32,48},{48,64},{64,80},{80,96},{96,112},{1,17},{17... | collective-permute-start | bytes 393224
  734.8 8.0 collective-permute-start.1
  740.7 5.2 collective-permute-start.7
  748.0 16.8 %all-to-all-start.3 = ((f32[8,6,4096]{2,1,0:T(8,128)}), f32[8,6,4096]{2,1,0:T(8,128)}, u32[]{:S(2)}, u32[]{:S(2)}) async-start(f32[8,6,4096]{2,1,0:T(8,128)} %get-tuple-element.369), calls=%async_computation.3 | async-start | bytes 2097152 | tf_op jit(solution)/shard_map/all_to_all | solution.py:127
  752.8 170.4 %all-reduce.12.cloned.1.call-start = ((), (), s32[]{:S(2)}) async-start(), calls=%async_computation.4 | async-start | bytes 1056768 | tf_op jit(solution)/shard_map/psum | solution.py:24
  756.7 14.5 %copy-start.20 = (f32[6,16,4096]{2,1,0:T(8,128)S(1)}, f32[6,16,4096]{2,1,0:T(8,128)}, u32[]{:S(2)}) copy-start(f32[6,16,4096]{2,1,0:T(8,128)} %get-tuple-element.649) | copy-start | bytes 4718596
  764.8 19.4 %all-to-all-start.2 = ((f32[8,6,4096]{2,1,0:T(8,128)}), f32[8,6,4096]{2,1,0:T(8,128)}, u32[]{:S(2)}, u32[]{:S(2)}) async-start(f32[8,6,4096]{2,1,0:T(8,128)} %get-tuple-element.370), calls=%async_computation.2 | async-start | bytes 2097152 | tf_op jit(solution)/shard_map/all_to_all | solution.py:126
  771.2 15.2 %copy-start.19 = (f32[6,16,4096]{2,1,0:T(8,128)S(1)}, f32[6,16,4096]{2,1,0:T(8,128)}, u32[]{:S(2)}) copy-start(f32[6,16,4096]{2,1,0:T(8,128)} %get-tuple-element.149) | copy-start | bytes 4718596
  839.6 91.9 %collective-permute-start.10 = (bf16[8,4096]{1,0:T(8,128)(2,1)S(1)}, bf16[8,4096]{1,0:T(8,128)(2,1)S(1)}, u32[]{:S(2)}, u32[]{:S(2)}) collective-permute-start(bf16[8,4096]{1,0:T(8,128)(2,1)S(1)} %convert.60), channel_id=1, source_target_pairs={{0,3},{1,4},{2,5},{3,6},{4,7},{5,8},{6,9},{7,10},{8,11},{9,12},{10... | collective-permute-start | bytes 196616
  841.6 94.2 %collective-permute-start.8 = (bf16[8,4096]{1,0:T(8,128)(2,1)S(1)}, bf16[8,4096]{1,0:T(8,128)(2,1)S(1)}, u32[]{:S(2)}, u32[]{:S(2)}) collective-permute-start(bf16[8,4096]{1,0:T(8,128)(2,1)S(1)} %convert.60), channel_id=1, source_target_pairs={{0,1},{1,2},{2,3},{3,4},{4,5},{5,6},{6,7},{7,8},{8,9},{9,10},{10,1... | collective-permute-start | bytes 196616
  843.5 94.3 %collective-permute-start.9 = (bf16[8,4096]{1,0:T(8,128)(2,1)S(1)}, bf16[8,4096]{1,0:T(8,128)(2,1)S(1)}, u32[]{:S(2)}, u32[]{:S(2)}) collective-permute-start(bf16[8,4096]{1,0:T(8,128)(2,1)S(1)} %convert.60), channel_id=1, source_target_pairs={{0,2},{1,3},{2,4},{3,5},{4,6},{5,7},{6,8},{7,9},{8,10},{9,11},{10,... | collective-permute-start | bytes 196616
  848.1 80.5 %collective-permute-start.11 = (bf16[6,4096]{1,0:T(8,128)(2,1)S(1)}, bf16[6,4096]{1,0:T(8,128)(2,1)S(1)}, u32[]{:S(2)}, u32[]{:S(2)}) collective-permute-start(bf16[6,4096]{1,0:T(8,128)(2,1)S(1)} %slice.24), channel_id=1, source_target_pairs={{0,4},{1,5},{2,6},{3,7},{4,8},{5,9},{6,10},{7,11},{8,12},{9,13},{1... | collective-permute-start | bytes 147464
  926.2 17.1 %collective-permute-start.2 = (bf16[8,4096]{1,0:T(8,128)(2,1)S(1)}, bf16[8,4096]{1,0:T(8,128)(2,1)S(1)}, u32[]{:S(2)}, u32[]{:S(2)}) collective-permute-start(bf16[8,4096]{1,0:T(8,128)(2,1)S(1)} %convert.61), channel_id=1, source_target_pairs={{0,1},{1,2},{2,3},{3,4},{4,5},{5,6},{6,7},{7,8},{8,9},{9,10},{10,1... | collective-permute-start | bytes 196616
  928.7 14.7 %collective-permute-start.3 = (bf16[8,4096]{1,0:T(8,128)(2,1)S(1)}, bf16[8,4096]{1,0:T(8,128)(2,1)S(1)}, u32[]{:S(2)}, u32[]{:S(2)}) collective-permute-start(bf16[8,4096]{1,0:T(8,128)(2,1)S(1)} %convert.61), channel_id=1, source_target_pairs={{0,2},{1,3},{2,4},{3,5},{4,6},{5,7},{6,8},{7,9},{8,10},{9,11},{10,... | collective-permute-start | bytes 196616
  931.5 11.8 %collective-permute-start.4 = (bf16[8,4096]{1,0:T(8,128)(2,1)S(1)}, bf16[8,4096]{1,0:T(8,128)(2,1)S(1)}, u32[]{:S(2)}, u32[]{:S(2)}) collective-permute-start(bf16[8,4096]{1,0:T(8,128)(2,1)S(1)} %convert.61), channel_id=1, source_target_pairs={{0,3},{1,4},{2,5},{3,6},{4,7},{5,8},{6,9},{7,10},{8,11},{9,12},{10... | collective-permute-start | bytes 196616
  935.8 7.6 collective-permute-start.5
  (85 other events, 312.8 us)
Sparse Core Ops, SparseCore 0:
  758.4 164.7 all-reduce.11
where the time goes:
time: 960 us; the launch traced here: 952 us
  local copies, waits for them, and re-layouts  369 us (38%)
  matrix products  216 us (22%)
  blocking collectives  154 us (16%)
  waiting for transfers between devices  111 us (12%)
  starting transfers between devices  54.6 us (6%)
  loops' own time  22.4 us (2%)
  between operations  16.2 us (2%)
    convert_element_type x24, local copies, waits for them, and re-layouts, one_block(): outer = outer.reshape(block_rows * across, CH * CH).astype(jnp.bfloat16)  143 us
    unnamed x2, blocking collectives  79.5 us
    dot_general x12, matrix products, one_block(): jnp.einsum(col_form, d_outer, rows, preferred_element_type=jnp.float32)  73.9 us
    psum x1, waiting for transfers between devices, together(): total = lax.psum(jnp.concatenate([a.ravel() for a in arrays]), axis)  73.1 us
    reshape x12, local copies, waits for them, and re-layouts, one_block(): d_outer = d_outer.reshape(block_rows, across, CH, CH)  71.9 us
    dot_general x12, matrix products, one_block(): jnp.einsum(row_form, d_outer, col3, preferred_element_type=jnp.float32)  46.9 us
    unnamed x12, starting transfers between devices  33.1 us
    all_gather x1, blocking collectives, side_by_side(): whole = lax.all_gather(both, axis, axis=dim, tiled=True)  30.8 us
  transfers between devices with their start and end apart: 17, of which 6 were waited for; matrix products, arithmetic and copies ran while one was open for 7% of the time, Pallas kernels for 0%

commit v1 on v0

v1 whole, which is shorter than its diff:
```python
import functools

import jax
import jax.numpy as jnp
from jax import lax
from jax.experimental import pallas as pl
from jax.experimental.pallas import tpu as pltpu
from jax.sharding import PartitionSpec as P

CH = 32
SEQS = 128
GROUP = 4
BLOCK = 32
BF16 = jnp.bfloat16
F32 = jnp.float32


def contract(a, b, dims):
    numbers = (((dims[0],), (dims[1],)), ((), ()))
    return lax.dot_general(a, b, numbers, preferred_element_type=F32)


def spread(parts, places, turn):
    p0, p1, p2, p3 = (parts[(p - turn) % GROUP] for p in range(GROUP))
    odd, high = places
    return jnp.where(high, jnp.where(odd, p3, p2), jnp.where(odd, p1, p0))


def pair_kernel(
    steps,
    across,
    lane_ref,
    row_ref,
    weight_ref,
    bias_ref,
    up_ref,
    pair_ref,
    dlane_ref,
    drow_ref,
    dweight_ref,
    dbias_ref,
    squares,
    products,
    packed,
    grads,
    row_t,
    drow_acc,
    dweight_acc,
    dbias_acc,
):
    term, step = pl.program_id(0), pl.program_id(1)
    quarters = CH // GROUP
    groups = BLOCK // GROUP
    depth = quarters * across
    scale = 1.0 / SEQS
    lane = lax.broadcasted_iota(jnp.int32, (across, 128), 1) // CH
    places = (lane % 2 == 1, lane >= 2)

    @pl.when(step == 0)
    def _():
        for m in range(GROUP):
            row_t[m] = row_ref[0, m * depth : (m + 1) * depth, :].T
        drow_acc[...] = jnp.zeros_like(drow_acc)
        dweight_acc[...] = jnp.zeros_like(dweight_acc)

    @pl.when((step == 0) & (term == 0))
    def _():
        dbias_acc[...] = jnp.zeros_like(dbias_acc)

    def turned_lanes(m):
        return jnp.concatenate(
            [
                lane_ref[0, pl.ds((GROUP * g + (p - m) % GROUP) * CH, CH), :]
                for g in range(groups)
                for p in range(GROUP)
            ],
            axis=0,
        )

    def turned_weight(q):
        return jnp.concatenate(
            [
                weight_ref[0, pl.ds((GROUP * k + (p - q) % GROUP) * CH, CH), :]
                for k in range(quarters)
                for p in range(GROUP)
            ],
            axis=0,
        )

    for m in range(GROUP):
        outer = contract(row_ref[0, m * depth : (m + 1) * depth, :], turned_lanes(m), (1, 1))
        products[m] = (outer * scale).astype(BF16)
    for k in range(quarters):
        for g in range(groups):
            rows, lanes = pl.ds(k * across, across), pl.ds(g * 128, 128)
            parts = [products[m, rows, lanes] for m in range(GROUP)]
            for q in range(GROUP):
                packed[q, pl.ds(g * across, across), pl.ds(k * 128, 128)] = spread(parts, places, q)
    for q in range(GROUP):
        outer = packed[q]
        weight_q = turned_weight(q)
        pre = jnp.dot(outer, weight_q, preferred_element_type=F32) + bias_ref[...]
        active = jnp.maximum(pre, 0.0)
        squared = active * active
        up = jnp.concatenate([up_ref[GROUP * g + q] for g in range(groups)], axis=0)
        d_pre = (active * up.astype(F32)).astype(BF16)

        @pl.when(term == 0)
        def _():
            for g in range(groups):
                squares[step * BLOCK + GROUP * g + q] = squared[g * across : (g + 1) * across]

        @pl.when(term == 1)
        def _():
            for g in range(groups):
                both = squared[g * across : (g + 1) * across] + squares[step * BLOCK + GROUP * g + q]
                pair_ref[GROUP * g + q] = (both * 0.5).astype(BF16)

        products[q] = contract(d_pre, weight_q, (1, 1)).astype(BF16)
        dweight_acc[q] += contract(d_pre, outer, (0, 0))
        dbias_acc[...] += jnp.sum(
            d_pre.astype(F32).reshape(groups * across // 8, 8, 128), axis=0
        )
    for k in range(quarters):
        for g in range(groups):
            parts = [
                products[q, pl.ds(g * across, across), pl.ds(k * 128, 128)] for q in range(GROUP)
            ]
            rows, lanes = pl.ds(k * across, across), pl.ds(g * 128, 128)
            for m in range(GROUP):
                grads[m, rows, lanes] = spread(parts, places, m)

    def unturned(wide, turn):
        if turn == 0:
            return wide
        return jnp.concatenate(
            [
                pltpu.roll(wide[:, n * 128 : (n + 1) * 128], 128 - CH * turn, 1)
                for n in range(wide.shape[1] // 128)
            ],
            axis=1,
        )

    d_lane = None
    for m in range(GROUP):
        drow_acc[m * depth : (m + 1) * depth, :] += jnp.dot(
            grads[m], turned_lanes(m), preferred_element_type=F32
        )
        one = unturned(jnp.dot(row_t[m], grads[m], preferred_element_type=F32), m)
        d_lane = one if d_lane is None else d_lane + one
    dlane_ref[0] = (d_lane.T * scale).astype(BF16)

    @pl.when(step == steps - 1)
    def _():
        drow_ref[0] = (drow_acc[...] * scale).astype(BF16)
        total = dweight_acc[0]
        for q in range(1, GROUP):
            total = total + unturned(dweight_acc[q], q)
        flat = total.T

        @pl.when(term == 0)
        def _():
            for k in range(CH):
                dweight_ref[pl.ds(k, CH, stride=CH), :] = flat[k * CH : (k + 1) * CH]

        @pl.when(term == 1)
        def _():
            dweight_ref[...] += flat
            dbias_ref[...] = dbias_acc[...]


def pair_block(lanes, rows, weights, bias, upstream):
    count, across, pairs = upstream.shape
    steps = count // BLOCK
    width = BLOCK * CH
    depth = CH // GROUP * across
    once = lambda t, s: (0, 0)
    return pl.pallas_call(
        functools.partial(pair_kernel, steps, across),
        grid=(2, steps),
        in_specs=[
            pl.BlockSpec((1, width, SEQS), lambda t, s: (t, s, 0)),
            pl.BlockSpec((1, CH * across, SEQS), lambda t, s: (t, 0, 0)),
            pl.BlockSpec((1, CH * CH, pairs), lambda t, s: (t, 0, 0)),
            pl.BlockSpec((1, pairs), once),
            pl.BlockSpec((BLOCK, across, pairs), lambda t, s: (s, 0, 0)),
        ],
        out_specs=[
            pl.BlockSpec((BLOCK, across, pairs), lambda t, s: (t * s, 0, 0)),
            pl.BlockSpec((1, width, SEQS), lambda t, s: (t, s, 0)),
            pl.BlockSpec((1, CH * across, SEQS), lambda t, s: (t, 0, 0)),
            pl.BlockSpec((CH * CH, pairs), once),
            pl.BlockSpec((8, pairs), once),
        ],
        out_shape=[
            jax.ShapeDtypeStruct((count, across, pairs), BF16),
            jax.ShapeDtypeStruct((2, count * CH, SEQS), BF16),
            jax.ShapeDtypeStruct((2, CH * across, SEQS), BF16),
            jax.ShapeDtypeStruct((CH * CH, pairs), F32),
            jax.ShapeDtypeStruct((8, pairs), F32),
        ],
        scratch_shapes=[
            pltpu.VMEM((count, across, pairs), F32),
            pltpu.VMEM((GROUP, depth, width), BF16),
            pltpu.VMEM((GROUP, BLOCK // GROUP * across, CH * CH), BF16),
            pltpu.VMEM((GROUP, depth, width), BF16),
            pltpu.VMEM((GROUP, SEQS, depth), BF16),
            pltpu.VMEM((CH * across, SEQS), F32),
            pltpu.VMEM((GROUP, pairs, CH * CH), F32),
            pltpu.VMEM((8, pairs), F32),
        ],
        compiler_params=pltpu.CompilerParams(vmem_limit_bytes=60 * 1024 * 1024),
        cost_estimate=pl.CostEstimate(
            flops=12 * count * across * CH * CH * SEQS * 2,
            bytes_accessed=16 * 1024 * 1024,
            transcendentals=0,
        ),
    )(lanes, rows, weights, bias, upstream)


def exchange(x, axis):
    return lax.all_to_all(x, axis, split_axis=0, concat_axis=0, tiled=True)


def everywhere(x, axis):
    members = lax.axis_size(axis)
    return exchange(jnp.broadcast_to(x[None], (members,) + x.shape), axis)


def local(left_features, right_features, weight, bias, upstream):
    rows_n, cols_n = lax.axis_size("row"), lax.axis_size("col")
    own, pairs = left_features.shape[0], weight.shape[1]
    count, across = upstream.shape[0], upstream.shape[1]
    to_part = [(o, (o % rows_n) * cols_n + o // rows_n) for o in range(rows_n * cols_n)]
    to_owner = [(b, a) for a, b in to_part]
    both = ("row", "col")

    def channels_first(x):
        return x.reshape(own, SEQS, CH).transpose(0, 2, 1)

    mine = jnp.stack([channels_first(left_features), channels_first(right_features)])
    mine = mine.reshape(2, own * CH, SEQS)
    part = lax.ppermute(mine, both, to_part)
    lanes = everywhere(mine, "col").transpose(1, 0, 2, 3).reshape(2, count * CH, SEQS)
    rows = everywhere(part, "row").reshape(rows_n, 2, own, CH // GROUP, GROUP, SEQS)
    rows = rows[:, ::-1].transpose(1, 4, 3, 0, 2, 5).reshape(2, CH * across, SEQS)
    weights = jnp.stack(
        [weight.reshape(CH, CH, pairs).transpose(1, 0, 2).reshape(CH * CH, pairs), weight]
    )
    pair_out, d_lanes, d_rows, d_weight, d_bias = pair_block(
        lanes, rows, weights, bias.reshape(1, pairs), upstream
    )
    d_rows = d_rows.reshape(2, GROUP, CH // GROUP, rows_n, own, SEQS)[::-1]
    d_rows = d_rows.transpose(3, 0, 4, 2, 1, 5).reshape(rows_n, 2 * own * CH, SEQS)
    d_bias = jnp.sum(d_bias, axis=0, keepdims=True)

    def two_parts(x):
        high = x.astype(BF16)
        low = (x - high.astype(F32)).astype(BF16)
        return jnp.concatenate([high, low, jnp.zeros((14, pairs), BF16)], axis=0)

    def one_part(x):
        return jnp.sum(x[:2], axis=0, keepdims=True)

    slices = d_weight.reshape(rows_n, CH * CH // rows_n, pairs).astype(BF16)
    bias_rows = jnp.broadcast_to(two_parts(d_bias)[None], (rows_n, 16, pairs))
    sent = exchange(jnp.concatenate([d_rows, slices, bias_rows], axis=1), "row")
    summed = jnp.sum(sent.astype(F32), axis=0)
    n_own = 2 * own * CH
    n_slice = CH * CH // rows_n
    part_grads = lax.ppermute(summed[:n_own].astype(BF16), both, to_owner)
    slice_sum = summed[n_own : n_own + n_slice].astype(BF16)
    bias_sum = two_parts(one_part(summed[n_own + n_slice :]))
    d_lanes = d_lanes.reshape(2, cols_n, own * CH, SEQS).transpose(1, 0, 2, 3)
    d_lanes = d_lanes.reshape(cols_n, n_own, SEQS)
    shared = jnp.concatenate([slice_sum, bias_sum], axis=0)
    shared = jnp.broadcast_to(shared[None], (cols_n,) + shared.shape)
    sent = exchange(jnp.concatenate([d_lanes, shared], axis=1), "col")
    summed = jnp.sum(sent.astype(F32), axis=0)
    grads = summed[:n_own] + part_grads.astype(F32)
    grad_slice = summed[n_own : n_own + n_slice]
    grad_bias = one_part(summed[n_own + n_slice :]).reshape(pairs)
    grad_weight = everywhere(grad_slice, "row").reshape(CH * CH, pairs)
    grads = grads.reshape(2, own, CH, SEQS).transpose(0, 1, 3, 2).reshape(2, own, SEQS * CH)
    grads = grads.astype(BF16)
    return pair_out, grads[0], grads[1], grad_weight, grad_bias


def solution(mesh):
    placed = (P(("row", "col"), None), P(("row", "col"), None), P(), P(), P("row", "col", None))
    return jax.shard_map(
        local,
        mesh=mesh,
        in_specs=placed,
        out_specs=(
            P("row", "col", None),
            P(("row", "col"), None),
            P(("row", "col"), None),
            P(),
            P(),
        ),
        check_vma=False,
    )
```

time: 960 us -> 206 us (0.21)
  local copies, waits for them, and re-layouts: 369 us -> 26.3 us
  matrix products: 216 us -> 0 us
  blocking collectives: 154 us -> 0 us
  Pallas kernels: 0 us -> 50.4 us
  waiting for transfers between devices: 111 us -> 88.6 us
  loops' own time: 22.4 us -> 0 us
  starting transfers between devices: 54.6 us -> 33.8 us
  between operations: 16.2 us -> 0.89 us
    dot_general x72 -> x0, matrix products: 216 us -> none  [the longest x12 73.9 us: one_block(): jnp.einsum(col_form, d_outer, rows, preferred_element_type=jnp.float32)]
    convert_element_type x38 -> x1, local copies, waits for them, and re-layouts: 164 us -> 0.18 us  [local(): slices = d_weight.reshape(rows_n, CH * CH // rows_n, pairs).astype(BF16)]
    reshape x28 -> x5, local copies, waits for them, and re-layouts: 85.2 us -> 4.64 us  [the longest x2 2.03 us: channels_first(): return x.reshape(own, SEQS, CH).transpose(0, 2, 1)]
    unnamed x2 -> x0, blocking collectives: 79.5 us -> none
    all_gather x3 -> x0, blocking collectives: 74.4 us -> none  [the longest x1 30.8 us: side_by_side(): whole = lax.all_gather(both, axis, axis=dim, tiled=True)]
    psum x1 -> x0, waiting for transfers between devices: 73.1 us -> none  [together(): total = lax.psum(jnp.concatenate([a.ravel() for a in arrays]), axis)]
    all_to_all x4 -> x5, waiting for transfers between devices: 31.2 us -> 83.7 us  [exchange(): return lax.all_to_all(x, axis, split_axis=0, concat_axis=0, tiled=True)]
    pallas_call x0 -> x1, Pallas kernels: none -> 50.4 us  [pair_block(): pl.pallas_call(functools.partial(pair_kernel, steps, across), grid=(2, st...]
  transfers between devices with their start and end apart: 17 -> 7, of which waited for: 6 -> 6; matrix products, arithmetic and copies ran while one was open for 7% -> 4% of each run, Pallas kernels for 0% -> 0%
where the time goes in v1:
time: 206 us; the launch traced here: 204 us
  waiting for transfers between devices  88.6 us (43%)
  Pallas kernels  50.4 us (24%)
  starting transfers between devices  33.8 us (16%)
  local copies, waits for them, and re-layouts  26.3 us (13%)
  other arithmetic  4.32 us (2%)
    all_to_all x5, waiting for transfers between devices, exchange(): return lax.all_to_all(x, axis, split_axis=0, concat_axis=0, tiled=True)  83.7 us
    pallas_call x1, Pallas kernels, pair_block(): pl.pallas_call(functools.partial(pair_kernel, steps, across), grid=(2, st...  50.4 us
    all_to_all x5, starting transfers between devices, exchange(): return lax.all_to_all(x, axis, split_axis=0, concat_axis=0, tiled=True)  28.8 us
    pallas_call x1, local copies, waits for them, and re-layouts, pair_block(): pl.pallas_call(functools.partial(pair_kernel, steps, across), grid=(2, st...  6.89 us
    ppermute x1, waiting for transfers between devices, local(): part = lax.ppermute(mine, both, to_part)  4.88 us
  transfers between devices with their start and end apart: 7, of which 6 were waited for; matrix products, arithmetic and copies ran while one was open for 4% of the time, Pallas kernels for 0%

profile of v1, /device:TPU:33, one launch (start us, length us, event | category | flops | bytes accessed | tf_op | source)
XLA Modules:
  0.0 204.4 jit_solution(16391162088983271889)
XLA Ops:
  0.6 1.0 reshape.117
  1.6 0.1 copy.24
  1.8 1.0 reshape.118
  2.8 0.1 copy.25
  2.9 2.7 %collective-permute-start = (bf16[2,192,128]{2,1,0:T(8,128)(2,1)S(1)}, bf16[2,192,128]{2,1,0:T(8,128)(2,1)S(1)}, u32[]{:S(2)}, u32[]{:S(2)}) collective-permute-start(bf16[2,192,128]{2,1,0:T(8,128)(2,1)S(1)} %pad_maximum_fusion.3), channel_id=1, source_target_pairs={{0,0},{1,16},{2,32},{3,48},{4,64},{5,80},{6,96},{7,112},{8,1},{9,1... | collective-permute-start | bytes 294920 | tf_op jit(solution)/shard_map/ppermute | solution.py:243
  5.6 4.9 %collective-permute-done = bf16[2,192,128]{2,1,0:T(8,128)(2,1)S(1)} collective-permute-done((bf16[2,192,128]{2,1,0:T(8,128)(2,1)S(1)}, bf16[2,192,128]{2,1,0:T(8,128)(2,1)S(1)}, u32[]{:S(2)}, u32[]{:S(2)}) %collective-permute-start) | collective-permute-done | bytes 98336 | tf_op jit(solution)/shard_map/ppermute | solution.py:243
  10.5 1.0 broadcast_in_dim.14
  11.5 8.5 %all-to-all-start.1 = ((bf16[8,2,192,128]{3,2,1,0:T(8,128)(2,1)}), bf16[8,2,192,128]{3,2,1,0:T(8,128)(2,1)S(1)}, u32[]{:S(2)}, u32[]{:S(2)}) async-start(bf16[8,2,192,128]{3,2,1,0:T(8,128)(2,1)} %broadcast_in_dim.14), calls=%async_computation.1 | async-start | bytes 1572864 | tf_op jit(solution)/shard_map/all_to_all | solution.py:222
  20.1 14.2 %all-to-all-done.1 = bf16[8,2,192,128]{3,2,1,0:T(8,128)(2,1)S(1)} async-done(((bf16[8,2,192,128]{3,2,1,0:T(8,128)(2,1)}), bf16[8,2,192,128]{3,2,1,0:T(8,128)(2,1)S(1)}, u32[]{:S(2)}, u32[]{:S(2)}) %all-to-all-start.1) | async-done | bytes 786464 | tf_op jit(solution)/shard_map/all_to_all | solution.py:222
  34.2 1.5 broadcast_in_dim.13
  35.8 0.0 copy-start
  35.8 6.8 %all-to-all-start = ((bf16[16,2,192,128]{3,2,1,0:T(8,128)(2,1)}), bf16[16,2,192,128]{3,2,1,0:T(8,128)(2,1)S(1)}, u32[]{:S(2)}, u32[]{:S(2)}) async-start(bf16[16,2,192,128]{3,2,1,0:T(8,128)(2,1)} %broadcast_in_dim.13), calls=%async_computation | async-start | bytes 3145728 | tf_op jit(solution)/shard_map/all_to_all | solution.py:222
  42.6 0.0 copy-done
  42.6 0.1 copy.31
  42.7 0.8 pad_maximum_fusion.2.weight_ref
  43.5 0.5 copy.29
  44.0 0.1 reverse_bitcast_fusion
  44.1 0.8 copy.30
  44.9 1.0 copy.32.row_ref
  45.9 17.3 %all-to-all-done = bf16[16,2,192,128]{3,2,1,0:T(8,128)(2,1)S(1)} async-done(((bf16[16,2,192,128]{3,2,1,0:T(8,128)(2,1)}), bf16[16,2,192,128]{3,2,1,0:T(8,128)(2,1)S(1)}, u32[]{:S(2)}, u32[]{:S(2)}) %all-to-all-start) | async-done | bytes 1572896 | tf_op jit(solution)/shard_map/all_to_all | solution.py:222
  63.1 1.3 copy.26
  64.4 50.4 %shard_map.92 = (bf16[96,48,128]{2,1,0:T(8,128)(2,1)}, bf16[2,3072,128]{2,1,0:T(8,128)(2,1)}, bf16[2,1536,128]{2,1,0:T(8,128)(2,1)}, f32[1024,128]{1,0:T(8,128)}, f32[8,128]{1,0:T(8,128)}) custom-call(bf16[2,3072,128]{2,1,0:T(8,128)(2,1)} %bitcast.59, bf16[2,1536,128]{2,1,0:T(8,128)(2,1)} %copy.32.row_ref, ...), custom_call_target="tpu_custom_call" | custom-call | flops 14495514624 | bytes 16777216 | tf_op jit(solution)/shard_map/pallas_call | solution.py:178
  114.9 0.7 reduce_sum.49
  115.6 6.9 %copy.34 = bf16[2,1536,128]{2,0,1:T(2,128)(2,1)S(1)} copy(bf16[2,1536,128]{2,1,0:T(8,128)(2,1)} %get-tuple-element.12) | data formatting | bytes 1572864 | tf_op jit(solution)/shard_map/pallas_call | solution.py:178
  122.5 0.0 copy-start.1
  122.5 4.1 %rev.7 = bf16[2,4,8,8,6,128]{5,0,4,3,2,1:T(2,128)(2,1)S(1)} reverse(bf16[2,4,8,8,6,128]{5,0,4,3,2,1:T(2,128)(2,1)S(1)} %bitcast.55), dimensions={0} | reverse | bytes 1572864 | tf_op jit(solution)/shard_map/rev | solution.py:253
  126.6 0.1 copy.35
  126.7 0.0 copy-done.1
  126.8 0.2 copy.36
  127.0 0.1 pad_maximum_fusion.1
  127.2 1.1 copy.37
  128.3 3.6 %all-to-all-start.2 = ((bf16[8,528,128]{2,1,0:T(8,128)(2,1)}), bf16[8,528,128]{2,1,0:T(8,128)(2,1)S(1)}, u32[]{:S(2)}, u32[]{:S(2)}) async-start(bf16[8,528,128]{2,1,0:T(8,128)(2,1)} %copy.37), calls=%async_computation.2 | async-start | bytes 2162688 | tf_op jit(solution)/shard_map/all_to_all | solution.py:222
  131.8 1.5 copy.33
  133.4 16.1 %all-to-all-done.2 = bf16[8,528,128]{2,1,0:T(8,128)(2,1)S(1)} async-done(((bf16[8,528,128]{2,1,0:T(8,128)(2,1)}), bf16[8,528,128]{2,1,0:T(8,128)(2,1)S(1)}, u32[]{:S(2)}, u32[]{:S(2)}) %all-to-all-start.2) | async-done | bytes 1081376 | tf_op jit(solution)/shard_map/all_to_all | solution.py:222
  149.5 0.1 convert_reduce_fusion.1
  149.7 0.1 broadcast_in_dim.16
  149.8 1.5 pad_maximum_fusion
  151.3 5.1 %all-to-all-start.3 = ((bf16[16,528,128]{2,1,0:T(8,128)(2,1)}), bf16[16,528,128]{2,1,0:T(8,128)(2,1)S(1)}, u32[]{:S(2)}, u32[]{:S(2)}) async-start(bf16[16,528,128]{2,1,0:T(8,128)(2,1)} %pad_maximum_fusion), calls=%async_computation.3 | async-start | bytes 4325376 | tf_op jit(solution)/shard_map/all_to_all | solution.py:222
  156.5 2.4 %collective-permute-start.1 = (bf16[384,128]{1,0:T(8,128)(2,1)S(1)}, bf16[384,128]{1,0:T(8,128)(2,1)S(1)}, u32[]{:S(2)}, u32[]{:S(2)}) collective-permute-start(bf16[384,128]{1,0:T(8,128)(2,1)S(1)} %slice.43), channel_id=1, source_target_pairs={{0,0},{16,1},{32,2},{48,3},{64,4},{80,5},{96,6},{112,7},{1,8},{17,... | collective-permute-start | bytes 294920 | tf_op jit(solution)/shard_map/ppermute | solution.py:271
  158.8 27.0 %all-to-all-done.3 = bf16[16,528,128]{2,1,0:T(8,128)(2,1)S(1)} async-done(((bf16[16,528,128]{2,1,0:T(8,128)(2,1)}), bf16[16,528,128]{2,1,0:T(8,128)(2,1)S(1)}, u32[]{:S(2)}, u32[]{:S(2)}) %all-to-all-start.3) | async-done | bytes 2162720 | tf_op jit(solution)/shard_map/all_to_all | solution.py:222
  185.9 0.3 convert_reduce_fusion
  186.2 0.8 broadcast_in_dim.17
  187.0 4.8 %all-to-all-start.4 = ((f32[8,128,128]{2,1,0:T(8,128)}), f32[8,128,128]{2,1,0:T(8,128)S(1)}, u32[]{:S(2)}, u32[]{:S(2)}) async-start(f32[8,128,128]{2,1,0:T(8,128)} %broadcast_in_dim.17), calls=%async_computation.4 | async-start | bytes 1048576 | tf_op jit(solution)/shard_map/all_to_all | solution.py:222
  191.8 0.0 collective-permute-done.1
  191.9 0.2 copy.38
  192.0 0.9 squeeze.6
  192.9 0.2 copy.39
  193.1 0.9 squeeze.7
  193.9 0.5 slice_reduce_fusion
  194.5 9.1 %all-to-all-done.4 = f32[8,128,128]{2,1,0:T(8,128)S(1)} async-done(((f32[8,128,128]{2,1,0:T(8,128)}), f32[8,128,128]{2,1,0:T(8,128)S(1)}, u32[]{:S(2)}, u32[]{:S(2)}) %all-to-all-start.4) | async-done | bytes 524320 | tf_op jit(solution)/shard_map/all_to_all | solution.py:222
  203.6 0.8 copy.41
  (18 shorter events, 0.2 us)
Async XLA Ops:
  2.9 7.5 %collective-permute-start = (bf16[2,192,128]{2,1,0:T(8,128)(2,1)S(1)}, bf16[2,192,128]{2,1,0:T(8,128)(2,1)S(1)}, u32[]{:S(2)}, u32[]{:S(2)}) collective-permute-start(bf16[2,192,128]{2,1,0:T(8,128)(2,1)S(1)} %pad_maximum_fusion.3), channel_id=1, source_target_pairs={{0,0},{1,16},{2,32},{3,48},{4,64},{5,80},{6,96},{7,112},{8,1},{9,1... | collective-permute-start | bytes 294920 | tf_op jit(solution)/shard_map/ppermute | solution.py:243
  11.5 22.7 %all-to-all-start.1 = ((bf16[8,2,192,128]{3,2,1,0:T(8,128)(2,1)}), bf16[8,2,192,128]{3,2,1,0:T(8,128)(2,1)S(1)}, u32[]{:S(2)}, u32[]{:S(2)}) async-start(bf16[8,2,192,128]{3,2,1,0:T(8,128)(2,1)} %broadcast_in_dim.14), calls=%async_computation.1 | async-start | bytes 1572864 | tf_op jit(solution)/shard_map/all_to_all | solution.py:222
  35.8 6.8 %copy-start = (bf16[1024,128]{1,0:T(8,128)(2,1)S(1)}, bf16[1024,128]{1,0:T(8,128)(2,1)}, u32[]{:S(2)}) copy-start(bf16[1024,128]{1,0:T(8,128)(2,1)} %param.7) | copy-start | bytes 786436
  35.8 27.4 %all-to-all-start = ((bf16[16,2,192,128]{3,2,1,0:T(8,128)(2,1)}), bf16[16,2,192,128]{3,2,1,0:T(8,128)(2,1)S(1)}, u32[]{:S(2)}, u32[]{:S(2)}) async-start(bf16[16,2,192,128]{3,2,1,0:T(8,128)(2,1)} %broadcast_in_dim.13), calls=%async_computation | async-start | bytes 3145728 | tf_op jit(solution)/shard_map/all_to_all | solution.py:222
  122.5 4.3 %copy-start.1 = (f32[1024,128]{1,0:T(8,128)S(1)}, f32[1024,128]{1,0:T(8,128)}, u32[]{:S(2)}) copy-start(f32[1024,128]{1,0:T(8,128)} %get-tuple-element.13) | copy-start | bytes 1572868
  128.3 21.2 %all-to-all-start.2 = ((bf16[8,528,128]{2,1,0:T(8,128)(2,1)}), bf16[8,528,128]{2,1,0:T(8,128)(2,1)S(1)}, u32[]{:S(2)}, u32[]{:S(2)}) async-start(bf16[8,528,128]{2,1,0:T(8,128)(2,1)} %copy.37), calls=%async_computation.2 | async-start | bytes 2162688 | tf_op jit(solution)/shard_map/all_to_all | solution.py:222
  151.3 34.6 %all-to-all-start.3 = ((bf16[16,528,128]{2,1,0:T(8,128)(2,1)}), bf16[16,528,128]{2,1,0:T(8,128)(2,1)S(1)}, u32[]{:S(2)}, u32[]{:S(2)}) async-start(bf16[16,528,128]{2,1,0:T(8,128)(2,1)} %pad_maximum_fusion), calls=%async_computation.3 | async-start | bytes 4325376 | tf_op jit(solution)/shard_map/all_to_all | solution.py:222
  156.5 35.3 %collective-permute-start.1 = (bf16[384,128]{1,0:T(8,128)(2,1)S(1)}, bf16[384,128]{1,0:T(8,128)(2,1)S(1)}, u32[]{:S(2)}, u32[]{:S(2)}) collective-permute-start(bf16[384,128]{1,0:T(8,128)(2,1)S(1)} %slice.43), channel_id=1, source_target_pairs={{0,0},{16,1},{32,2},{48,3},{64,4},{80,5},{96,6},{112,7},{1,8},{17,... | collective-permute-start | bytes 294920 | tf_op jit(solution)/shard_map/ppermute | solution.py:271
  187.0 16.5 %all-to-all-start.4 = ((f32[8,128,128]{2,1,0:T(8,128)}), f32[8,128,128]{2,1,0:T(8,128)S(1)}, u32[]{:S(2)}, u32[]{:S(2)}) async-start(f32[8,128,128]{2,1,0:T(8,128)} %broadcast_in_dim.17), calls=%async_computation.4 | async-start | bytes 1048576 | tf_op jit(solution)/shard_map/all_to_all | solution.py:222

commit v2 on v1

v2 whole, which is shorter than its diff:
```python
import functools

import jax
import jax.numpy as jnp
from jax import lax
from jax.experimental import pallas as pl
from jax.experimental.pallas import tpu as pltpu
from jax.sharding import PartitionSpec as P


CH = 32
SEQS = 128
GROUP = 4
BLOCK = 32
TILE = 16
BF16 = jnp.bfloat16
F32 = jnp.float32


def contract(a, b, dims):
    numbers = (((dims[0],), (dims[1],)), ((), ()))
    return lax.dot_general(a, b, numbers, preferred_element_type=F32)


def spread(parts, odd, high):
    once = [jnp.where(odd, parts[(r + 1) % GROUP], parts[r]) for r in range(GROUP)]
    twice = [jnp.where(high, once[(r + 2) % GROUP], once[r]) for r in range(GROUP)]
    return [twice[-q % GROUP] for q in range(GROUP)]


def to_tiles(ref, at, wide):
    for n in range(wide.shape[1] // 128):
        ref[at, n] = wide[:, n * 128 : (n + 1) * 128]


def from_tiles(ref, at, first=0, count=None):
    count = ref.shape[1] if count is None else count
    return jnp.concatenate([ref[at, first + n] for n in range(count)], axis=1)


def pair_kernel(
    steps,
    across,
    lane_ref,
    row_ref,
    weight_ref,
    bias_ref,
    up_ref,
    pair_ref,
    cols_ref,
    send_ref,
    squares,
    products,
    packed,
    grads,
    row_t,
    drow_acc,
    dweight_acc,
    dweight_sum,
    drow_turned,
    dbias_acc,
):
    term, step = pl.program_id(0), pl.program_id(1)
    quarters = CH // GROUP
    groups = BLOCK // GROUP
    depth = quarters * across
    scale = 1.0 / SEQS
    own = across // send_ref.shape[0]
    lane = lax.broadcasted_iota(jnp.int32, (TILE, 128), 1) // CH
    odd = (lane % 2).astype(F32).astype(BF16) > 0.5
    high = (lane // 2).astype(F32).astype(BF16) > 0.5

    @pl.when(step == 0)
    def _():
        for m in range(GROUP):
            row_t[m] = row_ref[0, m * depth : (m + 1) * depth, :].T
        drow_acc[...] = jnp.zeros_like(drow_acc)
        dweight_acc[...] = jnp.zeros_like(dweight_acc)

    @pl.when((step == 0) & (term == 0))
    def _():
        dbias_acc[...] = jnp.zeros_like(dbias_acc)

    def turned_lanes(m):
        return jnp.concatenate(
            [
                lane_ref[0, pl.ds((GROUP * g + (p - m) % GROUP) * CH, CH), :]
                for g in range(groups)
                for p in range(GROUP)
            ],
            axis=0,
        )

    def turned_weight(q):
        return jnp.concatenate(
            [
                weight_ref[0, pl.ds((GROUP * k + (p - q) % GROUP) * CH, CH), :]
                for k in range(quarters)
                for p in range(GROUP)
            ],
            axis=0,
        )

    for m in range(GROUP):
        outer = contract(row_ref[0, m * depth : (m + 1) * depth, :], turned_lanes(m), (1, 1))
        to_tiles(products, m, (outer * scale).astype(BF16))

    def by_pair(k, _):
        from_rows = pl.multiple_of(k * across, TILE)
        for g in range(groups):
            for t in range(0, across, TILE):
                parts = [
                    products[m, g, pl.ds(from_rows + t, TILE), :] for m in range(GROUP)
                ]
                for q, tile in enumerate(spread(parts, odd, high)):
                    packed[q, k, pl.ds(g * across + t, TILE), :] = tile
        return _

    lax.fori_loop(0, quarters, by_pair, 0)
    for q in range(GROUP):
        outer = from_tiles(packed, q)
        weight_q = turned_weight(q)
        pre = jnp.dot(outer, weight_q, preferred_element_type=F32) + bias_ref[...]
        active = jnp.maximum(pre, 0.0)
        squared = active * active
        up = jnp.concatenate([up_ref[GROUP * g + q] for g in range(groups)], axis=0)
        d_pre = (active * up.astype(F32)).astype(BF16)

        for g in range(groups):
            place = step * BLOCK + GROUP * g + q
            here = squared[g * across : (g + 1) * across]
            pair_ref[GROUP * g + q] = ((here + squares[place]) * 0.5).astype(BF16)
            squares[place] = here
        to_tiles(products, q, contract(d_pre, weight_q, (1, 1)).astype(BF16))
        dweight_acc[q] += contract(d_pre, outer, (0, 0))
        dbias_acc[...] += jnp.sum(
            d_pre.astype(F32).reshape(groups * across // 8, 8, 128), axis=0
        )

    def by_channel(k, _):
        to_rows = pl.multiple_of(k * across, TILE)
        for g in range(groups):
            for t in range(0, across, TILE):
                parts = [
                    products[q, k, pl.ds(g * across + t, TILE), :] for q in range(GROUP)
                ]
                for m, tile in enumerate(spread(parts, odd, high)):
                    grads[m, g, pl.ds(to_rows + t, TILE), :] = tile
        return _

    lax.fori_loop(0, quarters, by_channel, 0)

    def unturned(wide, turn):
        if turn == 0:
            return wide
        return jnp.concatenate(
            [
                pltpu.roll(wide[:, n * 128 : (n + 1) * 128], 128 - CH * turn, 1)
                for n in range(wide.shape[1] // 128)
            ],
            axis=1,
        )

    for n in range(0, BLOCK * CH, 256):
        d_lane = None
        for m in range(GROUP):
            wide = jnp.dot(
                row_t[m], from_tiles(grads, m, n // 128, 2), preferred_element_type=F32
            )
            wide = unturned(wide, m)
            d_lane = wide if d_lane is None else d_lane + wide
        d_lane = (d_lane.T * scale).astype(BF16)
        for r in range(256 // CH):
            residue = step * BLOCK + n // CH + r
            to_row = pl.multiple_of((term * own + residue % own) * CH, CH)
            cols_ref[residue // own, pl.ds(to_row, CH), :] = d_lane[r * CH : (r + 1) * CH]
    for m in range(GROUP):
        drow_acc[m * depth : (m + 1) * depth, :] += jnp.dot(
            from_tiles(grads, m), turned_lanes(m), preferred_element_type=F32
        )

    @pl.when(step == steps - 1)
    def _():
        for m in range(GROUP):
            for k in range(quarters):
                block = drow_acc[pl.ds(m * depth + k * across, across), :]
                drow_turned[pl.ds(k * GROUP + m, across, stride=CH), :] = block * scale
        sent = drow_turned[...].astype(BF16).reshape(send_ref.shape[0], -1, SEQS)
        count = sent.shape[1]
        total = dweight_acc[0]
        for q in range(1, GROUP):
            total = total + unturned(dweight_acc[q], q)
        flat = total.T

        @pl.when(term == 0)
        def _():
            send_ref[:, count : 2 * count, :] = sent
            for k in range(CH):
                dweight_sum[pl.ds(k, CH, stride=CH), :] = flat[k * CH : (k + 1) * CH]

        @pl.when(term == 1)
        def _():
            send_ref[:, :count, :] = sent
            whole = (dweight_sum[...] + flat).astype(BF16)
            peers = cols_ref.shape[0]
            end = 2 * count + whole.shape[0] // peers
            cols_ref[:, 2 * count : end, :] = whole.reshape(peers, -1, whole.shape[1])
            d_bias = jnp.sum(dbias_acc[...], axis=0, keepdims=True)
            first = d_bias.astype(BF16).astype(F32)
            place = lax.broadcasted_iota(jnp.int32, (TILE, 128), 0)
            rows = jnp.where(place == 0, first, jnp.where(place == 1, d_bias - first, 0.0))
            for r in range(peers):
                cols_ref[r, end : end + TILE, :] = rows.astype(BF16)


def pair_block(lanes, rows, weights, bias, upstream, row_peers, col_peers):
    count, across, pairs = upstream.shape
    steps = count // BLOCK
    width = BLOCK * CH
    depth = CH // GROUP * across
    once = lambda t, s: (0, 0)
    sent = 2 * CH * across // row_peers + CH * CH // col_peers + TILE
    return pl.pallas_call(
        functools.partial(pair_kernel, steps, across),
        grid=(2, steps),
        in_specs=[
            pl.BlockSpec((1, width, SEQS), lambda t, s: (t, s, 0)),
            pl.BlockSpec((1, CH * across, SEQS), lambda t, s: (t, 0, 0)),
            pl.BlockSpec((1, CH * CH, pairs), lambda t, s: (t, 0, 0)),
            pl.BlockSpec((1, pairs), once),
            pl.BlockSpec((BLOCK, across, pairs), lambda t, s: (s, 0, 0)),
        ],
        out_specs=[
            pl.BlockSpec((BLOCK, across, pairs), lambda t, s: (t * s, 0, 0)),
            pl.BlockSpec((col_peers, sent, SEQS), lambda t, s: (0, 0, 0)),
            pl.BlockSpec((row_peers, sent, SEQS), lambda t, s: (0, 0, 0)),
        ],
        out_shape=[
            jax.ShapeDtypeStruct((count, across, pairs), BF16),
            jax.ShapeDtypeStruct((col_peers, sent, SEQS), BF16),
            jax.ShapeDtypeStruct((row_peers, sent, SEQS), BF16),
        ],
        scratch_shapes=[
            pltpu.VMEM((count, across, pairs), F32),
            pltpu.VMEM((GROUP, width // 128, depth, 128), BF16),
            pltpu.VMEM((GROUP, width // 128, depth, 128), BF16),
            pltpu.VMEM((GROUP, width // 128, depth, 128), BF16),
            pltpu.VMEM((GROUP, SEQS, depth), BF16),
            pltpu.VMEM((CH * across, SEQS), F32),
            pltpu.VMEM((GROUP, pairs, CH * CH), F32),
            pltpu.VMEM((CH * CH, pairs), F32),
            pltpu.VMEM((CH * across, SEQS), F32),
            pltpu.VMEM((8, pairs), F32),
        ],
        compiler_params=pltpu.CompilerParams(vmem_limit_bytes=60 * 1024 * 1024),
        cost_estimate=pl.CostEstimate(
            flops=12 * count * across * CH * CH * SEQS * 2,
            bytes_accessed=16 * 1024 * 1024,
            transcendentals=0,
        ),
    )(lanes, rows, weights, bias, upstream)


def exchange(x, axis, groups=None):
    return lax.all_to_all(
        x, axis, split_axis=0, concat_axis=0, axis_index_groups=groups, tiled=True
    )


def everywhere(x, axis, groups=None):
    members = lax.axis_size(axis) if groups is None else len(groups[0])
    copies = jnp.broadcast_to(x[None], (members,) + x.shape)
    return exchange(copies, axis, groups)


def two_parts(x):
    high = x.astype(BF16)
    low = (x - high.astype(F32)).astype(BF16)
    return jnp.concatenate([high, low, jnp.zeros((TILE - 2, x.shape[1]), BF16)], axis=0)


def one_part(x):
    return jnp.sum(x[:2], axis=0, keepdims=True)


def local(left_features, right_features, weight, bias, upstream):
    rows_n, cols_n = lax.axis_size("row"), lax.axis_size("col")
    own, pairs = left_features.shape[0], weight.shape[1]
    count, across = upstream.shape[0], upstream.shape[1]
    to_part = [(o, (o % rows_n) * cols_n + o // rows_n) for o in range(rows_n * cols_n)]
    to_owner = [(b, a) for a, b in to_part]
    both = ("row", "col")
    same_core = [list(range(k, cols_n, 2)) for k in range(2)]
    other_core = [(k, k ^ 1) for k in range(cols_n)]
    n_own = 2 * own * CH

    def channels_first(x):
        return x.reshape(own, SEQS, CH).transpose(0, 2, 1)

    mine = jnp.stack([channels_first(left_features), channels_first(right_features)])
    mine = mine.reshape(2, own * CH, SEQS)
    part = lax.ppermute(mine, both, to_part)
    half = everywhere(mine, "col", same_core)
    other = lax.ppermute(half, "col", other_core)
    rows = everywhere(part, "row")
    second = lax.axis_index("col") % 2 == 1
    lanes = jnp.stack(
        [jnp.where(second, other, half), jnp.where(second, half, other)], axis=1
    )
    lanes = lanes.transpose(2, 0, 1, 3, 4).reshape(2, count * CH, SEQS)
    rows = rows.reshape(rows_n, 2, own, CH // GROUP, GROUP, SEQS)
    rows = rows[:, ::-1].transpose(1, 4, 3, 0, 2, 5).reshape(2, CH * across, SEQS)
    weights = jnp.stack(
        [weight.reshape(CH, CH, pairs).transpose(1, 0, 2).reshape(CH * CH, pairs), weight]
    )
    pair_out, to_cols, to_rows = pair_block(
        lanes, rows, weights, bias.reshape(1, pairs), upstream, rows_n, cols_n
    )
    n_slice = CH * CH // cols_n
    summed = jnp.sum(exchange(to_cols, "col").astype(F32), axis=0)
    grads = summed[:n_own]
    shared = jnp.concatenate(
        [summed[n_own : n_own + n_slice].astype(BF16), two_parts(one_part(summed[n_own + n_slice :]))],
        axis=0,
    )
    shared = jnp.broadcast_to(shared[None], (rows_n,) + shared.shape)
    to_rows = lax.dynamic_update_slice(to_rows, shared, (0, n_own, 0))
    summed = jnp.sum(exchange(to_rows, "row").astype(F32), axis=0)
    part_grads = lax.ppermute(summed[:n_own].astype(BF16), both, to_owner)
    grad_weight = everywhere(summed[n_own : n_own + n_slice], "col")
    grad_weight = grad_weight.reshape(CH * CH, pairs)
    grad_bias = one_part(summed[n_own + n_slice :]).reshape(pairs)
    grads = grads + part_grads.astype(F32)
    grads = grads.reshape(2, own, CH, SEQS).transpose(0, 1, 3, 2).reshape(2, own, SEQS * CH)
    grads = grads.astype(BF16)
    return pair_out, grads[0], grads[1], grad_weight, grad_bias


def solution(mesh):
    placed = (P(("row", "col"), None), P(("row", "col"), None), P(), P(), P("row", "col", None))
    return jax.shard_map(
        local,
        mesh=mesh,
        in_specs=placed,
        out_specs=(
            P("row", "col", None),
            P(("row", "col"), None),
            P(("row", "col"), None),
            P(),
            P(),
        ),
        check_vma=False,
    )
```

time: 206 us -> 170 us (0.83)
  the two profiles are of different devices: /device:TPU:33 before, /device:TPU:25 now
where the time goes in v2:
time: 170 us
  waiting for transfers between devices  48.1 us (28%)
  Pallas kernels  48.1 us (28%)
  starting transfers between devices  40 us (24%)
  blocking collectives  18.7 us (11%)
  local copies, waits for them, and re-layouts  12 us (7%)
  other arithmetic  2.17 us (1%)
    pallas_call x1, Pallas kernels, pair_block(): pl.pallas_call(functools.partial(pair_kernel, steps, across), grid=(2, st...  48.1 us
    all_to_all x4, waiting for transfers between devices, exchange(): lax.all_to_all(x, axis, split_axis=0, concat_axis=0, axis_index_groups=gr...  34.8 us
    all_to_all x4, starting transfers between devices, exchange(): lax.all_to_all(x, axis, split_axis=0, concat_axis=0, axis_index_groups=gr...  25.7 us
    all_to_all x1, blocking collectives, exchange(): lax.all_to_all(x, axis, split_axis=0, concat_axis=0, axis_index_groups=gr...  18.7 us
    ppermute x1, waiting for transfers between devices, local(): part_grads = lax.ppermute(summed[:n_own].astype(BF16), both, to_owner)  9.58 us
    ppermute x1, starting transfers between devices, local(): part = lax.ppermute(mine, both, to_part)  8.11 us
    ppermute x1, starting transfers between devices, local(): part_grads = lax.ppermute(summed[:n_own].astype(BF16), both, to_owner)  4.12 us
    ppermute x1, waiting for transfers between devices, local(): part = lax.ppermute(mine, both, to_part)  3.73 us
  transfers between devices with their start and end apart: 7, of which 4 were waited for; matrix products, arithmetic and copies ran while one was open for 4% of the time, Pallas kernels for 0%

profile of v2, /device:TPU:25, one launch (start us, length us, event | category | flops | bytes accessed | tf_op | source)
XLA Modules:
  0.0 169.9 jit_solution(16824489218627252306)
XLA Ops:
  0.6 1.0 reshape.78
  1.6 0.1 copy.31
  1.8 1.0 reshape.79
  2.8 0.1 copy.32
  2.9 1.0 broadcast_in_dim.13
  4.0 5.5 %all-to-all-start = ((bf16[8,2,192,128]{3,2,1,0:T(8,128)(2,1)}), bf16[8,2,192,128]{3,2,1,0:T(8,128)(2,1)S(1)}, u32[]{:S(2)}, u32[]{:S(2)}) async-start(bf16[8,2,192,128]{3,2,1,0:T(8,128)(2,1)} %broadcast_in_dim.13), calls=%async_computation | async-start | bytes 1572864 | tf_op jit(solution)/shard_map/all_to_all | solution.py:265
  9.5 0.0 copy-start
  9.5 8.1 %collective-permute-start.1 = (bf16[2,192,128]{2,1,0:T(8,128)(2,1)S(1)}, bf16[2,192,128]{2,1,0:T(8,128)(2,1)S(1)}, u32[]{:S(2)}, u32[]{:S(2)}) collective-permute-start(bf16[2,192,128]{2,1,0:T(8,128)(2,1)S(1)} %pad_maximum_fusion.1), channel_id=1, source_target_pairs={{0,0},{1,16},{2,32},{3,48},{4,64},{5,80},{6,96},{7,112},{8,1},{9,1... | collective-permute-start | bytes 294920 | tf_op jit(solution)/shard_map/ppermute | solution.py:302
  17.6 3.7 %collective-permute-done.1 = bf16[2,192,128]{2,1,0:T(8,128)(2,1)S(1)} collective-permute-done((bf16[2,192,128]{2,1,0:T(8,128)(2,1)S(1)}, bf16[2,192,128]{2,1,0:T(8,128)(2,1)S(1)}, u32[]{:S(2)}, u32[]{:S(2)}) %collective-permute-start.1) | collective-permute-done | bytes 98336 | tf_op jit(solution)/shard_map/ppermute | solution.py:302
  21.3 0.0 all-to-all-done
  21.3 1.0 broadcast_in_dim.14
  22.4 6.9 %all-to-all-start.1 = ((bf16[8,2,192,128]{3,2,1,0:T(8,128)(2,1)}), bf16[8,2,192,128]{3,2,1,0:T(8,128)(2,1)S(1)}, u32[]{:S(2)}, u32[]{:S(2)}) async-start(bf16[8,2,192,128]{3,2,1,0:T(8,128)(2,1)} %broadcast_in_dim.14), calls=%async_computation.1 | async-start | bytes 1572864 | tf_op jit(solution)/shard_map/all_to_all | solution.py:265
  29.3 2.1 %collective-permute-start = (bf16[8,2,192,128]{3,2,1,0:T(8,128)(2,1)S(1)}, bf16[8,2,192,128]{3,2,1,0:T(8,128)(2,1)S(1)}, u32[]{:S(2)}, u32[]{:S(2)}) collective-permute-start(bf16[8,2,192,128]{3,2,1,0:T(8,128)(2,1)S(1)} %all-to-all-done), channel_id=1, source_target_pairs={{0,1},{1,0},{2,3},{3,2},{4,5},{5,4},{6,7},{7,6},{8,9},{9,8},{10,11... | collective-permute-start | bytes 2359304 | tf_op jit(solution)/shard_map/ppermute | solution.py:304
  31.4 0.0 copy-done
  31.4 0.1 copy.38
  31.5 0.8 pad_maximum_fusion.weight_ref
  32.3 11.5 %all-to-all-done.1 = bf16[8,2,192,128]{3,2,1,0:T(8,128)(2,1)S(1)} async-done(((bf16[8,2,192,128]{3,2,1,0:T(8,128)(2,1)}), bf16[8,2,192,128]{3,2,1,0:T(8,128)(2,1)S(1)}, u32[]{:S(2)}, u32[]{:S(2)}) %all-to-all-start.1) | async-done | bytes 786464 | tf_op jit(solution)/shard_map/all_to_all | solution.py:265
  43.8 0.5 copy.36
  44.3 0.1 reverse_bitcast_fusion
  44.4 0.8 copy.37
  45.2 1.0 copy.39.row_ref
  46.2 0.0 collective-permute-done
  46.2 0.1 select_bitcast_fusion.1
  46.3 0.1 maximum_bitcast_fusion
  46.5 1.3 copy.33
  47.7 48.1 %shard_map.92 = (bf16[96,48,128]{2,1,0:T(8,128)(2,1)}, bf16[16,464,128]{2,1,0:T(8,128)(2,1)}, bf16[8,464,128]{2,1,0:T(8,128)(2,1)}) custom-call(bf16[2,3072,128]{2,1,0:T(8,128)(2,1)} %bitcast.43, bf16[2,1536,128]{2,1,0:T(8,128)(2,1)} %copy.39.row_ref, bf16[2,1024,128]{2,1,0:T(8,128)(2,1)} %pad_maximum_fusion.weight_ref, f32[1,128]{1,0:T(1,128)} %bitcast.54, ...), custom_call_target="tpu_custom_call" | custom-call | flops 14495514624 | bytes 16777216 | tf_op jit(solution)/shard_map/pallas_call | solution.py:223
  95.9 6.7 %all-to-all-start.2 = ((bf16[16,464,128]{2,1,0:T(8,128)(2,1)}), bf16[16,464,128]{2,1,0:T(8,128)(2,1)S(1)}, u32[]{:S(2)}, u32[]{:S(2)}) async-start(bf16[16,464,128]{2,1,0:T(8,128)(2,1)} %get-tuple-element.9), calls=%async_computation.2 | async-start | bytes 3801088 | tf_op jit(solution)/shard_map/all_to_all | solution.py:265
  102.6 0.0 copy-start.1
  102.6 0.1 pad.3.clone
  102.6 23.3 %all-to-all-done.2 = bf16[16,464,128]{2,1,0:T(8,128)(2,1)S(1)} async-done(((bf16[16,464,128]{2,1,0:T(8,128)(2,1)}), bf16[16,464,128]{2,1,0:T(8,128)(2,1)S(1)}, u32[]{:S(2)}, u32[]{:S(2)}) %all-to-all-start.2) | async-done | bytes 1900576 | tf_op jit(solution)/shard_map/all_to_all | solution.py:265
  125.9 0.3 convert_reduce_fusion
  126.3 0.1 maximum_maximum_fusion
  126.3 0.0 copy-done.1
  126.4 18.7 %all_to_all.25 = bf16[8,464,128]{2,1,0:T(8,128)(2,1)S(1)} all-to-all(bf16[8,464,128]{2,1,0:T(8,128)(2,1)S(1)} %broadcast_dynamic-update-slice_fusion), channel_id=1, replica_groups=mesh['row'=8,'col'=16] {'row'}, dimensions={0} | all-to-all | bytes 1900544 | tf_op jit(solution)/shard_map/all_to_all | solution.py:265
  145.1 0.1 convert_reduce_fusion.1
  145.3 0.8 broadcast_in_dim.34
  146.1 6.6 %all-to-all-start.4 = ((f32[16,64,128]{2,1,0:T(8,128)}), f32[16,64,128]{2,1,0:T(8,128)S(1)}, u32[]{:S(2)}, u32[]{:S(2)}) async-start(f32[16,64,128]{2,1,0:T(8,128)} %broadcast_in_dim.34), calls=%async_computation.4 | async-start | bytes 1048576 | tf_op jit(solution)/shard_map/all_to_all | solution.py:265
  152.7 4.1 %collective-permute-start.2 = (bf16[384,128]{1,0:T(8,128)(2,1)S(1)}, bf16[384,128]{1,0:T(8,128)(2,1)S(1)}, u32[]{:S(2)}, u32[]{:S(2)}) collective-permute-start(bf16[384,128]{1,0:T(8,128)(2,1)S(1)} %slice.55), channel_id=1, source_target_pairs={{0,0},{16,1},{32,2},{48,3},{64,4},{80,5},{96,6},{112,7},{1,8},{17,... | collective-permute-start | bytes 294920 | tf_op jit(solution)/shard_map/ppermute | solution.py:329
  156.9 0.5 slice_reduce_fusion
  157.4 9.6 %collective-permute-done.2 = bf16[384,128]{1,0:T(8,128)(2,1)S(1)} collective-permute-done((bf16[384,128]{1,0:T(8,128)(2,1)S(1)}, bf16[384,128]{1,0:T(8,128)(2,1)S(1)}, u32[]{:S(2)}, u32[]{:S(2)}) %collective-permute-start.2) | collective-permute-done | bytes 98336 | tf_op jit(solution)/shard_map/ppermute | solution.py:329
  167.0 0.2 copy.40
  167.2 0.9 squeeze.6
  168.1 0.2 copy.41
  168.2 0.9 squeeze.7
  169.1 0.0 all-to-all-done.4
  169.1 0.8 copy.44
  (12 shorter events, 0.2 us)
Async XLA Ops:
  4.0 17.3 %all-to-all-start = ((bf16[8,2,192,128]{3,2,1,0:T(8,128)(2,1)}), bf16[8,2,192,128]{3,2,1,0:T(8,128)(2,1)S(1)}, u32[]{:S(2)}, u32[]{:S(2)}) async-start(bf16[8,2,192,128]{3,2,1,0:T(8,128)(2,1)} %broadcast_in_dim.13), calls=%async_computation | async-start | bytes 1572864 | tf_op jit(solution)/shard_map/all_to_all | solution.py:265
  9.5 21.9 %copy-start = (bf16[1024,128]{1,0:T(8,128)(2,1)S(1)}, bf16[1024,128]{1,0:T(8,128)(2,1)}, u32[]{:S(2)}) copy-start(bf16[1024,128]{1,0:T(8,128)(2,1)} %param.7) | copy-start | bytes 786436
  9.5 11.8 %collective-permute-start.1 = (bf16[2,192,128]{2,1,0:T(8,128)(2,1)S(1)}, bf16[2,192,128]{2,1,0:T(8,128)(2,1)S(1)}, u32[]{:S(2)}, u32[]{:S(2)}) collective-permute-start(bf16[2,192,128]{2,1,0:T(8,128)(2,1)S(1)} %pad_maximum_fusion.1), channel_id=1, source_target_pairs={{0,0},{1,16},{2,32},{3,48},{4,64},{5,80},{6,96},{7,112},{8,1},{9,1... | collective-permute-start | bytes 294920 | tf_op jit(solution)/shard_map/ppermute | solution.py:302
  22.4 21.4 %all-to-all-start.1 = ((bf16[8,2,192,128]{3,2,1,0:T(8,128)(2,1)}), bf16[8,2,192,128]{3,2,1,0:T(8,128)(2,1)S(1)}, u32[]{:S(2)}, u32[]{:S(2)}) async-start(bf16[8,2,192,128]{3,2,1,0:T(8,128)(2,1)} %broadcast_in_dim.14), calls=%async_computation.1 | async-start | bytes 1572864 | tf_op jit(solution)/shard_map/all_to_all | solution.py:265
  29.3 16.9 %collective-permute-start = (bf16[8,2,192,128]{3,2,1,0:T(8,128)(2,1)S(1)}, bf16[8,2,192,128]{3,2,1,0:T(8,128)(2,1)S(1)}, u32[]{:S(2)}, u32[]{:S(2)}) collective-permute-start(bf16[8,2,192,128]{3,2,1,0:T(8,128)(2,1)S(1)} %all-to-all-done), channel_id=1, source_target_pairs={{0,1},{1,0},{2,3},{3,2},{4,5},{5,4},{6,7},{7,6},{8,9},{9,8},{10,11... | collective-permute-start | bytes 2359304 | tf_op jit(solution)/shard_map/ppermute | solution.py:304
  95.9 30.1 %all-to-all-start.2 = ((bf16[16,464,128]{2,1,0:T(8,128)(2,1)}), bf16[16,464,128]{2,1,0:T(8,128)(2,1)S(1)}, u32[]{:S(2)}, u32[]{:S(2)}) async-start(bf16[16,464,128]{2,1,0:T(8,128)(2,1)} %get-tuple-element.9), calls=%async_computation.2 | async-start | bytes 3801088 | tf_op jit(solution)/shard_map/all_to_all | solution.py:265
  102.6 23.8 %copy-start.1 = (bf16[8,464,128]{2,1,0:T(8,128)(2,1)S(1)}, bf16[8,464,128]{2,1,0:T(8,128)(2,1)}, u32[]{:S(2)}) copy-start(bf16[8,464,128]{2,1,0:T(8,128)(2,1)} %get-tuple-element.10) | copy-start | bytes 2850820
  146.1 23.0 %all-to-all-start.4 = ((f32[16,64,128]{2,1,0:T(8,128)}), f32[16,64,128]{2,1,0:T(8,128)S(1)}, u32[]{:S(2)}, u32[]{:S(2)}) async-start(f32[16,64,128]{2,1,0:T(8,128)} %broadcast_in_dim.34), calls=%async_computation.4 | async-start | bytes 1048576 | tf_op jit(solution)/shard_map/all_to_all | solution.py:265
  152.7 14.2 %collective-permute-start.2 = (bf16[384,128]{1,0:T(8,128)(2,1)S(1)}, bf16[384,128]{1,0:T(8,128)(2,1)S(1)}, u32[]{:S(2)}, u32[]{:S(2)}) collective-permute-start(bf16[384,128]{1,0:T(8,128)(2,1)S(1)} %slice.55), channel_id=1, source_target_pairs={{0,0},{16,1},{32,2},{48,3},{64,4},{80,5},{96,6},{112,7},{1,8},{17,... | collective-permute-start | bytes 294920 | tf_op jit(solution)/shard_map/ppermute | solution.py:329

commit v3 on v2

--- a/solution.py
+++ b/solution.py
@@ -26,6 +26,18 @@
     once = [jnp.where(odd, parts[(r + 1) % GROUP], parts[r]) for r in range(GROUP)]
     twice = [jnp.where(high, once[(r + 2) % GROUP], once[r]) for r in range(GROUP)]
     return [twice[-q % GROUP] for q in range(GROUP)]
+
+
+def unturned(wide, turn):
+    if turn == 0:
+        return wide
+    return jnp.concatenate(
+        [
+            pltpu.roll(wide[:, n * 128 : (n + 1) * 128], 128 - CH * turn, 1)
+            for n in range(wide.shape[1] // 128)
+        ],
+        axis=1,
+    )
 
 
 def to_tiles(ref, at, wide):
@@ -47,13 +59,11 @@
     bias_ref,
     up_ref,
     pair_ref,
-    cols_ref,
+    grads_ref,
     send_ref,
     squares,
     products,
     packed,
-    grads,
-    row_t,
     drow_acc,
     dweight_acc,
     dweight_sum,
@@ -65,15 +75,13 @@
     groups = BLOCK // GROUP
     depth = quarters * across
     scale = 1.0 / SEQS
-    own = across // send_ref.shape[0]
+    grads = grads_ref.at[0, 0]
     lane = lax.broadcasted_iota(jnp.int32, (TILE, 128), 1) // CH
     odd = (lane % 2).astype(F32).astype(BF16) > 0.5
     high = (lane // 2).astype(F32).astype(BF16) > 0.5
 
     @pl.when(step == 0)
     def _():
-        for m in range(GROUP):
-            row_t[m] = row_ref[0, m * depth : (m + 1) * depth, :].T
         drow_acc[...] = jnp.zeros_like(drow_acc)
         dweight_acc[...] = jnp.zeros_like(dweight_acc)
 
@@ -150,30 +158,6 @@
 
     lax.fori_loop(0, quarters, by_channel, 0)
 
-    def unturned(wide, turn):
-        if turn == 0:
-            return wide
-        return jnp.concatenate(
-            [
-                pltpu.roll(wide[:, n * 128 : (n + 1) * 128], 128 - CH * turn, 1)
-                for n in range(wide.shape[1] // 128)
-            ],
-            axis=1,
-        )
-
-    for n in range(0, BLOCK * CH, 256):
-        d_lane = None
-        for m in range(GROUP):
-            wide = jnp.dot(
-                row_t[m], from_tiles(grads, m, n // 128, 2), preferred_element_type=F32
-            )
-            wide = unturned(wide, m)
-            d_lane = wide if d_lane is None else d_lane + wide
-        d_lane = (d_lane.T * scale).astype(BF16)
-        for r in range(256 // CH):
-            residue = step * BLOCK + n // CH + r
-            to_row = pl.multiple_of((term * own + residue % own) * CH, CH)
-            cols_ref[residue // own, pl.ds(to_row, CH), :] = d_lane[r * CH : (r + 1) * CH]
     for m in range(GROUP):
         drow_acc[m * depth : (m + 1) * depth, :] += jnp.dot(
             from_tiles(grads, m), turned_lanes(m), preferred_element_type=F32
@@ -202,24 +186,81 @@
         def _():
             send_ref[:, :count, :] = sent
             whole = (dweight_sum[...] + flat).astype(BF16)
-            peers = cols_ref.shape[0]
+            peers = send_ref.shape[0]
             end = 2 * count + whole.shape[0] // peers
-            cols_ref[:, 2 * count : end, :] = whole.reshape(peers, -1, whole.shape[1])
+            send_ref[:, 2 * count : end, :] = whole.reshape(peers, -1, whole.shape[1])
             d_bias = jnp.sum(dbias_acc[...], axis=0, keepdims=True)
             first = d_bias.astype(BF16).astype(F32)
             place = lax.broadcasted_iota(jnp.int32, (TILE, 128), 0)
             rows = jnp.where(place == 0, first, jnp.where(place == 1, d_bias - first, 0.0))
             for r in range(peers):
-                cols_ref[r, end : end + TILE, :] = rows.astype(BF16)
-
-
-def pair_block(lanes, rows, weights, bias, upstream, row_peers, col_peers):
+                send_ref[r, end : end + TILE, :] = rows.astype(BF16)
+
+
+def lane_kernel(across, core_ref, grads_ref, row_ref, cols_ref, row_t):
+    term, step = pl.program_id(0), pl.program_id(1)
+    depth = CH // GROUP * across
+    _, owners, height, _ = cols_ref.shape
+    own = height // (2 * CH)
+    core = core_ref[0]
+
+    @pl.when(step == 0)
+    def _():
+        for m in range(GROUP):
+            row_t[m] = row_ref[0, m * depth : (m + 1) * depth, :].T
+
+    for n in range(0, BLOCK * CH, 256):
+        d_lane = None
+        for m in range(GROUP):
+            wide = jnp.dot(
+                row_t[m],
+                from_tiles(grads_ref.at[0, 0], m, n // 128, 2),
+                preferred_element_type=F32,
+            )
+            wide = unturned(wide, m)
+            d_lane = wide if d_lane is None else d_lane + wide
+        d_lane = (d_lane.T * (1.0 / SEQS)).astype(BF16)
+        for r in range(256 // CH):
+            residue = step * BLOCK + n // CH + r
+            owner = residue // own
+            place = (owner + core) % 2
+            to_row = pl.multiple_of((term * own + residue % own) * CH, CH)
+            cols_ref[place, owner // 2, pl.ds(to_row, CH), :] = d_lane[r * CH : (r + 1) * CH]
+
+
+def lane_block(core, grads, rows, own):
+    _, steps, _, groups, depth, _ = grads.shape
+    across = depth // (CH // GROUP)
+    owners = steps * BLOCK // own
+    return pl.pallas_call(
+        functools.partial(lane_kernel, across),
+        grid=(2, steps),
+        in_specs=[
+            pl.BlockSpec(memory_space=pltpu.SMEM),
+            pl.BlockSpec(
+                (1, 1, GROUP, groups, depth, 128), lambda t, s: (t, s, 0, 0, 0, 0)
+            ),
+            pl.BlockSpec((1, CH * across, SEQS), lambda t, s: (t, 0, 0)),
+        ],
+        out_specs=pl.BlockSpec((2, owners // 2, 2 * own * CH, SEQS), lambda t, s: (0, 0, 0, 0)),
+        out_shape=jax.ShapeDtypeStruct((2, owners // 2, 2 * own * CH, SEQS), BF16),
+        scratch_shapes=[pltpu.VMEM((GROUP, SEQS, depth), BF16)],
+        compiler_params=pltpu.CompilerParams(vmem_limit_bytes=40 * 1024 * 1024),
+        cost_estimate=pl.CostEstimate(
+            flops=4 * steps * BLOCK * across * CH * CH * SEQS,
+            bytes_accessed=24 * 1024 * 1024,
+            transcendentals=0,
+        ),
+    )(core, grads, rows)
+
+
+def pair_block(lanes, rows, weights, bias, upstream, row_peers):
     count, across, pairs = upstream.shape
     steps = count // BLOCK
     width = BLOCK * CH
     depth = CH // GROUP * across
     once = lambda t, s: (0, 0)
-    sent = 2 * CH * across // row_peers + CH * CH // col_peers + TILE
+    sent = 2 * CH * across // row_peers + CH * CH // row_peers + TILE
     return pl.pallas_call(
         functools.partial(pair_kernel, steps, across),
         grid=(2, steps),
@@ -232,20 +273,20 @@
         ],
         out_specs=[
             pl.BlockSpec((BLOCK, across, pairs), lambda t, s: (t * s, 0, 0)),
-            pl.BlockSpec((col_peers, sent, SEQS), lambda t, s: (0, 0, 0)),
+            pl.BlockSpec(
+                (1, 1, GROUP, width // 128, depth, 128), lambda t, s: (t, s, 0, 0, 0, 0)
+            ),
             pl.BlockSpec((row_peers, sent, SEQS), lambda t, s: (0, 0, 0)),
         ],
         out_shape=[
             jax.ShapeDtypeStruct((count, across, pairs), BF16),
-            jax.ShapeDtypeStruct((col_peers, sent, SEQS), BF16),
+            jax.ShapeDtypeStruct((2, steps, GROUP, width // 128, depth, 128), BF16),
             jax.ShapeDtypeStruct((row_peers, sent, SEQS), BF16),
         ],
         scratch_shapes=[
             pltpu.VMEM((count, across, pairs), F32),
             pltpu.VMEM((GROUP, width // 128, depth, 128), BF16),
             pltpu.VMEM((GROUP, width // 128, depth, 128), BF16),
-            pltpu.VMEM((GROUP, width // 128, depth, 128), BF16),
-            pltpu.VMEM((GROUP, SEQS, depth), BF16),
             pltpu.VMEM((CH * across, SEQS), F32),
             pltpu.VMEM((GROUP, pairs, CH * CH), F32),
             pltpu.VMEM((CH * CH, pairs), F32),
@@ -254,8 +295,8 @@
         ],
         compiler_params=pltpu.CompilerParams(vmem_limit_bytes=60 * 1024 * 1024),
         cost_estimate=pl.CostEstimate(
-            flops=12 * count * across * CH * CH * SEQS * 2,
-            bytes_accessed=16 * 1024 * 1024,
+            flops=10 * count * across * CH * CH * SEQS * 2,
+            bytes_accessed=32 * 1024 * 1024,
             transcendentals=0,
         ),
     )(lanes, rows, weights, bias, upstream)
@@ -313,24 +354,33 @@
     weights = jnp.stack(
         [weight.reshape(CH, CH, pairs).transpose(1, 0, 2).reshape(CH * CH, pairs), weight]
     )
-    pair_out, to_cols, to_rows = pair_block(
-        lanes, rows, weights, bias.reshape(1, pairs), upstream, rows_n, cols_n
-    )
-    n_slice = CH * CH // cols_n
-    summed = jnp.sum(exchange(to_cols, "col").astype(F32), axis=0)
-    grads = summed[:n_own]
-    shared = jnp.concatenate(
-        [summed[n_own : n_own + n_slice].astype(BF16), two_parts(one_part(summed[n_own + n_slice :]))],
-        axis=0,
-    )
-    shared = jnp.broadcast_to(shared[None], (rows_n,) + shared.shape)
-    to_rows = lax.dynamic_update_slice(to_rows, shared, (0, n_own, 0))
-    summed = jnp.sum(exchange(to_rows, "row").astype(F32), axis=0)
+    pair_out, g_terms, to_rows = pair_block(
+        lanes, rows, weights, bias.reshape(1, pairs), upstream, rows_n
+    )
+    n_slice = CH * CH // rows_n
+
+    def with_bias(x):
+        return jnp.concatenate(
+            [x[:n_slice].astype(BF16), two_parts(one_part(x[n_slice:]))], axis=0
+        )
+
+    sent = exchange(to_rows, "row")
+    core = (lax.axis_index("col") % 2).astype(jnp.int32).reshape(1)
+    to_cols = lane_block(core, g_terms, rows, own)
+    other = lax.ppermute(to_cols[1], "col", other_core)
+    summed = jnp.sum(sent.astype(F32), axis=0)
     part_grads = lax.ppermute(summed[:n_own].astype(BF16), both, to_owner)
-    grad_weight = everywhere(summed[n_own : n_own + n_slice], "col")
+    shared = with_bias(summed[n_own:])
+    shared_other = lax.ppermute(shared, "col", other_core)
+    shared = with_bias(shared.astype(F32) + shared_other.astype(F32))
+    to_cols = (to_cols[0].astype(F32) + other.astype(F32)).astype(BF16)
+    shared = jnp.broadcast_to(shared[None], (cols_n // 2,) + shared.shape)
+    sent = exchange(jnp.concatenate([to_cols, shared], axis=1), "col", same_core)
+    summed = jnp.sum(sent.astype(F32), axis=0)
+    grad_weight = everywhere(summed[n_own : n_own + n_slice], "row")
     grad_weight = grad_weight.reshape(CH * CH, pairs)
     grad_bias = one_part(summed[n_own + n_slice :]).reshape(pairs)
-    grads = grads + part_grads.astype(F32)
+    grads = summed[:n_own] + part_grads.astype(F32)
     grads = grads.reshape(2, own, CH, SEQS).transpose(0, 1, 3, 2).reshape(2, own, SEQS * CH)
     grads = grads.astype(BF16)
     return pair_out, grads[0], grads[1], grad_weight, grad_bias

time: 170 us -> 161 us (0.947)
  the two profiles are of different devices: /device:TPU:25 before, /device:TPU:33 now
where the time goes in v3:
time: 161 us; the launch traced here: 158 us
  Pallas kernels  56.1 us (35%)
  waiting for transfers between devices  50 us (31%)
  starting transfers between devices  34.4 us (21%)
  local copies, waits for them, and re-layouts  12 us (7%)
  other arithmetic  4.69 us (3%)
    pallas_call x1, Pallas kernels, pair_block(): pl.pallas_call(functools.partial(pair_kernel, steps, across), grid=(2, st...  44.7 us
    all_to_all x5, waiting for transfers between devices, exchange(): lax.all_to_all(x, axis, split_axis=0, concat_axis=0, axis_index_groups=gr...  41.5 us
    all_to_all x5, starting transfers between devices, exchange(): lax.all_to_all(x, axis, split_axis=0, concat_axis=0, axis_index_groups=gr...  26.2 us
    pallas_call x1, Pallas kernels, lane_block(): pl.pallas_call(functools.partial(lane_kernel, across), grid=(2, steps), i...  11.4 us
    ppermute x1, waiting for transfers between devices, local(): part = lax.ppermute(mine, both, to_part)  8.58 us
  transfers between devices with their start and end apart: 10, of which 6 were waited for; matrix products, arithmetic and copies ran while one was open for 6% of the time, Pallas kernels for 7%

profile of v3, /device:TPU:33, one launch (start us, length us, event | category | flops | bytes accessed | tf_op | source)
XLA Modules:
  0.0 158.1 jit_solution(16602421201631347658)
XLA Ops:
  0.6 1.0 reshape.107
  1.6 0.1 copy.33
  1.8 1.0 reshape.108
  2.8 0.1 copy.34
  2.9 1.0 broadcast_in_dim.11
  4.0 5.4 %all-to-all-start = ((bf16[8,2,192,128]{3,2,1,0:T(8,128)(2,1)}), bf16[8,2,192,128]{3,2,1,0:T(8,128)(2,1)S(1)}, u32[]{:S(2)}, u32[]{:S(2)}) async-start(bf16[8,2,192,128]{3,2,1,0:T(8,128)(2,1)} %broadcast_in_dim.11), calls=%async_computation | async-start | bytes 1572864 | tf_op jit(solution)/shard_map/all_to_all | solution.py:306
  9.4 0.0 copy-start.1
  9.4 3.0 %collective-permute-start.1 = (bf16[2,192,128]{2,1,0:T(8,128)(2,1)S(1)}, bf16[2,192,128]{2,1,0:T(8,128)(2,1)S(1)}, u32[]{:S(2)}, u32[]{:S(2)}) collective-permute-start(bf16[2,192,128]{2,1,0:T(8,128)(2,1)S(1)} %pad_maximum_fusion.2), channel_id=1, source_target_pairs={{0,0},{1,16},{2,32},{3,48},{4,64},{5,80},{6,96},{7,112},{8,1},{9,1... | collective-permute-start | bytes 294920 | tf_op jit(solution)/shard_map/ppermute | solution.py:343
  12.4 8.6 %collective-permute-done.1 = bf16[2,192,128]{2,1,0:T(8,128)(2,1)S(1)} collective-permute-done((bf16[2,192,128]{2,1,0:T(8,128)(2,1)S(1)}, bf16[2,192,128]{2,1,0:T(8,128)(2,1)S(1)}, u32[]{:S(2)}, u32[]{:S(2)}) %collective-permute-start.1) | collective-permute-done | bytes 98336 | tf_op jit(solution)/shard_map/ppermute | solution.py:343
  20.9 0.3 all-to-all-done
  21.2 1.0 broadcast_in_dim.12
  22.3 7.5 %all-to-all-start.1 = ((bf16[8,2,192,128]{3,2,1,0:T(8,128)(2,1)}), bf16[8,2,192,128]{3,2,1,0:T(8,128)(2,1)S(1)}, u32[]{:S(2)}, u32[]{:S(2)}) async-start(bf16[8,2,192,128]{3,2,1,0:T(8,128)(2,1)} %broadcast_in_dim.12), calls=%async_computation.1 | async-start | bytes 1572864 | tf_op jit(solution)/shard_map/all_to_all | solution.py:306
  29.7 1.1 collective-permute-start
  30.8 0.0 copy-done.1
  30.8 0.1 copy.40
  30.9 0.8 pad_maximum_fusion.1.weight_ref
  31.8 12.5 %all-to-all-done.1 = bf16[8,2,192,128]{3,2,1,0:T(8,128)(2,1)S(1)} async-done(((bf16[8,2,192,128]{3,2,1,0:T(8,128)(2,1)}), bf16[8,2,192,128]{3,2,1,0:T(8,128)(2,1)S(1)}, u32[]{:S(2)}, u32[]{:S(2)}) %all-to-all-start.1) | async-done | bytes 786464 | tf_op jit(solution)/shard_map/all_to_all | solution.py:306
  44.3 0.5 copy.38
  44.8 0.1 reverse_bitcast_fusion
  44.9 0.8 copy.39
  45.7 1.0 copy.41.row_ref
  46.7 0.0 collective-permute-done
  46.7 0.1 select_bitcast_fusion.1
  46.8 0.1 maximum_bitcast_fusion
  47.0 1.3 copy.35
  48.3 44.7 %shard_map.92 = (bf16[96,48,128]{2,1,0:T(8,128)(2,1)}, bf16[2,3,4,8,384,128]{5,4,3,2,1,0:T(8,128)(2,1)}, bf16[8,528,128]{2,1,0:T(8,128)(2,1)}) custom-call(bf16[2,3072,128]{2,1,0:T(8,128)(2,1)} %bitcast.58, bf16[2,1536,128]{2,1,0:T(8,128)(2,1)} %copy.41.row_ref, bf16[2,1024,128]{2,1,0:T(8,128)(2,1)} %pad_maximum_fusion.1.weight_ref, f32[1,128]{1,0:T(1,128)} %bitcast.69, ...), custom_call_target="tpu_custom_call" | custom-call | flops 12079595520 | bytes 33554432 | tf_op jit(solution)/shard_map/pallas_call | solution.py:264
  93.0 0.0 copy-start
  93.0 3.7 %all-to-all-start.2 = ((bf16[8,528,128]{2,1,0:T(8,128)(2,1)}), bf16[8,528,128]{2,1,0:T(8,128)(2,1)S(1)}, u32[]{:S(2)}, u32[]{:S(2)}) async-start(bf16[8,528,128]{2,1,0:T(8,128)(2,1)} %get-tuple-element.10), calls=%async_computation.2 | async-start | bytes 2162688 | tf_op jit(solution)/shard_map/all_to_all | solution.py:306
  96.7 0.1 pad.9.clone
  96.8 0.0 copy-done
  96.8 11.4 %shard_map.93 = bf16[2,8,384,128]{3,2,1,0:T(8,128)(2,1)S(1)} custom-call(s32[1]{0:T(128)} %bitcast.19.core_ref, bf16[2,3,4,8,384,128]{5,4,3,2,1,0:T(8,128)(2,1)} %get-tuple-element.9.grads_ref, bf16[2,1536,128]{2,1,0:T(8,128)(2,1)S(1)} %copy-done), custom_call_target="tpu_custom_call" | custom-call | flops 2415919104 | bytes 25165824 | tf_op jit(solution)/shard_map/pallas_call | solution.py:235
  108.2 0.1 slice_bitcast_fusion
  108.3 0.9 collective-permute-start.2
  109.1 5.3 %all-to-all-done.2 = bf16[8,528,128]{2,1,0:T(8,128)(2,1)S(1)} async-done(((bf16[8,528,128]{2,1,0:T(8,128)(2,1)}), bf16[8,528,128]{2,1,0:T(8,128)(2,1)S(1)}, u32[]{:S(2)}, u32[]{:S(2)}) %all-to-all-start.2) | async-done | bytes 1081376 | tf_op jit(solution)/shard_map/all_to_all | solution.py:306
  114.4 0.1 convert_reduce_fusion.1
  114.6 0.1 maximum_maximum_fusion
  114.7 0.9 collective-permute-start.3
  115.6 0.0 collective-permute-done.2
  115.6 1.3 fusion
  116.9 0.0 collective-permute-done.3
  116.9 0.1 convert_add_fusion.1
  117.1 0.1 maximum_maximum_fusion.1
  117.2 1.0 pad_maximum_fusion
  118.3 5.3 %all-to-all-start.3 = ((bf16[8,528,128]{2,1,0:T(8,128)(2,1)}), bf16[8,528,128]{2,1,0:T(8,128)(2,1)S(1)}, u32[]{:S(2)}, u32[]{:S(2)}) async-start(bf16[8,528,128]{2,1,0:T(8,128)(2,1)} %pad_maximum_fusion), calls=%async_computation.3 | async-start | bytes 2162688 | tf_op jit(solution)/shard_map/all_to_all | solution.py:306
  123.5 2.5 %collective-permute-start.4 = (bf16[384,128]{1,0:T(8,128)(2,1)S(1)}, bf16[384,128]{1,0:T(8,128)(2,1)S(1)}, u32[]{:S(2)}, u32[]{:S(2)}) collective-permute-start(bf16[384,128]{1,0:T(8,128)(2,1)S(1)} %slice.69), channel_id=1, source_target_pairs={{0,0},{16,1},{32,2},{48,3},{64,4},{80,5},{96,6},{112,7},{1,8},{17,... | collective-permute-start | bytes 294920 | tf_op jit(solution)/shard_map/ppermute | solution.py:372
  126.0 14.3 %all-to-all-done.3 = bf16[8,528,128]{2,1,0:T(8,128)(2,1)S(1)} async-done(((bf16[8,528,128]{2,1,0:T(8,128)(2,1)}), bf16[8,528,128]{2,1,0:T(8,128)(2,1)S(1)}, u32[]{:S(2)}, u32[]{:S(2)}) %all-to-all-start.3) | async-done | bytes 1081376 | tf_op jit(solution)/shard_map/all_to_all | solution.py:306
  140.3 0.1 convert_reduce_fusion
  140.4 0.8 broadcast_in_dim.14
  141.3 4.3 %all-to-all-start.4 = ((f32[8,128,128]{2,1,0:T(8,128)}), f32[8,128,128]{2,1,0:T(8,128)S(1)}, u32[]{:S(2)}, u32[]{:S(2)}) async-start(f32[8,128,128]{2,1,0:T(8,128)} %broadcast_in_dim.14), calls=%async_computation.4 | async-start | bytes 1048576 | tf_op jit(solution)/shard_map/all_to_all | solution.py:306
  145.6 0.0 collective-permute-done.4
  145.7 0.2 copy.43
  145.8 0.9 squeeze.11
  146.7 0.2 copy.44
  146.9 0.9 squeeze.12
  147.7 0.5 slice_reduce_fusion
  148.3 9.1 %all-to-all-done.4 = f32[8,128,128]{2,1,0:T(8,128)S(1)} async-done(((f32[8,128,128]{2,1,0:T(8,128)}), f32[8,128,128]{2,1,0:T(8,128)S(1)}, u32[]{:S(2)}, u32[]{:S(2)}) %all-to-all-start.4) | async-done | bytes 524320 | tf_op jit(solution)/shard_map/all_to_all | solution.py:306
  157.4 0.8 copy.46
  (17 shorter events, 0.2 us)
Async XLA Ops:
  4.0 17.2 %all-to-all-start = ((bf16[8,2,192,128]{3,2,1,0:T(8,128)(2,1)}), bf16[8,2,192,128]{3,2,1,0:T(8,128)(2,1)S(1)}, u32[]{:S(2)}, u32[]{:S(2)}) async-start(bf16[8,2,192,128]{3,2,1,0:T(8,128)(2,1)} %broadcast_in_dim.11), calls=%async_computation | async-start | bytes 1572864 | tf_op jit(solution)/shard_map/all_to_all | solution.py:306
  9.4 21.5 %copy-start.1 = (bf16[1024,128]{1,0:T(8,128)(2,1)S(1)}, bf16[1024,128]{1,0:T(8,128)(2,1)}, u32[]{:S(2)}) copy-start(bf16[1024,128]{1,0:T(8,128)(2,1)} %param.7) | copy-start | bytes 786436
  9.4 11.6 %collective-permute-start.1 = (bf16[2,192,128]{2,1,0:T(8,128)(2,1)S(1)}, bf16[2,192,128]{2,1,0:T(8,128)(2,1)S(1)}, u32[]{:S(2)}, u32[]{:S(2)}) collective-permute-start(bf16[2,192,128]{2,1,0:T(8,128)(2,1)S(1)} %pad_maximum_fusion.2), channel_id=1, source_target_pairs={{0,0},{1,16},{2,32},{3,48},{4,64},{5,80},{6,96},{7,112},{8,1},{9,1... | collective-permute-start | bytes 294920 | tf_op jit(solution)/shard_map/ppermute | solution.py:343
  22.3 22.0 %all-to-all-start.1 = ((bf16[8,2,192,128]{3,2,1,0:T(8,128)(2,1)}), bf16[8,2,192,128]{3,2,1,0:T(8,128)(2,1)S(1)}, u32[]{:S(2)}, u32[]{:S(2)}) async-start(bf16[8,2,192,128]{3,2,1,0:T(8,128)(2,1)} %broadcast_in_dim.12), calls=%async_computation.1 | async-start | bytes 1572864 | tf_op jit(solution)/shard_map/all_to_all | solution.py:306
  29.7 17.0 %collective-permute-start = (bf16[8,2,192,128]{3,2,1,0:T(8,128)(2,1)S(1)}, bf16[8,2,192,128]{3,2,1,0:T(8,128)(2,1)S(1)}, u32[]{:S(2)}, u32[]{:S(2)}) collective-permute-start(bf16[8,2,192,128]{3,2,1,0:T(8,128)(2,1)S(1)} %all-to-all-done), channel_id=1, source_target_pairs={{0,1},{1,0},{2,3},{3,2},{4,5},{5,4},{6,7},{7,6},{8,9},{9,8},{10,11... | collective-permute-start | bytes 2359304 | tf_op jit(solution)/shard_map/ppermute | solution.py:345
  93.0 3.8 %copy-start = (bf16[2,1536,128]{2,1,0:T(8,128)(2,1)S(1)}, bf16[2,1536,128]{2,1,0:T(8,128)(2,1)}, u32[]{:S(2)}) copy-start(bf16[2,1536,128]{2,1,0:T(8,128)(2,1)} %copy.41.row_ref) | copy-start | bytes 2359300
  93.0 21.4 %all-to-all-start.2 = ((bf16[8,528,128]{2,1,0:T(8,128)(2,1)}), bf16[8,528,128]{2,1,0:T(8,128)(2,1)S(1)}, u32[]{:S(2)}, u32[]{:S(2)}) async-start(bf16[8,528,128]{2,1,0:T(8,128)(2,1)} %get-tuple-element.10), calls=%async_computation.2 | async-start | bytes 2162688 | tf_op jit(solution)/shard_map/all_to_all | solution.py:306
  108.3 7.3 %collective-permute-start.2 = (bf16[8,384,128]{2,1,0:T(8,128)(2,1)S(1)}, bf16[8,384,128]{2,1,0:T(8,128)(2,1)}, u32[]{:S(2)}, u32[]{:S(2)}) collective-permute-start(bf16[8,384,128]{2,1,0:T(8,128)(2,1)S(1)} %slice_bitcast_fusion), channel_id=1, source_target_pairs={{0,1},{1,0},{2,3},{3,2},{4,5},{5,4},{6,7},{7,6},{8,9},{9,8},{10,11... | collective-permute-start | bytes 2359304 | tf_op jit(solution)/shard_map/ppermute | solution.py:370
  114.7 2.2 %collective-permute-start.3 = (bf16[144,128]{1,0:T(8,128)(2,1)S(1)}, bf16[144,128]{1,0:T(8,128)(2,1)S(1)}, u32[]{:S(2)}, u32[]{:S(2)}) collective-permute-start(bf16[144,128]{1,0:T(8,128)(2,1)S(1)} %maximum_maximum_fusion), channel_id=1, source_target_pairs={{0,1},{1,0},{2,3},{3,2},{4,5},{5,4},{6,7},{7,6},{8,9},{9,8},{10,11... | collective-permute-start | bytes 110600 | tf_op jit(solution)/shard_map/ppermute | solution.py:374
  118.3 22.0 %all-to-all-start.3 = ((bf16[8,528,128]{2,1,0:T(8,128)(2,1)}), bf16[8,528,128]{2,1,0:T(8,128)(2,1)S(1)}, u32[]{:S(2)}, u32[]{:S(2)}) async-start(bf16[8,528,128]{2,1,0:T(8,128)(2,1)} %pad_maximum_fusion), calls=%async_computation.3 | async-start | bytes 2162688 | tf_op jit(solution)/shard_map/all_to_all | solution.py:306
  123.5 22.1 %collective-permute-start.4 = (bf16[384,128]{1,0:T(8,128)(2,1)S(1)}, bf16[384,128]{1,0:T(8,128)(2,1)S(1)}, u32[]{:S(2)}, u32[]{:S(2)}) collective-permute-start(bf16[384,128]{1,0:T(8,128)(2,1)S(1)} %slice.69), channel_id=1, source_target_pairs={{0,0},{16,1},{32,2},{48,3},{64,4},{80,5},{96,6},{112,7},{1,8},{17,... | collective-permute-start | bytes 294920 | tf_op jit(solution)/shard_map/ppermute | solution.py:372
  141.3 16.1 %all-to-all-start.4 = ((f32[8,128,128]{2,1,0:T(8,128)}), f32[8,128,128]{2,1,0:T(8,128)S(1)}, u32[]{:S(2)}, u32[]{:S(2)}) async-start(f32[8,128,128]{2,1,0:T(8,128)} %broadcast_in_dim.14), calls=%async_computation.4 | async-start | bytes 1048576 | tf_op jit(solution)/shard_map/all_to_all | solution.py:306

commit v4 on v3

--- a/solution.py
+++ b/solution.py
@@ -11,7 +11,7 @@
 CH = 32
 SEQS = 128
 GROUP = 4
-BLOCK = 32
+BLOCK = 48
 TILE = 16
 BF16 = jnp.bfloat16
 F32 = jnp.float32
@@ -51,7 +51,6 @@
 
 
 def pair_kernel(
-    steps,
     across,
     lane_ref,
     row_ref,
@@ -64,30 +63,23 @@
     squares,
     products,
     packed,
+    g_packed,
+    g_tiles,
     drow_acc,
     dweight_acc,
     dweight_sum,
     drow_turned,
     dbias_acc,
+    sent_sems,
 ):
-    term, step = pl.program_id(0), pl.program_id(1)
+    term = pl.program_id(0)
     quarters = CH // GROUP
-    groups = BLOCK // GROUP
+    groups = lane_ref.shape[1] // (CH * GROUP)
     depth = quarters * across
     scale = 1.0 / SEQS
-    grads = grads_ref.at[0, 0]
     lane = lax.broadcasted_iota(jnp.int32, (TILE, 128), 1) // CH
     odd = (lane % 2).astype(F32).astype(BF16) > 0.5
     high = (lane // 2).astype(F32).astype(BF16) > 0.5
-
-    @pl.when(step == 0)
-    def _():
-        drow_acc[...] = jnp.zeros_like(drow_acc)
-        dweight_acc[...] = jnp.zeros_like(dweight_acc)
-
-    @pl.when((step == 0) & (term == 0))
-    def _():
-        dbias_acc[...] = jnp.zeros_like(dbias_acc)
 
     def turned_lanes(m):
         return jnp.concatenate(
@@ -135,14 +127,19 @@
         d_pre = (active * up.astype(F32)).astype(BF16)
 
         for g in range(groups):
-            place = step * BLOCK + GROUP * g + q
+            place = GROUP * g + q
             here = squared[g * across : (g + 1) * across]
             pair_ref[GROUP * g + q] = ((here + squares[place]) * 0.5).astype(BF16)
             squares[place] = here
-        to_tiles(products, q, contract(d_pre, weight_q, (1, 1)).astype(BF16))
-        dweight_acc[q] += contract(d_pre, outer, (0, 0))
-        dbias_acc[...] += jnp.sum(
-            d_pre.astype(F32).reshape(groups * across // 8, 8, 128), axis=0
+        to_tiles(g_packed, q, contract(d_pre, weight_q, (1, 1)).astype(BF16))
+        dweight_acc[q] = contract(d_pre, outer, (0, 0))
+        d_bias = jnp.sum(d_pre.astype(F32).reshape(groups * across // 8, 8, 128), axis=0)
+        dbias_acc[...] = d_bias + jnp.where((term == 0) & (q == 0), 0.0, dbias_acc[...])
+
+    def g_copy(term, k):
+        rows = pl.ds(pl.multiple_of(k * across, TILE), across)
+        return pltpu.make_async_copy(
+            g_tiles.at[term, :, :, rows, :], grads_ref.at[term, :, :, rows, :], sent_sems.at[term, k]
         )
 
     def by_channel(k, _):
@@ -150,54 +147,60 @@
         for g in range(groups):
             for t in range(0, across, TILE):
                 parts = [
-                    products[q, k, pl.ds(g * across + t, TILE), :] for q in range(GROUP)
+                    g_packed[q, k, pl.ds(g * across + t, TILE), :] for q in range(GROUP)
                 ]
                 for m, tile in enumerate(spread(parts, odd, high)):
-                    grads[m, g, pl.ds(to_rows + t, TILE), :] = tile
+                    g_tiles[term, m, g, pl.ds(to_rows + t, TILE), :] = tile
+        g_copy(term, k).start()
         return _
 
     lax.fori_loop(0, quarters, by_channel, 0)
 
     for m in range(GROUP):
-        drow_acc[m * depth : (m + 1) * depth, :] += jnp.dot(
-            from_tiles(grads, m), turned_lanes(m), preferred_element_type=F32
+        tiles = from_tiles(g_tiles.at[term], m)
+        drow_acc[pl.ds(m * depth, depth)] = jnp.dot(
+            tiles, turned_lanes(m), preferred_element_type=F32
         )
 
-    @pl.when(step == steps - 1)
+    for m in range(GROUP):
+        for k in range(quarters):
+            block = drow_acc[pl.ds(m * depth + k * across, across), :]
+            drow_turned[pl.ds(k * GROUP + m, across, stride=CH), :] = block * scale
+    sent = drow_turned[...].astype(BF16).reshape(send_ref.shape[0], -1, SEQS)
+    count = sent.shape[1]
+    total = dweight_acc[0]
+    for q in range(1, GROUP):
+        total = total + unturned(dweight_acc[q], q)
+    flat = total.T
+
+    @pl.when(term == 0)
     def _():
-        for m in range(GROUP):
+        send_ref[:, count : 2 * count, :] = sent
+        for k in range(CH):
+            dweight_sum[pl.ds(k, CH, stride=CH), :] = flat[k * CH : (k + 1) * CH]
+
+    @pl.when(term == 1)
+    def _():
+        send_ref[:, :count, :] = sent
+        whole = (dweight_sum[...] + flat).astype(BF16)
+        peers = send_ref.shape[0]
+        end = 2 * count + whole.shape[0] // peers
+        send_ref[:, 2 * count : end, :] = whole.reshape(peers, -1, whole.shape[1])
+        d_bias = jnp.sum(dbias_acc[...], axis=0, keepdims=True)
+        first = d_bias.astype(BF16).astype(F32)
+        place = lax.broadcasted_iota(jnp.int32, (TILE, 128), 0)
+        rows = jnp.where(place == 0, first, jnp.where(place == 1, d_bias - first, 0.0))
+        for r in range(peers):
+            send_ref[r, end : end + TILE, :] = rows.astype(BF16)
+
+    @pl.when(term == 1)
+    def _():
+        for t in range(2):
             for k in range(quarters):
-                block = drow_acc[pl.ds(m * depth + k * across, across), :]
-                drow_turned[pl.ds(k * GROUP + m, across, stride=CH), :] = block * scale
-        sent = drow_turned[...].astype(BF16).reshape(send_ref.shape[0], -1, SEQS)
-        count = sent.shape[1]
-        total = dweight_acc[0]
-        for q in range(1, GROUP):
-            total = total + unturned(dweight_acc[q], q)
-        flat = total.T
-
-        @pl.when(term == 0)
-        def _():
-            send_ref[:, count : 2 * count, :] = sent
-            for k in range(CH):
-                dweight_sum[pl.ds(k, CH, stride=CH), :] = flat[k * CH : (k + 1) * CH]
-
-        @pl.when(term == 1)
-        def _():
-            send_ref[:, :count, :] = sent
-            whole = (dweight_sum[...] + flat).astype(BF16)
-            peers = send_ref.shape[0]
-            end = 2 * count + whole.shape[0] // peers
-            send_ref[:, 2 * count : end, :] = whole.reshape(peers, -1, whole.shape[1])
-            d_bias = jnp.sum(dbias_acc[...], axis=0, keepdims=True)
-            first = d_bias.astype(BF16).astype(F32)
-            place = lax.broadcasted_iota(jnp.int32, (TILE, 128), 0)
-            rows = jnp.where(place == 0, first, jnp.where(place == 1, d_bias - first, 0.0))
-            for r in range(peers):
-                send_ref[r, end : end + TILE, :] = rows.astype(BF16)
-
-
-def lane_kernel(across, core_ref, grads_ref, row_ref, cols_ref, row_t):
+                g_copy(t, k).wait()
+
+
+def lane_kernel(across, core_ref, grads_ref, row_ref, mine_ref, theirs_ref, cols_ref, row_t):
     term, step = pl.program_id(0), pl.program_id(1)
     depth = CH // GROUP * across
     _, owners, height, _ = cols_ref.shape
@@ -214,7 +217,7 @@
         for m in range(GROUP):
             wide = jnp.dot(
                 row_t[m],
-                from_tiles(grads_ref.at[0, 0], m, n // 128, 2),
+                from_tiles(grads_ref.at[0], m, n // 128, 2),
                 preferred_element_type=F32,
             )
             wide = unturned(wide, m)
@@ -227,10 +230,16 @@
             to_row = pl.multiple_of((term * own + residue % own) * CH, CH)
             cols_ref[place, owner // 2, pl.ds(to_row, CH), :] = d_lane[r * CH : (r + 1) * CH]
 
-
-def lane_block(core, grads, rows, own):
-    _, steps, _, groups, depth, _ = grads.shape
+    @pl.when((term == 1) & (step == pl.num_programs(1) - 1))
+    def _():
+        mine_ref[:, : 2 * own * CH, :] = cols_ref[0]
+        theirs_ref[...] = cols_ref[1]
+
+
+def lane_block(core, grads, rows, own, height):
+    _, _, groups, depth, _ = grads.shape
     across = depth // (CH // GROUP)
+    steps = groups * GROUP // BLOCK
     owners = steps * BLOCK // own
     return pl.pallas_call(
         functools.partial(lane_kernel, across),
@@ -238,13 +247,22 @@
         in_specs=[
             pl.BlockSpec(memory_space=pltpu.SMEM),
             pl.BlockSpec(
-                (1, 1, GROUP, groups, depth, 128), lambda t, s: (t, s, 0, 0, 0, 0)
+                (1, GROUP, BLOCK // GROUP, depth, 128), lambda t, s: (t, 0, s, 0, 0)
             ),
-            pl.BlockSpec((1, CH * across, SEQS), lambda t, s: (t, 0, 0)),
-        ],
-        out_specs=pl.BlockSpec((2, owners // 2, 2 * own * CH, SEQS), lambda t, s: (0, 0, 0, 0)),
-        out_shape=jax.ShapeDtypeStruct((2, owners // 2, 2 * own * CH, SEQS), BF16),
-        scratch_shapes=[pltpu.VMEM((GROUP, SEQS, depth), BF16)],
+            pl.BlockSpec((1, CH * across, SEQS), lambda t, s: (1 - t, 0, 0)),
+        ],
+        out_specs=[
+            pl.BlockSpec((owners // 2, height, SEQS), lambda t, s: (0, 0, 0)),
+            pl.BlockSpec((owners // 2, 2 * own * CH, SEQS), lambda t, s: (0, 0, 0)),
+        ],
+        out_shape=[
+            jax.ShapeDtypeStruct((owners // 2, height, SEQS), BF16),
+            jax.ShapeDtypeStruct((owners // 2, 2 * own * CH, SEQS), BF16),
+        ],
+        scratch_shapes=[
+            pltpu.VMEM((2, owners // 2, 2 * own * CH, SEQS), BF16),
+            pltpu.VMEM((GROUP, SEQS, depth), BF16),
+        ],
         compiler_params=pltpu.CompilerParams(vmem_limit_bytes=40 * 1024 * 1024),
         cost_estimate=pl.CostEstimate(
             flops=4 * steps * BLOCK * across * CH * CH * SEQS,
@@ -256,42 +274,42 @@
 
 def pair_block(lanes, rows, weights, bias, upstream, row_peers):
     count, across, pairs = upstream.shape
-    steps = count // BLOCK
-    width = BLOCK * CH
+    width = count * CH
     depth = CH // GROUP * across
-    once = lambda t, s: (0, 0)
+    high = count // GROUP * across
     sent = 2 * CH * across // row_peers + CH * CH // row_peers + TILE
     return pl.pallas_call(
-        functools.partial(pair_kernel, steps, across),
-        grid=(2, steps),
+        functools.partial(pair_kernel, across),
+        grid=(2,),
         in_specs=[
-            pl.BlockSpec((1, width, SEQS), lambda t, s: (t, s, 0)),
-            pl.BlockSpec((1, CH * across, SEQS), lambda t, s: (t, 0, 0)),
-            pl.BlockSpec((1, CH * CH, pairs), lambda t, s: (t, 0, 0)),
-            pl.BlockSpec((1, pairs), once),
-            pl.BlockSpec((BLOCK, across, pairs), lambda t, s: (s, 0, 0)),
+            pl.BlockSpec((1, width, SEQS), lambda t: (t, 0, 0)),
+            pl.BlockSpec((1, CH * across, SEQS), lambda t: (1 - t, 0, 0)),
+            pl.BlockSpec((1, CH * CH, pairs), lambda t: (t, 0, 0)),
+            pl.BlockSpec((1, pairs), lambda t: (0, 0)),
+            pl.BlockSpec((count, across, pairs), lambda t: (0, 0, 0)),
         ],
         out_specs=[
-            pl.BlockSpec((BLOCK, across, pairs), lambda t, s: (t * s, 0, 0)),
-            pl.BlockSpec(
-                (1, 1, GROUP, width // 128, depth, 128), lambda t, s: (t, s, 0, 0, 0, 0)
-            ),
-            pl.BlockSpec((row_peers, sent, SEQS), lambda t, s: (0, 0, 0)),
+            pl.BlockSpec((count, across, pairs), lambda t: (0, 0, 0)),
+            pl.BlockSpec(memory_space=pl.ANY),
+            pl.BlockSpec((row_peers, sent, SEQS), lambda t: (0, 0, 0)),
         ],
         out_shape=[
             jax.ShapeDtypeStruct((count, across, pairs), BF16),
-            jax.ShapeDtypeStruct((2, steps, GROUP, width // 128, depth, 128), BF16),
+            jax.ShapeDtypeStruct((2, GROUP, width // 128, depth, 128), BF16),
             jax.ShapeDtypeStruct((row_peers, sent, SEQS), BF16),
         ],
         scratch_shapes=[
             pltpu.VMEM((count, across, pairs), F32),
             pltpu.VMEM((GROUP, width // 128, depth, 128), BF16),
-            pltpu.VMEM((GROUP, width // 128, depth, 128), BF16),
+            pltpu.VMEM((GROUP, CH // GROUP, high, 128), BF16),
+            pltpu.VMEM((GROUP, CH // GROUP, high, 128), BF16),
+            pltpu.VMEM((2, GROUP, width // 128, depth, 128), BF16),
             pltpu.VMEM((CH * across, SEQS), F32),
             pltpu.VMEM((GROUP, pairs, CH * CH), F32),
             pltpu.VMEM((CH * CH, pairs), F32),
             pltpu.VMEM((CH * across, SEQS), F32),
             pltpu.VMEM((8, pairs), F32),
+            pltpu.SemaphoreType.DMA((2, CH // GROUP)),
         ],
         compiler_params=pltpu.CompilerParams(vmem_limit_bytes=60 * 1024 * 1024),
         cost_estimate=pl.CostEstimate(
@@ -344,13 +362,11 @@
     half = everywhere(mine, "col", same_core)
     other = lax.ppermute(half, "col", other_core)
     rows = everywhere(part, "row")
-    second = lax.axis_index("col") % 2 == 1
-    lanes = jnp.stack(
-        [jnp.where(second, other, half), jnp.where(second, half, other)], axis=1
-    )
+    second = (lax.axis_index("col") & 1) == 1
+    lanes = jnp.stack([jnp.where(second, other, half), jnp.where(second, half, other)], axis=1)
     lanes = lanes.transpose(2, 0, 1, 3, 4).reshape(2, count * CH, SEQS)
     rows = rows.reshape(rows_n, 2, own, CH // GROUP, GROUP, SEQS)
-    rows = rows[:, ::-1].transpose(1, 4, 3, 0, 2, 5).reshape(2, CH * across, SEQS)
+    rows = rows.transpose(1, 4, 3, 0, 2, 5).reshape(2, CH * across, SEQS)
     weights = jnp.stack(
         [weight.reshape(CH, CH, pairs).transpose(1, 0, 2).reshape(CH * CH, pairs), weight]
     )
@@ -365,20 +381,22 @@
         )
 
     sent = exchange(to_rows, "row")
-    core = (lax.axis_index("col") % 2).astype(jnp.int32).reshape(1)
-    to_cols = lane_block(core, g_terms, rows, own)
-    other = lax.ppermute(to_cols[1], "col", other_core)
+    core = (lax.axis_index("col") & 1).astype(jnp.int32).reshape(1)
+    to_cols, theirs = lane_block(core, g_terms, rows, own, n_own + n_slice + TILE)
+    other = lax.ppermute(theirs, "col", other_core)
     summed = jnp.sum(sent.astype(F32), axis=0)
     part_grads = lax.ppermute(summed[:n_own].astype(BF16), both, to_owner)
     shared = with_bias(summed[n_own:])
     shared_other = lax.ppermute(shared, "col", other_core)
     shared = with_bias(shared.astype(F32) + shared_other.astype(F32))
-    to_cols = (to_cols[0].astype(F32) + other.astype(F32)).astype(BF16)
+    mine = (to_cols[:, :n_own].astype(F32) + other.astype(F32)).astype(BF16)
+    to_cols = lax.dynamic_update_slice(to_cols, mine, (0, 0, 0))
     shared = jnp.broadcast_to(shared[None], (cols_n // 2,) + shared.shape)
-    sent = exchange(jnp.concatenate([to_cols, shared], axis=1), "col", same_core)
+    to_cols = lax.dynamic_update_slice(to_cols, shared, (0, n_own, 0))
+    sent = exchange(to_cols, "col", same_core)
     summed = jnp.sum(sent.astype(F32), axis=0)
-    grad_weight = everywhere(summed[n_own : n_own + n_slice], "row")
-    grad_weight = grad_weight.reshape(CH * CH, pairs)
+    grad_weight = everywhere(summed[n_own : n_own + n_slice].astype(BF16), "row")
+    grad_weight = grad_weight.astype(F32).reshape(CH * CH, pairs)
     grad_bias = one_part(summed[n_own + n_slice :]).reshape(pairs)
     grads = summed[:n_own] + part_grads.astype(F32)
     grads = grads.reshape(2, own, CH, SEQS).transpose(0, 1, 3, 2).reshape(2, own, SEQS * CH)

time: 161 us -> 151 us (0.938)
  the two profiles are of different devices: /device:TPU:33 before, /device:TPU:0 now
where the time goes in v4:
time: 151 us; the launch traced here: 150 us
  waiting for transfers between devices  56.9 us (38%)
  Pallas kernels  47.2 us (31%)
  starting transfers between devices  27.9 us (18%)
  local copies, waits for them, and re-layouts  11.8 us (8%)
  other arithmetic  5.4 us (4%)
    all_to_all x5, waiting for transfers between devices, exchange(): lax.all_to_all(x, axis, split_axis=0, concat_axis=0, axis_index_groups=gr...  56.8 us
    pallas_call x1, Pallas kernels, pair_block(): pl.pallas_call(functools.partial(pair_kernel, across), grid=(2,), in_spec...  36.4 us
    all_to_all x5, starting transfers between devices, exchange(): lax.all_to_all(x, axis, split_axis=0, concat_axis=0, axis_index_groups=gr...  26.4 us
    pallas_call x1, Pallas kernels, lane_block(): pl.pallas_call(functools.partial(lane_kernel, across), grid=(2, steps), i...  10.8 us
  transfers between devices with their start and end apart: 10, of which 5 were waited for; matrix products, arithmetic and copies ran while one was open for 7% of the time, Pallas kernels for 7%

profile of v4, /device:TPU:0, one launch (start us, length us, event | category | flops | bytes accessed | tf_op | source)
XLA Modules:
  0.0 150.0 jit_solution(7196618256574459595)
XLA Ops:
  0.6 1.0 reshape.108
  1.6 0.1 copy.33
  1.8 1.0 reshape.109
  2.8 0.1 copy.34
  2.9 1.0 broadcast_in_dim.11
  4.0 5.9 %all-to-all-start = ((bf16[8,2,192,128]{3,2,1,0:T(8,128)(2,1)}), bf16[8,2,192,128]{3,2,1,0:T(8,128)(2,1)S(1)}, u32[]{:S(2)}, u32[]{:S(2)}) async-start(bf16[8,2,192,128]{3,2,1,0:T(8,128)(2,1)} %broadcast_in_dim.11), calls=%async_computation | async-start | bytes 1572864 | tf_op jit(solution)/shard_map/all_to_all | solution.py:324
  9.9 0.0 copy-start.1
  9.9 0.8 collective-permute-start.1
  10.8 12.1 %all-to-all-done = bf16[8,2,192,128]{3,2,1,0:T(8,128)(2,1)S(1)} async-done(((bf16[8,2,192,128]{3,2,1,0:T(8,128)(2,1)}), bf16[8,2,192,128]{3,2,1,0:T(8,128)(2,1)S(1)}, u32[]{:S(2)}, u32[]{:S(2)}) %all-to-all-start) | async-done | bytes 786464 | tf_op jit(solution)/shard_map/all_to_all | solution.py:324
  22.8 0.0 collective-permute-start
  22.8 0.0 collective-permute-done.1
  22.8 1.0 broadcast_in_dim.12
  23.9 8.4 %all-to-all-start.1 = ((bf16[8,2,192,128]{3,2,1,0:T(8,128)(2,1)}), bf16[8,2,192,128]{3,2,1,0:T(8,128)(2,1)S(1)}, u32[]{:S(2)}, u32[]{:S(2)}) async-start(bf16[8,2,192,128]{3,2,1,0:T(8,128)(2,1)} %broadcast_in_dim.12), calls=%async_computation.1 | async-start | bytes 1572864 | tf_op jit(solution)/shard_map/all_to_all | solution.py:324
  32.2 0.0 copy-done.1
  32.2 0.1 copy.40
  32.3 0.8 pad_maximum_fusion.weight_ref
  33.2 14.1 %all-to-all-done.1 = bf16[8,2,192,128]{3,2,1,0:T(8,128)(2,1)S(1)} async-done(((bf16[8,2,192,128]{3,2,1,0:T(8,128)(2,1)}), bf16[8,2,192,128]{3,2,1,0:T(8,128)(2,1)S(1)}, u32[]{:S(2)}, u32[]{:S(2)}) %all-to-all-start.1) | async-done | bytes 786464 | tf_op jit(solution)/shard_map/all_to_all | solution.py:324
  47.3 0.5 copy.38
  47.8 0.8 copy.39
  48.6 1.0 copy.41.row_ref
  49.7 0.0 collective-permute-done
  49.7 0.1 select_bitcast_fusion.1
  49.8 0.1 maximum_bitcast_fusion
  49.9 1.3 copy.35
  51.2 36.4 %shard_map.92 = (bf16[96,48,128]{2,1,0:T(8,128)(2,1)}, bf16[2,4,24,384,128]{4,3,2,1,0:T(8,128)(2,1)}, bf16[8,528,128]{2,1,0:T(8,128)(2,1)}) custom-call(bf16[2,3072,128]{2,1,0:T(8,128)(2,1)} %bitcast.52, bf16[2,1536,128]{2,1,0:T(8,128)(2,1)} %copy.41.row_ref, bf16[2,1024,128]{2,1,0:T(8,128)(2,1)} %pad_maximum_fusion.weight_ref, f32[1,128]{1,0:T(1,128)} %bitcast.63, ...), custom_call_target="tpu_custom_call" | custom-call | flops 12079595520 | bytes 33554432 | tf_op jit(solution)/shard_map/pallas_call | solution.py:281
  87.6 0.0 copy-start
  87.6 3.7 %all-to-all-start.2 = ((bf16[8,528,128]{2,1,0:T(8,128)(2,1)}), bf16[8,528,128]{2,1,0:T(8,128)(2,1)S(1)}, u32[]{:S(2)}, u32[]{:S(2)}) async-start(bf16[8,528,128]{2,1,0:T(8,128)(2,1)} %get-tuple-element.14), calls=%async_computation.2 | async-start | bytes 2162688 | tf_op jit(solution)/shard_map/all_to_all | solution.py:324
  91.4 0.1 pad.7.clone
  91.4 0.0 copy-done
  91.4 10.8 %shard_map.93 = (bf16[8,528,128]{2,1,0:T(8,128)(2,1)}, bf16[8,384,128]{2,1,0:T(8,128)(2,1)S(1)}) custom-call(s32[1]{0:T(128)} %bitcast.19.core_ref, bf16[2,4,24,384,128]{4,3,2,1,0:T(8,128)(2,1)} %get-tuple-element.11.grads_ref, bf16[2,1536,128]{2,1,0:T(8,128)(2,1)S(1)} %copy-done), custom_call_target="tpu_custom_call" | custom-call | flops 2415919104 | bytes 25165824 | tf_op jit(solution)/shard_map/pallas_call | solution.py:244
  102.2 0.0 collective-permute-start.2
  102.2 6.8 %all-to-all-done.2 = bf16[8,528,128]{2,1,0:T(8,128)(2,1)S(1)} async-done(((bf16[8,528,128]{2,1,0:T(8,128)(2,1)}), bf16[8,528,128]{2,1,0:T(8,128)(2,1)S(1)}, u32[]{:S(2)}, u32[]{:S(2)}) %all-to-all-start.2) | async-done | bytes 1081376 | tf_op jit(solution)/shard_map/all_to_all | solution.py:324
  109.0 0.1 convert_reduce_fusion.1
  109.2 0.1 maximum_maximum_fusion
  109.3 0.1 collective-permute-start.3
  109.4 0.0 collective-permute-done.2
  109.4 2.3 %fusion = bf16[8,528,128]{2,1,0:T(8,128)(2,1)} fusion(bf16[8,528,128]{2,1,0:T(8,128)(2,1)} %get-tuple-element.12, bf16[8,384,128]{2,1,0:T(8,128)(2,1)S(1)} %collective-permute-done.2), kind=kLoop, calls=%fused_computation.4 | loop fusion | flops 1572864 | bytes 2359296 | tf_op jit(solution)/shard_map/dynamic_update_slice | solution.py:393
  111.7 0.0 collective-permute-done.3
  111.7 0.1 convert_add_fusion
  111.8 0.1 maximum_maximum_fusion.1
  111.9 0.8 broadcast_dynamic-update-slice_fusion
  112.7 3.6 %all-to-all-start.3 = ((bf16[8,528,128]{2,1,0:T(8,128)(2,1)}), bf16[8,528,128]{2,1,0:T(8,128)(2,1)S(1)}, u32[]{:S(2)}, u32[]{:S(2)}) async-start(bf16[8,528,128]{2,1,0:T(8,128)(2,1)} %broadcast_dynamic-update-slice_fusion), calls=%async_computation.3 | async-start | bytes 2162688 | tf_op jit(solution)/shard_map/all_to_all | solution.py:324
  116.3 0.7 collective-permute-start.4
  116.9 17.8 %all-to-all-done.3 = bf16[8,528,128]{2,1,0:T(8,128)(2,1)S(1)} async-done(((bf16[8,528,128]{2,1,0:T(8,128)(2,1)}), bf16[8,528,128]{2,1,0:T(8,128)(2,1)S(1)}, u32[]{:S(2)}, u32[]{:S(2)}) %all-to-all-start.3) | async-done | bytes 1081376 | tf_op jit(solution)/shard_map/all_to_all | solution.py:324
  134.7 0.1 convert_reduce_fusion
  134.9 0.7 broadcast_in_dim.14
  135.6 4.8 %all-to-all-start.4 = ((bf16[8,128,128]{2,1,0:T(8,128)(2,1)}), bf16[8,128,128]{2,1,0:T(8,128)(2,1)S(1)}, u32[]{:S(2)}, u32[]{:S(2)}) async-start(bf16[8,128,128]{2,1,0:T(8,128)(2,1)} %broadcast_in_dim.14), calls=%async_computation.4 | async-start | bytes 524288 | tf_op jit(solution)/shard_map/all_to_all | solution.py:324
  140.4 0.0 collective-permute-done.4
  140.5 0.2 copy.43
  140.6 0.9 squeeze.6
  141.5 0.2 copy.44
  141.7 0.9 squeeze.7
  142.5 0.5 slice_reduce_fusion
  143.1 6.1 %all-to-all-done.4 = bf16[8,128,128]{2,1,0:T(8,128)(2,1)S(1)} async-done(((bf16[8,128,128]{2,1,0:T(8,128)(2,1)}), bf16[8,128,128]{2,1,0:T(8,128)(2,1)S(1)}, u32[]{:S(2)}, u32[]{:S(2)}) %all-to-all-start.4) | async-done | bytes 262176 | tf_op jit(solution)/shard_map/all_to_all | solution.py:324
  149.2 0.8 bitcast_convert_fusion
  (16 shorter events, 0.2 us)
Async XLA Ops:
  4.0 18.8 %all-to-all-start = ((bf16[8,2,192,128]{3,2,1,0:T(8,128)(2,1)}), bf16[8,2,192,128]{3,2,1,0:T(8,128)(2,1)S(1)}, u32[]{:S(2)}, u32[]{:S(2)}) async-start(bf16[8,2,192,128]{3,2,1,0:T(8,128)(2,1)} %broadcast_in_dim.11), calls=%async_computation | async-start | bytes 1572864 | tf_op jit(solution)/shard_map/all_to_all | solution.py:324
  9.9 22.3 %copy-start.1 = (bf16[1024,128]{1,0:T(8,128)(2,1)S(1)}, bf16[1024,128]{1,0:T(8,128)(2,1)}, u32[]{:S(2)}) copy-start(bf16[1024,128]{1,0:T(8,128)(2,1)} %param.7) | copy-start | bytes 786436
  9.9 12.9 %collective-permute-start.1 = (bf16[2,192,128]{2,1,0:T(8,128)(2,1)S(1)}, bf16[2,192,128]{2,1,0:T(8,128)(2,1)S(1)}, u32[]{:S(2)}, u32[]{:S(2)}) collective-permute-start(bf16[2,192,128]{2,1,0:T(8,128)(2,1)S(1)} %pad_maximum_fusion.1), channel_id=1, source_target_pairs={{0,0},{1,16},{2,32},{3,48},{4,64},{5,80},{6,96},{7,112},{8,1},{9,1... | collective-permute-start | bytes 294920 | tf_op jit(solution)/shard_map/ppermute | solution.py:361
  22.8 26.9 %collective-permute-start = (bf16[8,2,192,128]{3,2,1,0:T(8,128)(2,1)S(1)}, bf16[8,2,192,128]{3,2,1,0:T(8,128)(2,1)S(1)}, u32[]{:S(2)}, u32[]{:S(2)}) collective-permute-start(bf16[8,2,192,128]{3,2,1,0:T(8,128)(2,1)S(1)} %all-to-all-done), channel_id=1, source_target_pairs={{0,1},{1,0},{2,3},{3,2},{4,5},{5,4},{6,7},{7,6},{8,9},{9,8},{10,11... | collective-permute-start | bytes 2359304 | tf_op jit(solution)/shard_map/ppermute | solution.py:363
  23.9 23.4 %all-to-all-start.1 = ((bf16[8,2,192,128]{3,2,1,0:T(8,128)(2,1)}), bf16[8,2,192,128]{3,2,1,0:T(8,128)(2,1)S(1)}, u32[]{:S(2)}, u32[]{:S(2)}) async-start(bf16[8,2,192,128]{3,2,1,0:T(8,128)(2,1)} %broadcast_in_dim.12), calls=%async_computation.1 | async-start | bytes 1572864 | tf_op jit(solution)/shard_map/all_to_all | solution.py:324
  87.6 3.8 %copy-start = (bf16[2,1536,128]{2,1,0:T(8,128)(2,1)S(1)}, bf16[2,1536,128]{2,1,0:T(8,128)(2,1)}, u32[]{:S(2)}) copy-start(bf16[2,1536,128]{2,1,0:T(8,128)(2,1)} %copy.41.row_ref) | copy-start | bytes 2359300
  87.6 21.4 %all-to-all-start.2 = ((bf16[8,528,128]{2,1,0:T(8,128)(2,1)}), bf16[8,528,128]{2,1,0:T(8,128)(2,1)S(1)}, u32[]{:S(2)}, u32[]{:S(2)}) async-start(bf16[8,528,128]{2,1,0:T(8,128)(2,1)} %get-tuple-element.14), calls=%async_computation.2 | async-start | bytes 2162688 | tf_op jit(solution)/shard_map/all_to_all | solution.py:324
  102.2 7.2 %collective-permute-start.2 = (bf16[8,384,128]{2,1,0:T(8,128)(2,1)S(1)}, bf16[8,384,128]{2,1,0:T(8,128)(2,1)S(1)}, u32[]{:S(2)}, u32[]{:S(2)}) collective-permute-start(bf16[8,384,128]{2,1,0:T(8,128)(2,1)S(1)} %get-tuple-element.13), channel_id=1, source_target_pairs={{0,1},{1,0},{2,3},{3,2},{4,5},{5,4},{6,7},{7,6},{8,9},{9,8},{10,11... | collective-permute-start | bytes 2359304 | tf_op jit(solution)/shard_map/ppermute | solution.py:386
  109.3 2.4 %collective-permute-start.3 = (bf16[144,128]{1,0:T(8,128)(2,1)S(1)}, bf16[144,128]{1,0:T(8,128)(2,1)S(1)}, u32[]{:S(2)}, u32[]{:S(2)}) collective-permute-start(bf16[144,128]{1,0:T(8,128)(2,1)S(1)} %maximum_maximum_fusion), channel_id=1, source_target_pairs={{0,1},{1,0},{2,3},{3,2},{4,5},{5,4},{6,7},{7,6},{8,9},{9,8},{10,11... | collective-permute-start | bytes 110600 | tf_op jit(solution)/shard_map/ppermute | solution.py:390
  112.7 22.0 %all-to-all-start.3 = ((bf16[8,528,128]{2,1,0:T(8,128)(2,1)}), bf16[8,528,128]{2,1,0:T(8,128)(2,1)S(1)}, u32[]{:S(2)}, u32[]{:S(2)}) async-start(bf16[8,528,128]{2,1,0:T(8,128)(2,1)} %broadcast_dynamic-update-slice_fusion), calls=%async_computation.3 | async-start | bytes 2162688 | tf_op jit(solution)/shard_map/all_to_all | solution.py:324
  116.3 24.1 %collective-permute-start.4 = (bf16[384,128]{1,0:T(8,128)(2,1)S(1)}, bf16[384,128]{1,0:T(8,128)(2,1)S(1)}, u32[]{:S(2)}, u32[]{:S(2)}) collective-permute-start(bf16[384,128]{1,0:T(8,128)(2,1)S(1)} %slice.64), channel_id=1, source_target_pairs={{0,0},{16,1},{32,2},{48,3},{64,4},{80,5},{96,6},{112,7},{1,8},{17,... | collective-permute-start | bytes 294920 | tf_op jit(solution)/shard_map/ppermute | solution.py:388
  135.6 13.6 %all-to-all-start.4 = ((bf16[8,128,128]{2,1,0:T(8,128)(2,1)}), bf16[8,128,128]{2,1,0:T(8,128)(2,1)S(1)}, u32[]{:S(2)}, u32[]{:S(2)}) async-start(bf16[8,128,128]{2,1,0:T(8,128)(2,1)} %broadcast_in_dim.14), calls=%async_computation.4 | async-start | bytes 524288 | tf_op jit(solution)/shard_map/all_to_all | solution.py:324

commit v5 on v4

--- a/solution.py
+++ b/solution.py
@@ -353,11 +353,10 @@
     other_core = [(k, k ^ 1) for k in range(cols_n)]
     n_own = 2 * own * CH
 
-    def channels_first(x):
-        return x.reshape(own, SEQS, CH).transpose(0, 2, 1)
-
-    mine = jnp.stack([channels_first(left_features), channels_first(right_features)])
-    mine = mine.reshape(2, own * CH, SEQS)
+    mine = jnp.concatenate([left_features, right_features], axis=0)
+    mine = mine.reshape(2 * own, SEQS, CH).transpose(0, 2, 1).reshape(2, own * CH, SEQS)
+    turned = weight.reshape(CH, CH, pairs).transpose(1, 0, 2).reshape(CH * CH, pairs)
+    weights = jnp.stack([turned, weight])
     part = lax.ppermute(mine, both, to_part)
     half = everywhere(mine, "col", same_core)
     other = lax.ppermute(half, "col", other_core)
@@ -367,9 +366,6 @@
     lanes = lanes.transpose(2, 0, 1, 3, 4).reshape(2, count * CH, SEQS)
     rows = rows.reshape(rows_n, 2, own, CH // GROUP, GROUP, SEQS)
     rows = rows.transpose(1, 4, 3, 0, 2, 5).reshape(2, CH * across, SEQS)
-    weights = jnp.stack(
-        [weight.reshape(CH, CH, pairs).transpose(1, 0, 2).reshape(CH * CH, pairs), weight]
-    )
     pair_out, g_terms, to_rows = pair_block(
         lanes, rows, weights, bias.reshape(1, pairs), upstream, rows_n
     )
@@ -382,7 +378,7 @@
 
     sent = exchange(to_rows, "row")
     core = (lax.axis_index("col") & 1).astype(jnp.int32).reshape(1)
-    to_cols, theirs = lane_block(core, g_terms, rows, own, n_own + n_slice + TILE)
+    to_cols, theirs = lane_block(core, g_terms, rows, own, n_own)
     other = lax.ppermute(theirs, "col", other_core)
     summed = jnp.sum(sent.astype(F32), axis=0)
     part_grads = lax.ppermute(summed[:n_own].astype(BF16), both, to_owner)
@@ -390,10 +386,8 @@
     shared_other = lax.ppermute(shared, "col", other_core)
     shared = with_bias(shared.astype(F32) + shared_other.astype(F32))
     mine = (to_cols[:, :n_own].astype(F32) + other.astype(F32)).astype(BF16)
-    to_cols = lax.dynamic_update_slice(to_cols, mine, (0, 0, 0))
     shared = jnp.broadcast_to(shared[None], (cols_n // 2,) + shared.shape)
-    to_cols = lax.dynamic_update_slice(to_cols, shared, (0, n_own, 0))
-    sent = exchange(to_cols, "col", same_core)
+    sent = exchange(jnp.concatenate([mine, shared], axis=1), "col", same_core)
     summed = jnp.sum(sent.astype(F32), axis=0)
     grad_weight = everywhere(summed[n_own : n_own + n_slice].astype(BF16), "row")
     grad_weight = grad_weight.astype(F32).reshape(CH * CH, pairs)

time: 151 us -> 149 us (0.987)
  local copies, waits for them, and re-layouts: 11.8 us -> 9.22 us
    dynamic_update_slice x1 -> x0, other arithmetic: 2.26 us -> none  [local(): to_cols = lax.dynamic_update_slice(to_cols, mine, (0, 0, 0))]
    concatenate x0 -> x2, other arithmetic: none -> 1.97 us  [the longest x1 1.06 us: local(): sent = exchange(jnp.concatenate([mine, shared], axis=1), 'col', same_core)]
    reshape x2 -> x1, local copies, waits for them, and re-layouts: 2.03 us -> 0.26 us  [local(): mine.reshape(2 * own, SEQS, CH).transpose(0, 2, 1)]
  transfers between devices with their start and end apart: 10 -> 10, of which waited for: 5 -> 6; matrix products, arithmetic and copies ran while one was open for 7% -> 6% of each run, Pallas kernels for 7% -> 7%
where the time goes in v5:
time: 149 us; the launch traced here: 148 us
  waiting for transfers between devices  57.9 us (39%)
  Pallas kernels  46.2 us (31%)
  starting transfers between devices  28.5 us (19%)
  local copies, waits for them, and re-layouts  9.22 us (6%)
  other arithmetic  5.3 us (4%)
    all_to_all x5, waiting for transfers between devices, exchange(): lax.all_to_all(x, axis, split_axis=0, concat_axis=0, axis_index_groups=gr...  56.9 us
    pallas_call x1, Pallas kernels, pair_block(): pl.pallas_call(functools.partial(pair_kernel, across), grid=(2,), in_spec...  36.4 us
    all_to_all x5, starting transfers between devices, exchange(): lax.all_to_all(x, axis, split_axis=0, concat_axis=0, axis_index_groups=gr...  26.9 us
    pallas_call x1, Pallas kernels, lane_block(): pl.pallas_call(functools.partial(lane_kernel, across), grid=(2, steps), i...  9.79 us
  transfers between devices with their start and end apart: 10, of which 6 were waited for; matrix products, arithmetic and copies ran while one was open for 6% of the time, Pallas kernels for 7%

profile of v5, /device:TPU:0, one launch (start us, length us, event | category | flops | bytes accessed | tf_op | source)
XLA Modules:
  0.0 148.0 jit_solution(6843793090399733254)
XLA Ops:
  0.6 0.9 pad_maximum_fusion.2
  1.6 0.3 reshape.98
  1.8 0.2 copy.27
  2.0 1.0 broadcast_in_dim.11
  3.0 5.9 %all-to-all-start = ((bf16[8,2,192,128]{3,2,1,0:T(8,128)(2,1)}), bf16[8,2,192,128]{3,2,1,0:T(8,128)(2,1)S(1)}, u32[]{:S(2)}, u32[]{:S(2)}) async-start(bf16[8,2,192,128]{3,2,1,0:T(8,128)(2,1)} %broadcast_in_dim.11), calls=%async_computation | async-start | bytes 1572864 | tf_op jit(solution)/shard_map/all_to_all | solution.py:324
  9.0 0.0 copy-start.1
  9.0 0.8 collective-permute-start.1
  9.8 12.1 %all-to-all-done = bf16[8,2,192,128]{3,2,1,0:T(8,128)(2,1)S(1)} async-done(((bf16[8,2,192,128]{3,2,1,0:T(8,128)(2,1)}), bf16[8,2,192,128]{3,2,1,0:T(8,128)(2,1)S(1)}, u32[]{:S(2)}, u32[]{:S(2)}) %all-to-all-start) | async-done | bytes 786464 | tf_op jit(solution)/shard_map/all_to_all | solution.py:324
  21.8 0.0 collective-permute-start
  21.8 0.0 collective-permute-done.1
  21.9 1.0 broadcast_in_dim.12
  22.9 8.4 %all-to-all-start.1 = ((bf16[8,2,192,128]{3,2,1,0:T(8,128)(2,1)}), bf16[8,2,192,128]{3,2,1,0:T(8,128)(2,1)S(1)}, u32[]{:S(2)}, u32[]{:S(2)}) async-start(bf16[8,2,192,128]{3,2,1,0:T(8,128)(2,1)} %broadcast_in_dim.12), calls=%async_computation.1 | async-start | bytes 1572864 | tf_op jit(solution)/shard_map/all_to_all | solution.py:324
  31.3 0.0 copy-done.1
  31.3 0.1 copy.31
  31.4 0.8 pad_maximum_fusion.1.weight_ref
  32.2 14.1 %all-to-all-done.1 = bf16[8,2,192,128]{3,2,1,0:T(8,128)(2,1)S(1)} async-done(((bf16[8,2,192,128]{3,2,1,0:T(8,128)(2,1)}), bf16[8,2,192,128]{3,2,1,0:T(8,128)(2,1)S(1)}, u32[]{:S(2)}, u32[]{:S(2)}) %all-to-all-start.1) | async-done | bytes 786464 | tf_op jit(solution)/shard_map/all_to_all | solution.py:324
  46.3 0.5 copy.29
  46.8 0.8 copy.30
  47.7 1.0 copy.32.row_ref
  48.7 0.0 collective-permute-done
  48.7 0.1 select_bitcast_fusion.1
  48.8 0.1 maximum_bitcast_fusion
  49.0 1.3 copy.28
  50.3 36.4 %shard_map.92 = (bf16[96,48,128]{2,1,0:T(8,128)(2,1)}, bf16[2,4,24,384,128]{4,3,2,1,0:T(8,128)(2,1)}, bf16[8,528,128]{2,1,0:T(8,128)(2,1)}) custom-call(bf16[2,3072,128]{2,1,0:T(8,128)(2,1)} %bitcast.46, bf16[2,1536,128]{2,1,0:T(8,128)(2,1)} %copy.32.row_ref, bf16[2,1024,128]{2,1,0:T(8,128)(2,1)} %pad_maximum_fusion.1.weight_ref, f32[1,128]{1,0:T(1,128)} %bitcast.54, ...), custom_call_target="tpu_custom_call" | custom-call | flops 12079595520 | bytes 33554432 | tf_op jit(solution)/shard_map/pallas_call | solution.py:281
  86.7 0.0 copy-start
  86.7 3.7 %all-to-all-start.2 = ((bf16[8,528,128]{2,1,0:T(8,128)(2,1)}), bf16[8,528,128]{2,1,0:T(8,128)(2,1)S(1)}, u32[]{:S(2)}, u32[]{:S(2)}) async-start(bf16[8,528,128]{2,1,0:T(8,128)(2,1)} %get-tuple-element.14), calls=%async_computation.2 | async-start | bytes 2162688 | tf_op jit(solution)/shard_map/all_to_all | solution.py:324
  90.4 0.1 pad.9.clone
  90.5 0.0 copy-done
  90.5 9.8 %shard_map.93 = (bf16[8,384,128]{2,1,0:T(8,128)(2,1)S(1)}, bf16[8,384,128]{2,1,0:T(8,128)(2,1)S(1)}) custom-call(s32[1]{0:T(128)} %bitcast.14.core_ref, bf16[2,4,24,384,128]{4,3,2,1,0:T(8,128)(2,1)} %get-tuple-element.11.grads_ref, bf16[2,1536,128]{2,1,0:T(8,128)(2,1)S(1)} %copy-done), custom_call_target="tpu_custom_call" | custom-call | flops 2415919104 | bytes 25165824 | tf_op jit(solution)/shard_map/pallas_call | solution.py:244
  100.3 0.1 collective-permute-start.2
  100.4 7.7 %all-to-all-done.2 = bf16[8,528,128]{2,1,0:T(8,128)(2,1)S(1)} async-done(((bf16[8,528,128]{2,1,0:T(8,128)(2,1)}), bf16[8,528,128]{2,1,0:T(8,128)(2,1)S(1)}, u32[]{:S(2)}, u32[]{:S(2)}) %all-to-all-start.2) | async-done | bytes 1081376 | tf_op jit(solution)/shard_map/all_to_all | solution.py:324
  108.1 0.1 convert_reduce_fusion.1
  108.3 0.1 maximum_maximum_fusion
  108.4 0.1 collective-permute-start.3
  108.5 0.0 collective-permute-done.2
  108.5 0.2 add_convert_fusion
  108.7 1.0 collective-permute-done.3
  109.7 0.1 convert_add_fusion
  109.8 0.1 maximum_maximum_fusion.1
  109.9 1.1 pad_maximum_fusion
  111.0 3.6 %all-to-all-start.3 = ((bf16[8,528,128]{2,1,0:T(8,128)(2,1)}), bf16[8,528,128]{2,1,0:T(8,128)(2,1)S(1)}, u32[]{:S(2)}, u32[]{:S(2)}) async-start(bf16[8,528,128]{2,1,0:T(8,128)(2,1)} %pad_maximum_fusion), calls=%async_computation.3 | async-start | bytes 2162688 | tf_op jit(solution)/shard_map/all_to_all | solution.py:324
  114.6 0.7 collective-permute-start.4
  115.3 16.9 %all-to-all-done.3 = bf16[8,528,128]{2,1,0:T(8,128)(2,1)S(1)} async-done(((bf16[8,528,128]{2,1,0:T(8,128)(2,1)}), bf16[8,528,128]{2,1,0:T(8,128)(2,1)S(1)}, u32[]{:S(2)}, u32[]{:S(2)}) %all-to-all-start.3) | async-done | bytes 1081376 | tf_op jit(solution)/shard_map/all_to_all | solution.py:324
  132.2 0.1 convert_reduce_fusion
  132.4 0.7 broadcast_in_dim.14
  133.1 5.3 %all-to-all-start.4 = ((bf16[8,128,128]{2,1,0:T(8,128)(2,1)}), bf16[8,128,128]{2,1,0:T(8,128)(2,1)S(1)}, u32[]{:S(2)}, u32[]{:S(2)}) async-start(bf16[8,128,128]{2,1,0:T(8,128)(2,1)} %broadcast_in_dim.14), calls=%async_computation.4 | async-start | bytes 524288 | tf_op jit(solution)/shard_map/all_to_all | solution.py:324
  138.4 0.0 collective-permute-done.4
  138.4 0.2 copy.34
  138.6 0.9 squeeze.6
  139.5 0.2 copy.35
  139.7 0.9 squeeze.7
  140.5 0.5 slice_reduce_fusion
  141.1 6.1 %all-to-all-done.4 = bf16[8,128,128]{2,1,0:T(8,128)(2,1)S(1)} async-done(((bf16[8,128,128]{2,1,0:T(8,128)(2,1)}), bf16[8,128,128]{2,1,0:T(8,128)(2,1)S(1)}, u32[]{:S(2)}, u32[]{:S(2)}) %all-to-all-start.4) | async-done | bytes 262176 | tf_op jit(solution)/shard_map/all_to_all | solution.py:324
  147.2 0.8 bitcast_convert_fusion
  (15 shorter events, 0.2 us)
Async XLA Ops:
  3.0 18.8 %all-to-all-start = ((bf16[8,2,192,128]{3,2,1,0:T(8,128)(2,1)}), bf16[8,2,192,128]{3,2,1,0:T(8,128)(2,1)S(1)}, u32[]{:S(2)}, u32[]{:S(2)}) async-start(bf16[8,2,192,128]{3,2,1,0:T(8,128)(2,1)} %broadcast_in_dim.11), calls=%async_computation | async-start | bytes 1572864 | tf_op jit(solution)/shard_map/all_to_all | solution.py:324
  9.0 22.3 %copy-start.1 = (bf16[1024,128]{1,0:T(8,128)(2,1)S(1)}, bf16[1024,128]{1,0:T(8,128)(2,1)}, u32[]{:S(2)}) copy-start(bf16[1024,128]{1,0:T(8,128)(2,1)} %param.7) | copy-start | bytes 786436
  9.0 12.9 %collective-permute-start.1 = (bf16[2,192,128]{2,1,0:T(8,128)(2,1)S(1)}, bf16[2,192,128]{2,1,0:T(8,128)(2,1)S(1)}, u32[]{:S(2)}, u32[]{:S(2)}) collective-permute-start(bf16[2,192,128]{2,1,0:T(8,128)(2,1)S(1)} %bitcast.53), channel_id=1, source_target_pairs={{0,0},{1,16},{2,32},{3,48},{4,64},{5,80},{6,96},{7,112},{8,1},{9,1... | collective-permute-start | bytes 294920 | tf_op jit(solution)/shard_map/ppermute | solution.py:360
  21.8 26.9 %collective-permute-start = (bf16[8,2,192,128]{3,2,1,0:T(8,128)(2,1)S(1)}, bf16[8,2,192,128]{3,2,1,0:T(8,128)(2,1)S(1)}, u32[]{:S(2)}, u32[]{:S(2)}) collective-permute-start(bf16[8,2,192,128]{3,2,1,0:T(8,128)(2,1)S(1)} %all-to-all-done), channel_id=1, source_target_pairs={{0,1},{1,0},{2,3},{3,2},{4,5},{5,4},{6,7},{7,6},{8,9},{9,8},{10,11... | collective-permute-start | bytes 2359304 | tf_op jit(solution)/shard_map/ppermute | solution.py:362
  22.9 23.4 %all-to-all-start.1 = ((bf16[8,2,192,128]{3,2,1,0:T(8,128)(2,1)}), bf16[8,2,192,128]{3,2,1,0:T(8,128)(2,1)S(1)}, u32[]{:S(2)}, u32[]{:S(2)}) async-start(bf16[8,2,192,128]{3,2,1,0:T(8,128)(2,1)} %broadcast_in_dim.12), calls=%async_computation.1 | async-start | bytes 1572864 | tf_op jit(solution)/shard_map/all_to_all | solution.py:324
  86.7 3.8 %copy-start = (bf16[2,1536,128]{2,1,0:T(8,128)(2,1)S(1)}, bf16[2,1536,128]{2,1,0:T(8,128)(2,1)}, u32[]{:S(2)}) copy-start(bf16[2,1536,128]{2,1,0:T(8,128)(2,1)} %copy.32.row_ref) | copy-start | bytes 2359300
  86.7 21.4 %all-to-all-start.2 = ((bf16[8,528,128]{2,1,0:T(8,128)(2,1)}), bf16[8,528,128]{2,1,0:T(8,128)(2,1)S(1)}, u32[]{:S(2)}, u32[]{:S(2)}) async-start(bf16[8,528,128]{2,1,0:T(8,128)(2,1)} %get-tuple-element.14), calls=%async_computation.2 | async-start | bytes 2162688 | tf_op jit(solution)/shard_map/all_to_all | solution.py:324
  100.3 8.2 %collective-permute-start.2 = (bf16[8,384,128]{2,1,0:T(8,128)(2,1)S(1)}, bf16[8,384,128]{2,1,0:T(8,128)(2,1)S(1)}, u32[]{:S(2)}, u32[]{:S(2)}) collective-permute-start(bf16[8,384,128]{2,1,0:T(8,128)(2,1)S(1)} %get-tuple-element.13), channel_id=1, source_target_pairs={{0,1},{1,0},{2,3},{3,2},{4,5},{5,4},{6,7},{7,6},{8,9},{9,8},{10,11... | collective-permute-start | bytes 2359304 | tf_op jit(solution)/shard_map/ppermute | solution.py:382
  108.4 1.3 collective-permute-start.3
  111.0 21.2 %all-to-all-start.3 = ((bf16[8,528,128]{2,1,0:T(8,128)(2,1)}), bf16[8,528,128]{2,1,0:T(8,128)(2,1)S(1)}, u32[]{:S(2)}, u32[]{:S(2)}) async-start(bf16[8,528,128]{2,1,0:T(8,128)(2,1)} %pad_maximum_fusion), calls=%async_computation.3 | async-start | bytes 2162688 | tf_op jit(solution)/shard_map/all_to_all | solution.py:324
  114.6 23.8 %collective-permute-start.4 = (bf16[384,128]{1,0:T(8,128)(2,1)S(1)}, bf16[384,128]{1,0:T(8,128)(2,1)S(1)}, u32[]{:S(2)}, u32[]{:S(2)}) collective-permute-start(bf16[384,128]{1,0:T(8,128)(2,1)S(1)} %slice.60), channel_id=1, source_target_pairs={{0,0},{16,1},{32,2},{48,3},{64,4},{80,5},{96,6},{112,7},{1,8},{17,... | collective-permute-start | bytes 294920 | tf_op jit(solution)/shard_map/ppermute | solution.py:384
  133.1 14.1 %all-to-all-start.4 = ((bf16[8,128,128]{2,1,0:T(8,128)(2,1)}), bf16[8,128,128]{2,1,0:T(8,128)(2,1)S(1)}, u32[]{:S(2)}, u32[]{:S(2)}) async-start(bf16[8,128,128]{2,1,0:T(8,128)(2,1)} %broadcast_in_dim.14), calls=%async_computation.4 | async-start | bytes 524288 | tf_op jit(solution)/shard_map/all_to_all | solution.py:324

commit v6 on v5

--- a/solution.py
+++ b/solution.py
@@ -68,7 +68,6 @@
     drow_acc,
     dweight_acc,
     dweight_sum,
-    drow_turned,
     dbias_acc,
     sent_sems,
 ):
@@ -162,11 +161,15 @@
             tiles, turned_lanes(m), preferred_element_type=F32
         )
 
-    for m in range(GROUP):
-        for k in range(quarters):
-            block = drow_acc[pl.ds(m * depth + k * across, across), :]
-            drow_turned[pl.ds(k * GROUP + m, across, stride=CH), :] = block * scale
-    sent = drow_turned[...].astype(BF16).reshape(send_ref.shape[0], -1, SEQS)
+    by_channel_rows = jnp.stack(
+        [
+            drow_acc[pl.ds(m * depth + k * across, across), :]
+            for k in range(quarters)
+            for m in range(GROUP)
+        ]
+    )
+    sent = (jnp.swapaxes(by_channel_rows, 0, 1) * scale).astype(BF16)
+    sent = sent.reshape(send_ref.shape[0], -1, SEQS)
     count = sent.shape[1]
     total = dweight_acc[0]
     for q in range(1, GROUP):
@@ -176,8 +179,7 @@
     @pl.when(term == 0)
     def _():
         send_ref[:, count : 2 * count, :] = sent
-        for k in range(CH):
-            dweight_sum[pl.ds(k, CH, stride=CH), :] = flat[k * CH : (k + 1) * CH]
+        dweight_sum[...] = jnp.swapaxes(flat.reshape(CH, CH, -1), 0, 1).reshape(flat.shape)
 
     @pl.when(term == 1)
     def _():
@@ -307,7 +309,6 @@
             pltpu.VMEM((CH * across, SEQS), F32),
             pltpu.VMEM((GROUP, pairs, CH * CH), F32),
             pltpu.VMEM((CH * CH, pairs), F32),
-            pltpu.VMEM((CH * across, SEQS), F32),
             pltpu.VMEM((8, pairs), F32),
             pltpu.SemaphoreType.DMA((2, CH // GROUP)),
         ],

time: 149 us -> 148 us (level)
  no operation moved by 1% of the time
where the time goes in v6:
time: 148 us; the launch traced here: 147 us
  waiting for transfers between devices  57.9 us (39%)
  Pallas kernels  45.3 us (31%)
  starting transfers between devices  28.7 us (19%)
  local copies, waits for them, and re-layouts  9.22 us (6%)
  other arithmetic  5.3 us (4%)
    all_to_all x5, waiting for transfers between devices, exchange(): lax.all_to_all(x, axis, split_axis=0, concat_axis=0, axis_index_groups=gr...  56.9 us
    pallas_call x1, Pallas kernels, pair_block(): pl.pallas_call(functools.partial(pair_kernel, across), grid=(2,), in_spec...  35.5 us
    all_to_all x5, starting transfers between devices, exchange(): lax.all_to_all(x, axis, split_axis=0, concat_axis=0, axis_index_groups=gr...  27.1 us
    pallas_call x1, Pallas kernels, lane_block(): pl.pallas_call(functools.partial(lane_kernel, across), grid=(2, steps), i...  9.79 us
  transfers between devices with their start and end apart: 10, of which 6 were waited for; matrix products, arithmetic and copies ran while one was open for 6% of the time, Pallas kernels for 7%

profile of v6, /device:TPU:0, one launch (start us, length us, event | category | flops | bytes accessed | tf_op | source)
XLA Modules:
  0.0 147.4 jit_solution(4780261392570837350)
XLA Ops:
  0.6 0.9 pad_maximum_fusion.2
  1.6 0.3 reshape.98
  1.8 0.2 copy.27
  2.0 1.0 broadcast_in_dim.11
  3.0 5.9 %all-to-all-start = ((bf16[8,2,192,128]{3,2,1,0:T(8,128)(2,1)}), bf16[8,2,192,128]{3,2,1,0:T(8,128)(2,1)S(1)}, u32[]{:S(2)}, u32[]{:S(2)}) async-start(bf16[8,2,192,128]{3,2,1,0:T(8,128)(2,1)} %broadcast_in_dim.11), calls=%async_computation | async-start | bytes 1572864 | tf_op jit(solution)/shard_map/all_to_all | solution.py:325
  9.0 0.0 copy-start.1
  9.0 0.8 collective-permute-start.1
  9.8 12.1 %all-to-all-done = bf16[8,2,192,128]{3,2,1,0:T(8,128)(2,1)S(1)} async-done(((bf16[8,2,192,128]{3,2,1,0:T(8,128)(2,1)}), bf16[8,2,192,128]{3,2,1,0:T(8,128)(2,1)S(1)}, u32[]{:S(2)}, u32[]{:S(2)}) %all-to-all-start) | async-done | bytes 786464 | tf_op jit(solution)/shard_map/all_to_all | solution.py:325
  21.8 0.0 collective-permute-start
  21.8 0.0 collective-permute-done.1
  21.9 1.0 broadcast_in_dim.12
  22.9 8.4 %all-to-all-start.1 = ((bf16[8,2,192,128]{3,2,1,0:T(8,128)(2,1)}), bf16[8,2,192,128]{3,2,1,0:T(8,128)(2,1)S(1)}, u32[]{:S(2)}, u32[]{:S(2)}) async-start(bf16[8,2,192,128]{3,2,1,0:T(8,128)(2,1)} %broadcast_in_dim.12), calls=%async_computation.1 | async-start | bytes 1572864 | tf_op jit(solution)/shard_map/all_to_all | solution.py:325
  31.3 0.0 copy-done.1
  31.3 0.1 copy.31
  31.4 0.8 pad_maximum_fusion.1.weight_ref
  32.2 14.1 %all-to-all-done.1 = bf16[8,2,192,128]{3,2,1,0:T(8,128)(2,1)S(1)} async-done(((bf16[8,2,192,128]{3,2,1,0:T(8,128)(2,1)}), bf16[8,2,192,128]{3,2,1,0:T(8,128)(2,1)S(1)}, u32[]{:S(2)}, u32[]{:S(2)}) %all-to-all-start.1) | async-done | bytes 786464 | tf_op jit(solution)/shard_map/all_to_all | solution.py:325
  46.3 0.5 copy.29
  46.8 0.8 copy.30
  47.7 1.0 copy.32.row_ref
  48.7 0.0 collective-permute-done
  48.7 0.1 select_bitcast_fusion.1
  48.8 0.1 maximum_bitcast_fusion
  49.0 1.3 copy.28
  50.3 35.5 %shard_map.92 = (bf16[96,48,128]{2,1,0:T(8,128)(2,1)}, bf16[2,4,24,384,128]{4,3,2,1,0:T(8,128)(2,1)}, bf16[8,528,128]{2,1,0:T(8,128)(2,1)}) custom-call(bf16[2,3072,128]{2,1,0:T(8,128)(2,1)} %bitcast.46, bf16[2,1536,128]{2,1,0:T(8,128)(2,1)} %copy.32.row_ref, bf16[2,1024,128]{2,1,0:T(8,128)(2,1)} %pad_maximum_fusion.1.weight_ref, f32[1,128]{1,0:T(1,128)} %bitcast.54, ...), custom_call_target="tpu_custom_call" | custom-call | flops 12079595520 | bytes 33554432 | tf_op jit(solution)/shard_map/pallas_call | solution.py:283
  85.8 0.0 copy-start
  85.8 3.9 %all-to-all-start.2 = ((bf16[8,528,128]{2,1,0:T(8,128)(2,1)}), bf16[8,528,128]{2,1,0:T(8,128)(2,1)S(1)}, u32[]{:S(2)}, u32[]{:S(2)}) async-start(bf16[8,528,128]{2,1,0:T(8,128)(2,1)} %get-tuple-element.14), calls=%async_computation.2 | async-start | bytes 2162688 | tf_op jit(solution)/shard_map/all_to_all | solution.py:325
  89.8 0.1 pad.9.clone
  89.8 0.0 copy-done
  89.8 9.8 %shard_map.93 = (bf16[8,384,128]{2,1,0:T(8,128)(2,1)S(1)}, bf16[8,384,128]{2,1,0:T(8,128)(2,1)S(1)}) custom-call(s32[1]{0:T(128)} %bitcast.14.core_ref, bf16[2,4,24,384,128]{4,3,2,1,0:T(8,128)(2,1)} %get-tuple-element.11.grads_ref, bf16[2,1536,128]{2,1,0:T(8,128)(2,1)S(1)} %copy-done), custom_call_target="tpu_custom_call" | custom-call | flops 2415919104 | bytes 25165824 | tf_op jit(solution)/shard_map/pallas_call | solution.py:246
  99.6 0.1 collective-permute-start.2
  99.7 7.7 %all-to-all-done.2 = bf16[8,528,128]{2,1,0:T(8,128)(2,1)S(1)} async-done(((bf16[8,528,128]{2,1,0:T(8,128)(2,1)}), bf16[8,528,128]{2,1,0:T(8,128)(2,1)S(1)}, u32[]{:S(2)}, u32[]{:S(2)}) %all-to-all-start.2) | async-done | bytes 1081376 | tf_op jit(solution)/shard_map/all_to_all | solution.py:325
  107.4 0.1 convert_reduce_fusion.1
  107.6 0.1 maximum_maximum_fusion
  107.7 0.1 collective-permute-start.3
  107.8 0.0 collective-permute-done.2
  107.8 0.2 add_convert_fusion
  108.1 1.0 collective-permute-done.3
  109.0 0.1 convert_add_fusion
  109.2 0.1 maximum_maximum_fusion.1
  109.3 1.1 pad_maximum_fusion
  110.4 3.6 %all-to-all-start.3 = ((bf16[8,528,128]{2,1,0:T(8,128)(2,1)}), bf16[8,528,128]{2,1,0:T(8,128)(2,1)S(1)}, u32[]{:S(2)}, u32[]{:S(2)}) async-start(bf16[8,528,128]{2,1,0:T(8,128)(2,1)} %pad_maximum_fusion), calls=%async_computation.3 | async-start | bytes 2162688 | tf_op jit(solution)/shard_map/all_to_all | solution.py:325
  113.9 0.7 collective-permute-start.4
  114.6 16.9 %all-to-all-done.3 = bf16[8,528,128]{2,1,0:T(8,128)(2,1)S(1)} async-done(((bf16[8,528,128]{2,1,0:T(8,128)(2,1)}), bf16[8,528,128]{2,1,0:T(8,128)(2,1)S(1)}, u32[]{:S(2)}, u32[]{:S(2)}) %all-to-all-start.3) | async-done | bytes 1081376 | tf_op jit(solution)/shard_map/all_to_all | solution.py:325
  131.6 0.1 convert_reduce_fusion
  131.7 0.7 broadcast_in_dim.14
  132.5 5.3 %all-to-all-start.4 = ((bf16[8,128,128]{2,1,0:T(8,128)(2,1)}), bf16[8,128,128]{2,1,0:T(8,128)(2,1)S(1)}, u32[]{:S(2)}, u32[]{:S(2)}) async-start(bf16[8,128,128]{2,1,0:T(8,128)(2,1)} %broadcast_in_dim.14), calls=%async_computation.4 | async-start | bytes 524288 | tf_op jit(solution)/shard_map/all_to_all | solution.py:325
  137.8 0.0 collective-permute-done.4
  137.8 0.2 copy.34
  138.0 0.9 squeeze.6
  138.9 0.2 copy.35
  139.0 0.9 squeeze.7
  139.9 0.5 slice_reduce_fusion
  140.4 6.1 %all-to-all-done.4 = bf16[8,128,128]{2,1,0:T(8,128)(2,1)S(1)} async-done(((bf16[8,128,128]{2,1,0:T(8,128)(2,1)}), bf16[8,128,128]{2,1,0:T(8,128)(2,1)S(1)}, u32[]{:S(2)}, u32[]{:S(2)}) %all-to-all-start.4) | async-done | bytes 262176 | tf_op jit(solution)/shard_map/all_to_all | solution.py:325
  146.5 0.8 bitcast_convert_fusion
  (15 shorter events, 0.2 us)
Async XLA Ops:
  3.0 18.8 %all-to-all-start = ((bf16[8,2,192,128]{3,2,1,0:T(8,128)(2,1)}), bf16[8,2,192,128]{3,2,1,0:T(8,128)(2,1)S(1)}, u32[]{:S(2)}, u32[]{:S(2)}) async-start(bf16[8,2,192,128]{3,2,1,0:T(8,128)(2,1)} %broadcast_in_dim.11), calls=%async_computation | async-start | bytes 1572864 | tf_op jit(solution)/shard_map/all_to_all | solution.py:325
  9.0 22.3 %copy-start.1 = (bf16[1024,128]{1,0:T(8,128)(2,1)S(1)}, bf16[1024,128]{1,0:T(8,128)(2,1)}, u32[]{:S(2)}) copy-start(bf16[1024,128]{1,0:T(8,128)(2,1)} %param.7) | copy-start | bytes 786436
  9.0 12.9 %collective-permute-start.1 = (bf16[2,192,128]{2,1,0:T(8,128)(2,1)S(1)}, bf16[2,192,128]{2,1,0:T(8,128)(2,1)S(1)}, u32[]{:S(2)}, u32[]{:S(2)}) collective-permute-start(bf16[2,192,128]{2,1,0:T(8,128)(2,1)S(1)} %bitcast.53), channel_id=1, source_target_pairs={{0,0},{1,16},{2,32},{3,48},{4,64},{5,80},{6,96},{7,112},{8,1},{9,1... | collective-permute-start | bytes 294920 | tf_op jit(solution)/shard_map/ppermute | solution.py:361
  21.8 26.9 %collective-permute-start = (bf16[8,2,192,128]{3,2,1,0:T(8,128)(2,1)S(1)}, bf16[8,2,192,128]{3,2,1,0:T(8,128)(2,1)S(1)}, u32[]{:S(2)}, u32[]{:S(2)}) collective-permute-start(bf16[8,2,192,128]{3,2,1,0:T(8,128)(2,1)S(1)} %all-to-all-done), channel_id=1, source_target_pairs={{0,1},{1,0},{2,3},{3,2},{4,5},{5,4},{6,7},{7,6},{8,9},{9,8},{10,11... | collective-permute-start | bytes 2359304 | tf_op jit(solution)/shard_map/ppermute | solution.py:363
  22.9 23.4 %all-to-all-start.1 = ((bf16[8,2,192,128]{3,2,1,0:T(8,128)(2,1)}), bf16[8,2,192,128]{3,2,1,0:T(8,128)(2,1)S(1)}, u32[]{:S(2)}, u32[]{:S(2)}) async-start(bf16[8,2,192,128]{3,2,1,0:T(8,128)(2,1)} %broadcast_in_dim.12), calls=%async_computation.1 | async-start | bytes 1572864 | tf_op jit(solution)/shard_map/all_to_all | solution.py:325
  85.8 4.0 %copy-start = (bf16[2,1536,128]{2,1,0:T(8,128)(2,1)S(1)}, bf16[2,1536,128]{2,1,0:T(8,128)(2,1)}, u32[]{:S(2)}) copy-start(bf16[2,1536,128]{2,1,0:T(8,128)(2,1)} %copy.32.row_ref) | copy-start | bytes 2359300
  85.8 21.6 %all-to-all-start.2 = ((bf16[8,528,128]{2,1,0:T(8,128)(2,1)}), bf16[8,528,128]{2,1,0:T(8,128)(2,1)S(1)}, u32[]{:S(2)}, u32[]{:S(2)}) async-start(bf16[8,528,128]{2,1,0:T(8,128)(2,1)} %get-tuple-element.14), calls=%async_computation.2 | async-start | bytes 2162688 | tf_op jit(solution)/shard_map/all_to_all | solution.py:325
  99.6 8.2 %collective-permute-start.2 = (bf16[8,384,128]{2,1,0:T(8,128)(2,1)S(1)}, bf16[8,384,128]{2,1,0:T(8,128)(2,1)S(1)}, u32[]{:S(2)}, u32[]{:S(2)}) collective-permute-start(bf16[8,384,128]{2,1,0:T(8,128)(2,1)S(1)} %get-tuple-element.13), channel_id=1, source_target_pairs={{0,1},{1,0},{2,3},{3,2},{4,5},{5,4},{6,7},{7,6},{8,9},{9,8},{10,11... | collective-permute-start | bytes 2359304 | tf_op jit(solution)/shard_map/ppermute | solution.py:383
  107.7 1.3 collective-permute-start.3
  110.4 21.2 %all-to-all-start.3 = ((bf16[8,528,128]{2,1,0:T(8,128)(2,1)}), bf16[8,528,128]{2,1,0:T(8,128)(2,1)S(1)}, u32[]{:S(2)}, u32[]{:S(2)}) async-start(bf16[8,528,128]{2,1,0:T(8,128)(2,1)} %pad_maximum_fusion), calls=%async_computation.3 | async-start | bytes 2162688 | tf_op jit(solution)/shard_map/all_to_all | solution.py:325
  113.9 23.8 %collective-permute-start.4 = (bf16[384,128]{1,0:T(8,128)(2,1)S(1)}, bf16[384,128]{1,0:T(8,128)(2,1)S(1)}, u32[]{:S(2)}, u32[]{:S(2)}) collective-permute-start(bf16[384,128]{1,0:T(8,128)(2,1)S(1)} %slice.60), channel_id=1, source_target_pairs={{0,0},{16,1},{32,2},{48,3},{64,4},{80,5},{96,6},{112,7},{1,8},{17,... | collective-permute-start | bytes 294920 | tf_op jit(solution)/shard_map/ppermute | solution.py:385
  132.5 14.1 %all-to-all-start.4 = ((bf16[8,128,128]{2,1,0:T(8,128)(2,1)}), bf16[8,128,128]{2,1,0:T(8,128)(2,1)S(1)}, u32[]{:S(2)}, u32[]{:S(2)}) async-start(bf16[8,128,128]{2,1,0:T(8,128)(2,1)} %broadcast_in_dim.14), calls=%async_computation.4 | async-start | bytes 524288 | tf_op jit(solution)/shard_map/all_to_all | solution.py:325

commit v7 on v6

--- a/solution.py
+++ b/solution.py
@@ -105,7 +105,7 @@
         to_tiles(products, m, (outer * scale).astype(BF16))
 
     def by_pair(k, _):
-        from_rows = pl.multiple_of(k * across, TILE)
+        from_rows = k * across
         for g in range(groups):
             for t in range(0, across, TILE):
                 parts = [
@@ -115,7 +115,8 @@
                     packed[q, k, pl.ds(g * across + t, TILE), :] = tile
         return _
 
-    lax.fori_loop(0, quarters, by_pair, 0)
+    for k in range(quarters):
+        by_pair(k, 0)
     for q in range(GROUP):
         outer = from_tiles(packed, q)
         weight_q = turned_weight(q)

time: 148 us -> 146 us (0.986)
  Pallas kernels: 45.3 us -> 43.7 us
    pallas_call x1, Pallas kernels: 35.5 us -> 33.9 us  [pair_block(): pl.pallas_call(functools.partial(pair_kernel, across), grid=(2,), in_spec...]
where the time goes in v7:
time: 146 us
  waiting for transfers between devices  57.9 us (40%)
  Pallas kernels  43.7 us (30%)
  starting transfers between devices  28.5 us (20%)
  local copies, waits for them, and re-layouts  9.22 us (6%)
  other arithmetic  5.3 us (4%)
    all_to_all x5, waiting for transfers between devices, exchange(): lax.all_to_all(x, axis, split_axis=0, concat_axis=0, axis_index_groups=gr...  56.9 us
    pallas_call x1, Pallas kernels, pair_block(): pl.pallas_call(functools.partial(pair_kernel, across), grid=(2,), in_spec...  33.9 us
    all_to_all x5, starting transfers between devices, exchange(): lax.all_to_all(x, axis, split_axis=0, concat_axis=0, axis_index_groups=gr...  26.9 us
    pallas_call x1, Pallas kernels, lane_block(): pl.pallas_call(functools.partial(lane_kernel, across), grid=(2, steps), i...  9.78 us
  transfers between devices with their start and end apart: 10, of which 6 were waited for; matrix products, arithmetic and copies ran while one was open for 6% of the time, Pallas kernels for 7%

profile of v7, /device:TPU:0, one launch (start us, length us, event | category | flops | bytes accessed | tf_op | source)
XLA Modules:
  0.0 145.5 jit_solution(10054660201769940049)
XLA Ops:
  0.6 0.9 pad_maximum_fusion.2
  1.6 0.3 reshape.98
  1.8 0.2 copy.27
  2.0 1.0 broadcast_in_dim.11
  3.0 5.9 %all-to-all-start = ((bf16[8,2,192,128]{3,2,1,0:T(8,128)(2,1)}), bf16[8,2,192,128]{3,2,1,0:T(8,128)(2,1)S(1)}, u32[]{:S(2)}, u32[]{:S(2)}) async-start(bf16[8,2,192,128]{3,2,1,0:T(8,128)(2,1)} %broadcast_in_dim.11), calls=%async_computation | async-start | bytes 1572864 | tf_op jit(solution)/shard_map/all_to_all | solution.py:326
  9.0 0.0 copy-start.1
  9.0 0.8 collective-permute-start.1
  9.8 12.1 %all-to-all-done = bf16[8,2,192,128]{3,2,1,0:T(8,128)(2,1)S(1)} async-done(((bf16[8,2,192,128]{3,2,1,0:T(8,128)(2,1)}), bf16[8,2,192,128]{3,2,1,0:T(8,128)(2,1)S(1)}, u32[]{:S(2)}, u32[]{:S(2)}) %all-to-all-start) | async-done | bytes 786464 | tf_op jit(solution)/shard_map/all_to_all | solution.py:326
  21.8 0.0 collective-permute-start
  21.8 0.0 collective-permute-done.1
  21.9 1.0 broadcast_in_dim.12
  22.9 8.4 %all-to-all-start.1 = ((bf16[8,2,192,128]{3,2,1,0:T(8,128)(2,1)}), bf16[8,2,192,128]{3,2,1,0:T(8,128)(2,1)S(1)}, u32[]{:S(2)}, u32[]{:S(2)}) async-start(bf16[8,2,192,128]{3,2,1,0:T(8,128)(2,1)} %broadcast_in_dim.12), calls=%async_computation.1 | async-start | bytes 1572864 | tf_op jit(solution)/shard_map/all_to_all | solution.py:326
  31.3 0.0 copy-done.1
  31.3 0.1 copy.31
  31.4 0.8 pad_maximum_fusion.1.weight_ref
  32.2 14.1 %all-to-all-done.1 = bf16[8,2,192,128]{3,2,1,0:T(8,128)(2,1)S(1)} async-done(((bf16[8,2,192,128]{3,2,1,0:T(8,128)(2,1)}), bf16[8,2,192,128]{3,2,1,0:T(8,128)(2,1)S(1)}, u32[]{:S(2)}, u32[]{:S(2)}) %all-to-all-start.1) | async-done | bytes 786464 | tf_op jit(solution)/shard_map/all_to_all | solution.py:326
  46.3 0.5 copy.29
  46.8 0.8 copy.30
  47.7 1.0 copy.32.row_ref
  48.7 0.0 collective-permute-done
  48.7 0.1 select_bitcast_fusion.1
  48.8 0.1 maximum_bitcast_fusion
  49.0 1.3 copy.28
  50.3 33.9 %shard_map.92 = (bf16[96,48,128]{2,1,0:T(8,128)(2,1)}, bf16[2,4,24,384,128]{4,3,2,1,0:T(8,128)(2,1)}, bf16[8,528,128]{2,1,0:T(8,128)(2,1)}) custom-call(bf16[2,3072,128]{2,1,0:T(8,128)(2,1)} %bitcast.46, bf16[2,1536,128]{2,1,0:T(8,128)(2,1)} %copy.32.row_ref, bf16[2,1024,128]{2,1,0:T(8,128)(2,1)} %pad_maximum_fusion.1.weight_ref, f32[1,128]{1,0:T(1,128)} %bitcast.54, ...), custom_call_target="tpu_custom_call" | custom-call | flops 12079595520 | bytes 33554432 | tf_op jit(solution)/shard_map/pallas_call | solution.py:284
  84.2 0.0 copy-start
  84.2 3.7 %all-to-all-start.2 = ((bf16[8,528,128]{2,1,0:T(8,128)(2,1)}), bf16[8,528,128]{2,1,0:T(8,128)(2,1)S(1)}, u32[]{:S(2)}, u32[]{:S(2)}) async-start(bf16[8,528,128]{2,1,0:T(8,128)(2,1)} %get-tuple-element.14), calls=%async_computation.2 | async-start | bytes 2162688 | tf_op jit(solution)/shard_map/all_to_all | solution.py:326
  87.9 0.1 pad.9.clone
  88.0 0.0 copy-done
  88.0 9.8 %shard_map.93 = (bf16[8,384,128]{2,1,0:T(8,128)(2,1)S(1)}, bf16[8,384,128]{2,1,0:T(8,128)(2,1)S(1)}) custom-call(s32[1]{0:T(128)} %bitcast.14.core_ref, bf16[2,4,24,384,128]{4,3,2,1,0:T(8,128)(2,1)} %get-tuple-element.11.grads_ref, bf16[2,1536,128]{2,1,0:T(8,128)(2,1)S(1)} %copy-done), custom_call_target="tpu_custom_call" | custom-call | flops 2415919104 | bytes 25165824 | tf_op jit(solution)/shard_map/pallas_call | solution.py:247
  97.8 0.1 collective-permute-start.2
  97.9 7.7 %all-to-all-done.2 = bf16[8,528,128]{2,1,0:T(8,128)(2,1)S(1)} async-done(((bf16[8,528,128]{2,1,0:T(8,128)(2,1)}), bf16[8,528,128]{2,1,0:T(8,128)(2,1)S(1)}, u32[]{:S(2)}, u32[]{:S(2)}) %all-to-all-start.2) | async-done | bytes 1081376 | tf_op jit(solution)/shard_map/all_to_all | solution.py:326
  105.6 0.1 convert_reduce_fusion.1
  105.8 0.1 maximum_maximum_fusion
  105.9 0.1 collective-permute-start.3
  106.0 0.0 collective-permute-done.2
  106.0 0.2 add_convert_fusion
  106.2 1.0 collective-permute-done.3
  107.2 0.1 convert_add_fusion
  107.3 0.1 maximum_maximum_fusion.1
  107.5 1.1 pad_maximum_fusion
  108.5 3.6 %all-to-all-start.3 = ((bf16[8,528,128]{2,1,0:T(8,128)(2,1)}), bf16[8,528,128]{2,1,0:T(8,128)(2,1)S(1)}, u32[]{:S(2)}, u32[]{:S(2)}) async-start(bf16[8,528,128]{2,1,0:T(8,128)(2,1)} %pad_maximum_fusion), calls=%async_computation.3 | async-start | bytes 2162688 | tf_op jit(solution)/shard_map/all_to_all | solution.py:326
  112.1 0.7 collective-permute-start.4
  112.8 16.9 %all-to-all-done.3 = bf16[8,528,128]{2,1,0:T(8,128)(2,1)S(1)} async-done(((bf16[8,528,128]{2,1,0:T(8,128)(2,1)}), bf16[8,528,128]{2,1,0:T(8,128)(2,1)S(1)}, u32[]{:S(2)}, u32[]{:S(2)}) %all-to-all-start.3) | async-done | bytes 1081376 | tf_op jit(solution)/shard_map/all_to_all | solution.py:326
  129.7 0.1 convert_reduce_fusion
  129.9 0.7 broadcast_in_dim.14
  130.6 5.3 %all-to-all-start.4 = ((bf16[8,128,128]{2,1,0:T(8,128)(2,1)}), bf16[8,128,128]{2,1,0:T(8,128)(2,1)S(1)}, u32[]{:S(2)}, u32[]{:S(2)}) async-start(bf16[8,128,128]{2,1,0:T(8,128)(2,1)} %broadcast_in_dim.14), calls=%async_computation.4 | async-start | bytes 524288 | tf_op jit(solution)/shard_map/all_to_all | solution.py:326
  135.9 0.0 collective-permute-done.4
  136.0 0.2 copy.34
  136.1 0.9 squeeze.6
  137.0 0.2 copy.35
  137.2 0.9 squeeze.7
  138.0 0.5 slice_reduce_fusion
  138.6 6.1 %all-to-all-done.4 = bf16[8,128,128]{2,1,0:T(8,128)(2,1)S(1)} async-done(((bf16[8,128,128]{2,1,0:T(8,128)(2,1)}), bf16[8,128,128]{2,1,0:T(8,128)(2,1)S(1)}, u32[]{:S(2)}, u32[]{:S(2)}) %all-to-all-start.4) | async-done | bytes 262176 | tf_op jit(solution)/shard_map/all_to_all | solution.py:326
  144.7 0.8 bitcast_convert_fusion
  (15 shorter events, 0.2 us)
Async XLA Ops:
  3.0 18.8 %all-to-all-start = ((bf16[8,2,192,128]{3,2,1,0:T(8,128)(2,1)}), bf16[8,2,192,128]{3,2,1,0:T(8,128)(2,1)S(1)}, u32[]{:S(2)}, u32[]{:S(2)}) async-start(bf16[8,2,192,128]{3,2,1,0:T(8,128)(2,1)} %broadcast_in_dim.11), calls=%async_computation | async-start | bytes 1572864 | tf_op jit(solution)/shard_map/all_to_all | solution.py:326
  9.0 22.3 %copy-start.1 = (bf16[1024,128]{1,0:T(8,128)(2,1)S(1)}, bf16[1024,128]{1,0:T(8,128)(2,1)}, u32[]{:S(2)}) copy-start(bf16[1024,128]{1,0:T(8,128)(2,1)} %param.7) | copy-start | bytes 786436
  9.0 12.9 %collective-permute-start.1 = (bf16[2,192,128]{2,1,0:T(8,128)(2,1)S(1)}, bf16[2,192,128]{2,1,0:T(8,128)(2,1)S(1)}, u32[]{:S(2)}, u32[]{:S(2)}) collective-permute-start(bf16[2,192,128]{2,1,0:T(8,128)(2,1)S(1)} %bitcast.53), channel_id=1, source_target_pairs={{0,0},{1,16},{2,32},{3,48},{4,64},{5,80},{6,96},{7,112},{8,1},{9,1... | collective-permute-start | bytes 294920 | tf_op jit(solution)/shard_map/ppermute | solution.py:362
  21.8 26.9 %collective-permute-start = (bf16[8,2,192,128]{3,2,1,0:T(8,128)(2,1)S(1)}, bf16[8,2,192,128]{3,2,1,0:T(8,128)(2,1)S(1)}, u32[]{:S(2)}, u32[]{:S(2)}) collective-permute-start(bf16[8,2,192,128]{3,2,1,0:T(8,128)(2,1)S(1)} %all-to-all-done), channel_id=1, source_target_pairs={{0,1},{1,0},{2,3},{3,2},{4,5},{5,4},{6,7},{7,6},{8,9},{9,8},{10,11... | collective-permute-start | bytes 2359304 | tf_op jit(solution)/shard_map/ppermute | solution.py:364
  22.9 23.4 %all-to-all-start.1 = ((bf16[8,2,192,128]{3,2,1,0:T(8,128)(2,1)}), bf16[8,2,192,128]{3,2,1,0:T(8,128)(2,1)S(1)}, u32[]{:S(2)}, u32[]{:S(2)}) async-start(bf16[8,2,192,128]{3,2,1,0:T(8,128)(2,1)} %broadcast_in_dim.12), calls=%async_computation.1 | async-start | bytes 1572864 | tf_op jit(solution)/shard_map/all_to_all | solution.py:326
  84.2 3.8 %copy-start = (bf16[2,1536,128]{2,1,0:T(8,128)(2,1)S(1)}, bf16[2,1536,128]{2,1,0:T(8,128)(2,1)}, u32[]{:S(2)}) copy-start(bf16[2,1536,128]{2,1,0:T(8,128)(2,1)} %copy.32.row_ref) | copy-start | bytes 2359300
  84.2 21.4 %all-to-all-start.2 = ((bf16[8,528,128]{2,1,0:T(8,128)(2,1)}), bf16[8,528,128]{2,1,0:T(8,128)(2,1)S(1)}, u32[]{:S(2)}, u32[]{:S(2)}) async-start(bf16[8,528,128]{2,1,0:T(8,128)(2,1)} %get-tuple-element.14), calls=%async_computation.2 | async-start | bytes 2162688 | tf_op jit(solution)/shard_map/all_to_all | solution.py:326
  97.8 8.2 %collective-permute-start.2 = (bf16[8,384,128]{2,1,0:T(8,128)(2,1)S(1)}, bf16[8,384,128]{2,1,0:T(8,128)(2,1)S(1)}, u32[]{:S(2)}, u32[]{:S(2)}) collective-permute-start(bf16[8,384,128]{2,1,0:T(8,128)(2,1)S(1)} %get-tuple-element.13), channel_id=1, source_target_pairs={{0,1},{1,0},{2,3},{3,2},{4,5},{5,4},{6,7},{7,6},{8,9},{9,8},{10,11... | collective-permute-start | bytes 2359304 | tf_op jit(solution)/shard_map/ppermute | solution.py:384
  105.9 1.3 collective-permute-start.3
  108.5 21.2 %all-to-all-start.3 = ((bf16[8,528,128]{2,1,0:T(8,128)(2,1)}), bf16[8,528,128]{2,1,0:T(8,128)(2,1)S(1)}, u32[]{:S(2)}, u32[]{:S(2)}) async-start(bf16[8,528,128]{2,1,0:T(8,128)(2,1)} %pad_maximum_fusion), calls=%async_computation.3 | async-start | bytes 2162688 | tf_op jit(solution)/shard_map/all_to_all | solution.py:326
  112.1 23.8 %collective-permute-start.4 = (bf16[384,128]{1,0:T(8,128)(2,1)S(1)}, bf16[384,128]{1,0:T(8,128)(2,1)S(1)}, u32[]{:S(2)}, u32[]{:S(2)}) collective-permute-start(bf16[384,128]{1,0:T(8,128)(2,1)S(1)} %slice.60), channel_id=1, source_target_pairs={{0,0},{16,1},{32,2},{48,3},{64,4},{80,5},{96,6},{112,7},{1,8},{17,... | collective-permute-start | bytes 294920 | tf_op jit(solution)/shard_map/ppermute | solution.py:386
  130.6 14.1 %all-to-all-start.4 = ((bf16[8,128,128]{2,1,0:T(8,128)(2,1)}), bf16[8,128,128]{2,1,0:T(8,128)(2,1)S(1)}, u32[]{:S(2)}, u32[]{:S(2)}) async-start(bf16[8,128,128]{2,1,0:T(8,128)(2,1)} %broadcast_in_dim.14), calls=%async_computation.4 | async-start | bytes 524288 | tf_op jit(solution)/shard_map/all_to_all | solution.py:326
